TPU v7x, 32 devices: a whole 2x2x4 slice. The times are simulated.
32 devices in a mesh: grp: 2 (over core), gx: 4 (over z), gy: 4 (over y, x).
Axes of the slice: x: 2, y: 2, z: 4, core: 2. Of those that a mesh axis runs over, the one named last changes fastest.
Arguments:
- coarse_ez: float32 [256, 1024], P('gx', ('grp', 'gy')), may hold values from -6 to 6
- coarse_hx: float32 [256, 1024], P('gx', ('grp', 'gy')), may hold values from -6 to 6
- coarse_hy: float32 [256, 1024], P('gx', ('grp', 'gy')), may hold values from -6 to 6
- coarse_ids: int32 [256, 1024], P('gx', ('grp', 'gy')), may hold values from 0 to 7
- mat_eps: float32 [8], replicated, may hold values from 1 to 12
- mat_sig: float32 [8], replicated, may hold values from 0 to 0.5
- fine_ez: float32 [4, 8, 32, 2304], P(None, ('grp', 'gy'), 'gx'), may hold values from -6 to 6
- fine_hx: float32 [4, 8, 32, 2304], P(None, ('grp', 'gy'), 'gx'), may hold values from -6 to 6
- fine_hy: float32 [4, 8, 32, 2304], P(None, ('grp', 'gy'), 'gx'), may hold values from -6 to 6
- fine_ids: int32 [4, 8, 32, 2304], P(None, ('grp', 'gy'), 'gx'), may hold values from 0 to 7
- boxes: int32 [4, 8, 32, 4], P('gx', ('grp', 'gy')), may hold values from 1 to 14, as said below
- src_cells: int32 [4], replicated, may hold values from 0 to 262143
- src_wave: float32 [3, 4], replicated, may hold values from -6 to 6
- rcv_cells: int32 [128], replicated, may hold values from 0 to 262143
Outputs:
- end_ez: float32 [256, 1024], P('gx', ('grp', 'gy'))
- end_hx: float32 [256, 1024], P('gx', ('grp', 'gy'))
- end_hy: float32 [256, 1024], P('gx', ('grp', 'gy'))
- end_fine_ez: float32 [4, 8, 32, 2304], P(None, ('grp', 'gy'), 'gx')
- end_fine_hx: float32 [4, 8, 32, 2304], P(None, ('grp', 'gy'), 'gx')
- end_fine_hy: float32 [4, 8, 32, 2304], P(None, ('grp', 'gy'), 'gx')
- traces: float32 [3, 128], replicated
Inputs may be any that keep to these rules, and one draw needn't show every extreme that they name: `boxes`: each box lies one cell or more inside its tile: corner + size <= 15; sizes are 4 to 14, drawn independently for every subgrid.
All inputs are finite; a program needn't handle non-finite values.
Results may differ from a plain program's by a relative error of at most 0.00011.
Values sent between devices are 32-bit elements; how exact they have to be, the bound alone decides.
No kernel may reach another device: no remote copies, remote signals or barrier semaphores. Data moves between devices by JAX's collectives and lax.ppermute only.
A program may use at most 64 MiB of HBM per device.

v0:
```python
import jax
import jax.numpy as jnp
from jax import lax
from jax.sharding import PartitionSpec as P

TILE = 16
STEPS = 3


COURANT = 0.5
HCOEF = 0.5


def passed_along(value, axis, steps):
    count = lax.axis_size(axis)
    initial, last = (max(0, -steps), min(count, count - steps))
    return lax.ppermute(value, axis, [(source, source + steps) for source in range(initial, last)])


def coefficients(ids, eps_table, sig_table, ratio):
    damp = jnp.zeros(ids.shape, jnp.float32)
    gain = jnp.zeros(ids.shape, jnp.float32)
    for material in range(eps_table.shape[0]):
        loss = sig_table[material] / (eps_table[material] * ratio)
        hit = ids == material
        damp = jnp.where(hit, (1.0 - loss) / (1.0 + loss), damp)
        gain = jnp.where(hit, COURANT / (eps_table[material] * (1.0 + loss)), gain)
    return (damp, gain)


def box_masks(boxes, cells, scale):
    coarse_of = jnp.arange(cells, dtype=jnp.int32) // scale
    low_i = boxes[..., 0:1]
    low_j = boxes[..., 1:2]
    high_i = low_i + boxes[..., 2:3]
    high_j = low_j + boxes[..., 3:4]
    rows_in = (coarse_of >= low_i) & (coarse_of < high_i)
    cols_in = (coarse_of >= low_j) & (coarse_of < high_j)
    rows_mid = (coarse_of > low_i) & (coarse_of < high_i - 1)
    cols_mid = (coarse_of > low_j) & (coarse_of < high_j - 1)
    inbox = rows_in[..., :, None] & cols_in[..., None, :]
    middle = rows_mid[..., :, None] & cols_mid[..., None, :]
    return (inbox, middle)


def flat_masks(boxes):
    width = TILE * 3
    index = jnp.arange(width * width, dtype=jnp.int32)
    coarse_i = index // width // 3
    coarse_j = index % width // 3
    low_i = boxes[:, 0:1]
    low_j = boxes[:, 1:2]
    high_i = low_i + boxes[:, 2:3]
    high_j = low_j + boxes[:, 3:4]
    inbox = (coarse_i >= low_i) & (coarse_i < high_i) & (coarse_j >= low_j) & (coarse_j < high_j)
    middle = (
        (coarse_i > low_i) & (coarse_i < high_i - 1) & (coarse_j > low_j) & (coarse_j < high_j - 1)
    )
    return (inbox, middle)


def spread_table():
    width = TILE * 3
    index = jnp.arange(width * width, dtype=jnp.int32)
    owner = index // width // 3 * TILE + index % width // 3
    return (jnp.arange(TILE * TILE, dtype=jnp.int32)[:, None] == owner[None, :]).astype(jnp.float32)


def to_flat_tiles(field):
    rows, cols = field.shape
    along_x = rows // TILE
    along_y = cols // TILE
    shaped = field.reshape(along_x, TILE, along_y, TILE).transpose(0, 2, 1, 3)
    return shaped.reshape(1, 1, along_x * along_y, TILE * TILE)


def from_tiles(tiles, block_rows, block_cols):
    along_x = block_rows // TILE
    along_y = block_cols // TILE
    shaped = tiles.reshape(along_x, along_y, TILE, TILE).transpose(0, 2, 1, 3)
    return shaped.reshape(block_rows, block_cols)


def pad_last(array, before, after):
    widths = [(0, 0)] * (array.ndim - 1) + [(before, after)]
    return jnp.pad(array, widths)


def fine_substep(fine_ez, fine_hx, fine_hy, damp, gain, inbox, middle, border, cycle_value):
    width = TILE * 3
    column = jnp.arange(width * width, dtype=jnp.int32) % width
    ez_next_col = jnp.where(column < width - 1, pad_last(fine_ez[..., 1:], 0, 1), 0.0)
    ez_next_row = pad_last(fine_ez[..., width:], 0, width)
    fine_hx = jnp.where(inbox, fine_hx - HCOEF * (ez_next_col - fine_ez), 0.0)
    fine_hy = jnp.where(inbox, fine_hy + HCOEF * (ez_next_row - fine_ez), 0.0)
    hy_prev = pad_last(fine_hy[..., :-width], width, 0)
    hx_prev = jnp.where(column > 0, pad_last(fine_hx[..., :-1], 1, 0), 0.0)
    curl = fine_hy - hy_prev - (fine_hx - hx_prev)
    inner = damp * fine_ez + gain * curl
    fine_ez = jnp.where(middle, inner, jnp.where(border, cycle_value, 0.0))
    return (fine_ez, fine_hx, fine_hy)


def fine_round(
    fine_ez, fine_hx, fine_hy, damp, gain, inbox, middle, border, old_tiles, new_tiles, spread
):
    for sub in range(1, 4):
        weight = sub / 3.0
        mixed = (1.0 - weight) * old_tiles + weight * new_tiles
        cycle_value = jnp.dot(
            mixed, spread, precision=lax.Precision.HIGHEST, preferred_element_type=jnp.float32
        )
        fine_ez, fine_hx, fine_hy = fine_substep(
            fine_ez, fine_hx, fine_hy, damp, gain, inbox, middle, border, cycle_value
        )
    return (fine_ez, fine_hx, fine_hy)


def coarse_magnetic(ez, hx, hy):
    below = passed_along(ez[:1, :], "gx", -1)
    beside = passed_along(ez[:, :1], ("grp", "gy"), -1)
    ez_next_row = jnp.concatenate([ez[1:, :], below], axis=0)
    ez_next_col = jnp.concatenate([ez[:, 1:], beside], axis=1)
    hx = hx - HCOEF * (ez_next_col - ez)
    hy = hy + HCOEF * (ez_next_row - ez)
    above = passed_along(hy[-1:, :], "gx", 1)
    before = passed_along(hx[:, -1:], ("grp", "gy"), 1)
    hy_prev = jnp.concatenate([above, hy[:-1, :]], axis=0)
    hx_prev = jnp.concatenate([before, hx[:, :-1]], axis=1)
    curl = hy - hy_prev - (hx - hx_prev)
    return (hx, hy, curl)


def shards(
    coarse_ez,
    coarse_hx,
    coarse_hy,
    coarse_ids,
    mat_eps,
    mat_sig,
    fine_ez,
    fine_hx,
    fine_hy,
    fine_ids,
    boxes,
    src_cells,
    src_wave,
    rcv_cells,
):
    rows, cols = coarse_ez.shape
    fine_shape = fine_ez.shape
    flat_cells = fine_shape[-1]
    means_shape = fine_shape[:-1] + (TILE * TILE,)
    row_start = lax.axis_index("gx") * rows
    col_start = lax.axis_index(("grp", "gy")) * cols
    all_cols = cols * lax.axis_size(("grp", "gy"))
    spread = spread_table()
    damp, gain = coefficients(coarse_ids, mat_eps, mat_sig, 1.0)
    fine_damp, fine_gain = coefficients(fine_ids.reshape(-1, flat_cells), mat_eps, mat_sig, 3.0)
    owned_boxes = lax.all_to_all(boxes, "gx", split_axis=2, concat_axis=0, tiled=True).reshape(
        -1, 4
    )
    inbox, middle = flat_masks(owned_boxes)
    border = inbox & jnp.logical_not(middle)
    coarse_mid = from_tiles(box_masks(boxes, TILE, 1)[1], rows, cols)
    src_rows = (
        jnp.arange(rows, dtype=jnp.int32)[None, :] == (src_cells // all_cols - row_start)[:, None]
    ).astype(jnp.float32)
    src_cols = (
        jnp.arange(cols, dtype=jnp.int32)[None, :] == (src_cells % all_cols - col_start)[:, None]
    ).astype(jnp.float32)
    rcv_rows = (
        jnp.arange(rows, dtype=jnp.int32)[None, :] == (rcv_cells // all_cols - row_start)[:, None]
    ).astype(jnp.float32)
    rcv_cols = (
        jnp.arange(cols, dtype=jnp.int32)[None, :] == (rcv_cells % all_cols - col_start)[:, None]
    ).astype(jnp.float32)
    ez, hx, hy = (coarse_ez, coarse_hx, coarse_hy)
    field_ez = fine_ez.reshape(-1, flat_cells)
    field_hx = fine_hx.reshape(-1, flat_cells)
    field_hy = fine_hy.reshape(-1, flat_cells)
    held = lax.all_to_all(to_flat_tiles(ez), "gx", split_axis=2, concat_axis=0, tiled=True).reshape(
        -1, TILE * TILE
    )
    samples = []
    for step in range(STEPS):
        hx, hy, curl = coarse_magnetic(ez, hx, hy)
        weighted = src_rows * src_wave[step][:, None]
        drive = jnp.dot(
            weighted.T,
            src_cols,
            precision=lax.Precision.HIGHEST,
            preferred_element_type=jnp.float32,
        )
        new = damp * ez + gain * curl + drive
        old_tiles = held
        new_tiles = lax.all_to_all(
            to_flat_tiles(new), "gx", split_axis=2, concat_axis=0, tiled=True
        ).reshape(-1, TILE * TILE)
        held = new_tiles
        field_ez, field_hx, field_hy = fine_round(
            field_ez,
            field_hx,
            field_hy,
            fine_damp,
            fine_gain,
            inbox,
            middle,
            border,
            old_tiles,
            new_tiles,
            spread,
        )
        sums = lax.dot_general(
            field_ez,
            spread,
            (((1,), (1,)), ((), ())),
            precision=lax.Precision.HIGHEST,
            preferred_element_type=jnp.float32,
        )
        means = (sums / 9.0).reshape(means_shape)
        back = lax.all_to_all(means, "gx", split_axis=0, concat_axis=2, tiled=True)
        ez = jnp.where(coarse_mid, from_tiles(back, rows, cols), new)
        picked = jnp.dot(
            rcv_rows, ez, precision=lax.Precision.HIGHEST, preferred_element_type=jnp.float32
        )
        samples.append(jnp.sum(picked * rcv_cols, axis=1))
    traces = lax.psum(jnp.stack(samples), ("grp", "gx", "gy"))
    return (
        ez,
        hx,
        hy,
        field_ez.reshape(fine_shape),
        field_hx.reshape(fine_shape),
        field_hy.reshape(fine_shape),
        traces,
    )


def solution(mesh):
    placed = (
        P("gx", ("grp", "gy")),
        P("gx", ("grp", "gy")),
        P("gx", ("grp", "gy")),
        P("gx", ("grp", "gy")),
        P(),
        P(),
        P(None, ("grp", "gy"), "gx", None),
        P(None, ("grp", "gy"), "gx", None),
        P(None, ("grp", "gy"), "gx", None),
        P(None, ("grp", "gy"), "gx", None),
        P("gx", ("grp", "gy"), None, None),
        P(),
        P(),
        P(),
    )
    return jax.shard_map(
        shards,
        mesh=mesh,
        in_specs=placed,
        out_specs=(
            P("gx", ("grp", "gy")),
            P("gx", ("grp", "gy")),
            P("gx", ("grp", "gy")),
            P(None, ("grp", "gy"), "gx", None),
            P(None, ("grp", "gy"), "gx", None),
            P(None, ("grp", "gy"), "gx", None),
            P(),
        ),
        check_vma=False,
    )
```

profile of v0, /device:TPU:0, one launch (start us, length us, event | category | flops | bytes accessed | tf_op | source)
XLA Modules:
  0.0 221.0 jit_solution(844649320013483524)
XLA Ops:
  0.7 1.4 copy.34
  2.1 6.3 %all-to-all-start = ((s32[1,1,32,4]{3,1,0,2:T(1,128)}), s32[1,1,32,4]{3,1,0,2:T(1,128)S(1)}, u32[]{:S(2)}, u32[]{:S(2)}) async-start(s32[1,1,32,4]{3,1,0,2:T(1,128)} %copy.34), calls=%async_computation | async-start | bytes 32768 | tf_op jit(solution)/shard_map/all_to_all | solution.py:160
  12.6 1.6 fusion.129
  14.2 1.6 fusion.128
  51.5 4.6 %collective-permute-start.1 = (f32[1,128]{1,0:T(1,128)S(1)}, f32[1,128]{1,0:T(1,128)S(1)}, u32[]{:S(2)}, u32[]{:S(2)}) collective-permute-start(f32[1,128]{1,0:T(1,128)S(1)} %slice.384), channel_id=1, source_target_pairs={{0,4},{4,8},{8,12},{1,5},{5,9},{9,13},{2,6},{6,10},{10,14},{3,7},{... | collective-permute-start | bytes 1544 | tf_op jit(solution)/shard_map/ppermute | solution.py:17
  56.1 4.6 %collective-permute-start.3 = (f32[64,1]{1,0:T(8,128)S(1)}, f32[64,1]{1,0:T(8,128)S(1)}, u32[]{:S(2)}, u32[]{:S(2)}) collective-permute-start(f32[64,1]{1,0:T(8,128)S(1)} %slice.386), channel_id=1, source_target_pairs={{0,1},{1,2},{2,3},{3,16},{16,17},{17,18},{18,19},{4,5},{5,6},{6,7}... | collective-permute-start | bytes 776 | tf_op jit(solution)/shard_map/ppermute | solution.py:17
  60.7 4.2 %all-to-all-start.1 = ((f32[1,1,32,256]{3,1,0,2:T(1,128)}), f32[1,1,32,256]{3,1,0,2:T(1,128)S(1)}, u32[]{:S(2)}, u32[]{:S(2)}) async-start(f32[1,1,32,256]{3,1,0,2:T(1,128)} %reshape.417), calls=%async_computation.1 | async-start | bytes 65536 | tf_op jit(solution)/shard_map/all_to_all | solution.py:182
  66.3 4.3 %all-to-all-done.1 = f32[1,1,32,256]{3,1,0,2:T(1,128)S(1)} async-done(((f32[1,1,32,256]{3,1,0,2:T(1,128)}), f32[1,1,32,256]{3,1,0,2:T(1,128)S(1)}, u32[]{:S(2)}, u32[]{:S(2)}) %all-to-all-start.1) | async-done | bytes 32800 | tf_op jit(solution)/shard_map/all_to_all | solution.py:182
  70.5 3.3 %all-to-all-start.2 = ((f32[1,1,32,256]{3,1,0,2:T(1,128)}), f32[1,1,32,256]{3,1,0,2:T(1,128)S(1)}, u32[]{:S(2)}, u32[]{:S(2)}) async-start(f32[1,1,32,256]{3,1,0,2:T(1,128)} %reshape.418), calls=%async_computation.2 | async-start | bytes 65536 | tf_op jit(solution)/shard_map/all_to_all | solution.py:197
  74.1 5.3 %all-to-all-done.2 = f32[1,1,32,256]{3,1,0,2:T(1,128)S(1)} async-done(((f32[1,1,32,256]{3,1,0,2:T(1,128)}), f32[1,1,32,256]{3,1,0,2:T(1,128)S(1)}, u32[]{:S(2)}, u32[]{:S(2)}) %all-to-all-start.2) | async-done | bytes 32800 | tf_op jit(solution)/shard_map/all_to_all | solution.py:197
  83.8 1.8 fusion.28
  85.6 3.3 %all-to-all-start.3 = ((f32[4,1,8,256]{3,2,1,0:T(8,128)}), f32[4,1,8,256]{3,2,1,0:T(8,128)S(1)}, u32[]{:S(2)}, u32[]{:S(2)}) async-start(f32[4,1,8,256]{3,2,1,0:T(8,128)} %fusion.28), calls=%async_computation.3 | async-start | bytes 65536 | tf_op jit(solution)/shard_map/all_to_all | solution.py:222
  89.2 5.3 %all-to-all-done.3 = f32[4,1,8,256]{3,2,1,0:T(8,128)S(1)} async-done(((f32[4,1,8,256]{3,2,1,0:T(8,128)}), f32[4,1,8,256]{3,2,1,0:T(8,128)S(1)}, u32[]{:S(2)}, u32[]{:S(2)}) %all-to-all-start.3) | async-done | bytes 32800 | tf_op jit(solution)/shard_map/all_to_all | solution.py:222
  94.9 1.3 collective-permute-start.4
  96.2 1.3 collective-permute-start.6
  97.6 4.8 %collective-permute-done.6 = f32[64,1]{1,0:T(8,128)S(1)} collective-permute-done((f32[64,1]{1,0:T(8,128)S(1)}, f32[64,1]{1,0:T(8,128)S(1)}, u32[]{:S(2)}, u32[]{:S(2)}) %collective-permute-start.6) | collective-permute-done | bytes 288 | tf_op jit(solution)/shard_map/ppermute | solution.py:17
  102.5 4.5 %collective-permute-start.5 = (f32[1,128]{1,0:T(1,128)S(1)}, f32[1,128]{1,0:T(1,128)S(1)}, u32[]{:S(2)}, u32[]{:S(2)}) collective-permute-start(f32[1,128]{1,0:T(1,128)S(1)} %slice.402), channel_id=1, source_target_pairs={{0,4},{4,8},{8,12},{1,5},{5,9},{9,13},{2,6},{6,10},{10,14},{3,7},{... | collective-permute-start | bytes 1544 | tf_op jit(solution)/shard_map/ppermute | solution.py:17
  107.1 4.8 %collective-permute-start.7 = (f32[64,1]{1,0:T(8,128)S(1)}, f32[64,1]{1,0:T(8,128)S(1)}, u32[]{:S(2)}, u32[]{:S(2)}) collective-permute-start(f32[64,1]{1,0:T(8,128)S(1)} %slice.406), channel_id=1, source_target_pairs={{0,1},{1,2},{2,3},{3,16},{16,17},{17,18},{18,19},{4,5},{5,6},{6,7}... | collective-permute-start | bytes 776 | tf_op jit(solution)/shard_map/ppermute | solution.py:17
  112.2 1.3 collective-permute-done.7
  114.8 3.4 %all-to-all-start.4 = ((f32[1,1,32,256]{3,1,0,2:T(1,128)}), f32[1,1,32,256]{3,1,0,2:T(1,128)S(1)}, u32[]{:S(2)}, u32[]{:S(2)}) async-start(f32[1,1,32,256]{3,1,0,2:T(1,128)} %reshape.419), calls=%async_computation.4 | async-start | bytes 65536 | tf_op jit(solution)/shard_map/all_to_all | solution.py:197
  118.5 5.2 %all-to-all-done.4 = f32[1,1,32,256]{3,1,0,2:T(1,128)S(1)} async-done(((f32[1,1,32,256]{3,1,0,2:T(1,128)}), f32[1,1,32,256]{3,1,0,2:T(1,128)S(1)}, u32[]{:S(2)}, u32[]{:S(2)}) %all-to-all-start.4) | async-done | bytes 32800 | tf_op jit(solution)/shard_map/all_to_all | solution.py:197
  129.3 8.0 %all_to_all.32 = f32[4,1,8,256]{3,2,1,0:T(8,128)S(1)} all-to-all(f32[4,1,8,256]{3,2,1,0:T(8,128)S(1)} %fusion.30), channel_id=1, replica_groups=mesh['grp'=2,'gx'=4,'gy'=4] {'gx'}, dimensions={0} | all-to-all | bytes 65536 | tf_op jit(solution)/shard_map/all_to_all | solution.py:222
  137.7 1.3 collective-permute-start.10
  140.4 3.4 %collective-permute-done.10 = f32[64,1]{1,0:T(8,128)S(1)} collective-permute-done((f32[64,1]{1,0:T(8,128)S(1)}, f32[64,1]{1,0:T(8,128)S(1)}, u32[]{:S(2)}, u32[]{:S(2)}) %collective-permute-start.10) | collective-permute-done | bytes 288 | tf_op jit(solution)/shard_map/ppermute | solution.py:17
  144.6 2.6 %collective-permute-start.9 = (f32[1,128]{1,0:T(1,128)S(1)}, f32[1,128]{1,0:T(1,128)S(1)}, u32[]{:S(2)}, u32[]{:S(2)}) collective-permute-start(f32[1,128]{1,0:T(1,128)S(1)} %slice.422), channel_id=1, source_target_pairs={{0,4},{4,8},{8,12},{1,5},{5,9},{9,13},{2,6},{6,10},{10,14},{3,7},{... | collective-permute-start | bytes 1544 | tf_op jit(solution)/shard_map/ppermute | solution.py:17
  147.3 4.8 %collective-permute-start.11 = (f32[64,1]{1,0:T(8,128)S(1)}, f32[64,1]{1,0:T(8,128)S(1)}, u32[]{:S(2)}, u32[]{:S(2)}) collective-permute-start(f32[64,1]{1,0:T(8,128)S(1)} %slice.426), channel_id=1, source_target_pairs={{0,1},{1,2},{2,3},{3,16},{16,17},{17,18},{18,19},{4,5},{5,6},{6,7}... | collective-permute-start | bytes 776 | tf_op jit(solution)/shard_map/ppermute | solution.py:17
  155.0 3.3 %all-to-all-start.6 = ((f32[1,1,32,256]{3,1,0,2:T(1,128)}), f32[1,1,32,256]{3,1,0,2:T(1,128)S(1)}, u32[]{:S(2)}, u32[]{:S(2)}) async-start(f32[1,1,32,256]{3,1,0,2:T(1,128)} %reshape.420), calls=%async_computation.6 | async-start | bytes 65536 | tf_op jit(solution)/shard_map/all_to_all | solution.py:197
  158.6 5.4 %all-to-all-done.6 = f32[1,1,32,256]{3,1,0,2:T(1,128)S(1)} async-done(((f32[1,1,32,256]{3,1,0,2:T(1,128)}), f32[1,1,32,256]{3,1,0,2:T(1,128)S(1)}, u32[]{:S(2)}, u32[]{:S(2)}) %all-to-all-start.6) | async-done | bytes 32800 | tf_op jit(solution)/shard_map/all_to_all | solution.py:197
  168.3 1.8 fusion.32
  170.2 3.3 %all-to-all-start.7 = ((f32[4,1,8,256]{3,2,1,0:T(8,128)}), f32[4,1,8,256]{3,2,1,0:T(8,128)S(1)}, u32[]{:S(2)}, u32[]{:S(2)}) async-start(f32[4,1,8,256]{3,2,1,0:T(8,128)} %fusion.32), calls=%async_computation.7 | async-start | bytes 65536 | tf_op jit(solution)/shard_map/all_to_all | solution.py:222
  173.8 5.3 %all-to-all-done.7 = f32[4,1,8,256]{3,2,1,0:T(8,128)S(1)} async-done(((f32[4,1,8,256]{3,2,1,0:T(8,128)}), f32[4,1,8,256]{3,2,1,0:T(8,128)S(1)}, u32[]{:S(2)}, u32[]{:S(2)}) %all-to-all-start.7) | async-done | bytes 32800 | tf_op jit(solution)/shard_map/all_to_all | solution.py:222
  179.8 41.1 %psum.7 = f32[3,128]{1,0:T(4,128)} all-reduce(f32[3,128]{1,0:T(4,128)S(1)} %pad_maximum_fusion), channel_id=1, replica_groups=mesh['grp'=2,'gx'=4,'gy'=4] {'grp','gx','gy'}, use_global_device_ids=true, to_apply=%region_3.4 | all-reduce | flops 384 | bytes 3072 | tf_op jit(solution)/shard_map/psum | solution.py:228
  (158 shorter events, 33.5 us)
Async XLA Ops:
  0.6 46.8 %copy-start.13 = (f32[3,4]{1,0:T(4,128)S(1)}, f32[3,4]{1,0:T(4,128)}, u32[]{:S(2)}) copy-start(f32[3,4]{1,0:T(4,128)} %param.26) | copy-start | bytes 148
  0.6 46.9 %copy-start.14 = (s32[4]{0:T(128)S(1)}, s32[4]{0:T(128)}, u32[]{:S(2)}) copy-start(s32[4]{0:T(128)} %param.25) | copy-start | bytes 52
  0.7 47.0 %copy-start.4 = (s32[4,1,8,2304]{3,2,1,0:T(8,128)S(1)}, s32[4,1,8,2304]{3,2,1,0:T(8,128)}, u32[]{:S(2)}) copy-start(s32[4,1,8,2304]{3,2,1,0:T(8,128)} %param.23) | copy-start | bytes 884740
  2.1 58.6 %all-to-all-start = ((s32[1,1,32,4]{3,1,0,2:T(1,128)}), s32[1,1,32,4]{3,1,0,2:T(1,128)S(1)}, u32[]{:S(2)}, u32[]{:S(2)}) async-start(s32[1,1,32,4]{3,1,0,2:T(1,128)} %copy.34), calls=%async_computation | async-start | bytes 32768 | tf_op jit(solution)/shard_map/all_to_all | solution.py:160
  8.4 42.9 %collective-permute-start.2 = (f32[64,1]{1,0:T(8,128)}, f32[64,1]{1,0:T(8,128)S(1)}, u32[]{:S(2)}, u32[]{:S(2)}) collective-permute-start(f32[64,1]{1,0:T(8,128)} %bitcast.267), channel_id=1, source_target_pairs={{1,0},{2,1},{3,2},{16,3},{17,16},{18,17},{19,18},{5,4},{6,5},{7,6}... | collective-permute-start | bytes 776 | tf_op jit(solution)/shard_map/ppermute | solution.py:17
  10.4 41.0 %collective-permute-start = (f32[1,128]{1,0:T(1,128)S(1)}, f32[1,128]{1,0:T(1,128)S(1)}, u32[]{:S(2)}, u32[]{:S(2)}) collective-permute-start(f32[1,128]{1,0:T(1,128)S(1)} %slice.322), channel_id=1, source_target_pairs={{4,0},{8,4},{12,8},{5,1},{9,5},{13,9},{6,2},{10,6},{14,10},{7,3},{... | collective-permute-start | bytes 1544 | tf_op jit(solution)/shard_map/ppermute | solution.py:17
  48.4 1.0 copy-start
  51.5 13.5 %collective-permute-start.1 = (f32[1,128]{1,0:T(1,128)S(1)}, f32[1,128]{1,0:T(1,128)S(1)}, u32[]{:S(2)}, u32[]{:S(2)}) collective-permute-start(f32[1,128]{1,0:T(1,128)S(1)} %slice.384), channel_id=1, source_target_pairs={{0,4},{4,8},{8,12},{1,5},{5,9},{9,13},{2,6},{6,10},{10,14},{3,7},{... | collective-permute-start | bytes 1544 | tf_op jit(solution)/shard_map/ppermute | solution.py:17
  56.1 8.9 %collective-permute-start.3 = (f32[64,1]{1,0:T(8,128)S(1)}, f32[64,1]{1,0:T(8,128)S(1)}, u32[]{:S(2)}, u32[]{:S(2)}) collective-permute-start(f32[64,1]{1,0:T(8,128)S(1)} %slice.386), channel_id=1, source_target_pairs={{0,1},{1,2},{2,3},{3,16},{16,17},{17,18},{18,19},{4,5},{5,6},{6,7}... | collective-permute-start | bytes 776 | tf_op jit(solution)/shard_map/ppermute | solution.py:17
  60.7 9.9 %all-to-all-start.1 = ((f32[1,1,32,256]{3,1,0,2:T(1,128)}), f32[1,1,32,256]{3,1,0,2:T(1,128)S(1)}, u32[]{:S(2)}, u32[]{:S(2)}) async-start(f32[1,1,32,256]{3,1,0,2:T(1,128)} %reshape.417), calls=%async_computation.1 | async-start | bytes 65536 | tf_op jit(solution)/shard_map/all_to_all | solution.py:182
  65.4 8.4 %copy-start.6 = (f32[4,1,8,2304]{3,2,1,0:T(8,128)S(1)}, f32[4,1,8,2304]{3,2,1,0:T(8,128)}, u32[]{:S(2)}) copy-start(f32[4,1,8,2304]{3,2,1,0:T(8,128)} %param.21) | copy-start | bytes 884740
  65.5 8.3 %copy-start.5 = (f32[4,1,8,2304]{3,2,1,0:T(8,128)S(1)}, f32[4,1,8,2304]{3,2,1,0:T(8,128)}, u32[]{:S(2)}) copy-start(f32[4,1,8,2304]{3,2,1,0:T(8,128)} %param.22) | copy-start | bytes 884740
  70.5 8.9 %all-to-all-start.2 = ((f32[1,1,32,256]{3,1,0,2:T(1,128)}), f32[1,1,32,256]{3,1,0,2:T(1,128)S(1)}, u32[]{:S(2)}, u32[]{:S(2)}) async-start(f32[1,1,32,256]{3,1,0,2:T(1,128)} %reshape.418), calls=%async_computation.2 | async-start | bytes 65536 | tf_op jit(solution)/shard_map/all_to_all | solution.py:197
  85.6 8.9 %all-to-all-start.3 = ((f32[4,1,8,256]{3,2,1,0:T(8,128)}), f32[4,1,8,256]{3,2,1,0:T(8,128)S(1)}, u32[]{:S(2)}, u32[]{:S(2)}) async-start(f32[4,1,8,256]{3,2,1,0:T(8,128)} %fusion.28), calls=%async_computation.3 | async-start | bytes 65536 | tf_op jit(solution)/shard_map/all_to_all | solution.py:222
  94.9 7.5 %collective-permute-start.4 = (f32[1,128]{1,0:T(1,128)S(1)}, f32[1,128]{1,0:T(1,128)S(1)}, u32[]{:S(2)}, u32[]{:S(2)}) collective-permute-start(f32[1,128]{1,0:T(1,128)S(1)} %slice.401), channel_id=1, source_target_pairs={{4,0},{8,4},{12,8},{5,1},{9,5},{13,9},{6,2},{10,6},{14,10},{7,3},{... | collective-permute-start | bytes 1544 | tf_op jit(solution)/shard_map/ppermute | solution.py:17
  96.2 6.2 %collective-permute-start.6 = (f32[64,1]{1,0:T(8,128)S(1)}, f32[64,1]{1,0:T(8,128)S(1)}, u32[]{:S(2)}, u32[]{:S(2)}) collective-permute-start(f32[64,1]{1,0:T(8,128)S(1)} %bitcast.268), channel_id=1, source_target_pairs={{1,0},{2,1},{3,2},{16,3},{17,16},{18,17},{19,18},{5,4},{6,5},{7,6}... | collective-permute-start | bytes 776 | tf_op jit(solution)/shard_map/ppermute | solution.py:17
  102.5 11.0 %collective-permute-start.5 = (f32[1,128]{1,0:T(1,128)S(1)}, f32[1,128]{1,0:T(1,128)S(1)}, u32[]{:S(2)}, u32[]{:S(2)}) collective-permute-start(f32[1,128]{1,0:T(1,128)S(1)} %slice.402), channel_id=1, source_target_pairs={{0,4},{4,8},{8,12},{1,5},{5,9},{9,13},{2,6},{6,10},{10,14},{3,7},{... | collective-permute-start | bytes 1544 | tf_op jit(solution)/shard_map/ppermute | solution.py:17
  107.1 6.4 %collective-permute-start.7 = (f32[64,1]{1,0:T(8,128)S(1)}, f32[64,1]{1,0:T(8,128)S(1)}, u32[]{:S(2)}, u32[]{:S(2)}) collective-permute-start(f32[64,1]{1,0:T(8,128)S(1)} %slice.406), channel_id=1, source_target_pairs={{0,1},{1,2},{2,3},{3,16},{16,17},{17,18},{18,19},{4,5},{5,6},{6,7}... | collective-permute-start | bytes 776 | tf_op jit(solution)/shard_map/ppermute | solution.py:17
  114.8 8.9 %all-to-all-start.4 = ((f32[1,1,32,256]{3,1,0,2:T(1,128)}), f32[1,1,32,256]{3,1,0,2:T(1,128)S(1)}, u32[]{:S(2)}, u32[]{:S(2)}) async-start(f32[1,1,32,256]{3,1,0,2:T(1,128)} %reshape.419), calls=%async_computation.4 | async-start | bytes 65536 | tf_op jit(solution)/shard_map/all_to_all | solution.py:197
  137.5 2.8 %copy-start.15 = (s32[128]{0:T(128)S(1)}, s32[128]{0:T(128)}, u32[]{:S(2)}) copy-start(s32[128]{0:T(128)} %param.27) | copy-start | bytes 1540
  137.7 6.1 %collective-permute-start.10 = (f32[64,1]{1,0:T(8,128)S(1)}, f32[64,1]{1,0:T(8,128)S(1)}, u32[]{:S(2)}, u32[]{:S(2)}) collective-permute-start(f32[64,1]{1,0:T(8,128)S(1)} %bitcast.270), channel_id=1, source_target_pairs={{1,0},{2,1},{3,2},{16,3},{17,16},{18,17},{19,18},{5,4},{6,5},{7,6}... | collective-permute-start | bytes 776 | tf_op jit(solution)/shard_map/ppermute | solution.py:17
  139.0 5.5 %collective-permute-start.8 = (f32[1,128]{1,0:T(1,128)S(1)}, f32[1,128]{1,0:T(1,128)S(1)}, u32[]{:S(2)}, u32[]{:S(2)}) collective-permute-start(f32[1,128]{1,0:T(1,128)S(1)} %slice.421), channel_id=1, source_target_pairs={{4,0},{8,4},{12,8},{5,1},{9,5},{13,9},{6,2},{10,6},{14,10},{7,3},{... | collective-permute-start | bytes 1544 | tf_op jit(solution)/shard_map/ppermute | solution.py:17
  144.5 9.2 %copy-start.2 = (f32[64,128]{1,0:T(8,128)}, f32[64,128]{1,0:T(8,128)S(1)}, u32[]{:S(2)}) copy-start(f32[64,128]{1,0:T(8,128)S(1)} %get-tuple-element.77) | copy-start | bytes 98308
  144.5 9.2 %copy-start.3 = (f32[64,128]{1,0:T(8,128)}, f32[64,128]{1,0:T(8,128)S(1)}, u32[]{:S(2)}) copy-start(f32[64,128]{1,0:T(8,128)S(1)} %get-tuple-element.78) | copy-start | bytes 98308
  144.6 9.2 %collective-permute-start.9 = (f32[1,128]{1,0:T(1,128)S(1)}, f32[1,128]{1,0:T(1,128)S(1)}, u32[]{:S(2)}, u32[]{:S(2)}) collective-permute-start(f32[1,128]{1,0:T(1,128)S(1)} %slice.422), channel_id=1, source_target_pairs={{0,4},{4,8},{8,12},{1,5},{5,9},{9,13},{2,6},{6,10},{10,14},{3,7},{... | collective-permute-start | bytes 1544 | tf_op jit(solution)/shard_map/ppermute | solution.py:17
  147.3 6.4 %collective-permute-start.11 = (f32[64,1]{1,0:T(8,128)S(1)}, f32[64,1]{1,0:T(8,128)S(1)}, u32[]{:S(2)}, u32[]{:S(2)}) collective-permute-start(f32[64,1]{1,0:T(8,128)S(1)} %slice.426), channel_id=1, source_target_pairs={{0,1},{1,2},{2,3},{3,16},{16,17},{17,18},{18,19},{4,5},{5,6},{6,7}... | collective-permute-start | bytes 776 | tf_op jit(solution)/shard_map/ppermute | solution.py:17
  155.0 8.9 %all-to-all-start.6 = ((f32[1,1,32,256]{3,1,0,2:T(1,128)}), f32[1,1,32,256]{3,1,0,2:T(1,128)S(1)}, u32[]{:S(2)}, u32[]{:S(2)}) async-start(f32[1,1,32,256]{3,1,0,2:T(1,128)} %reshape.420), calls=%async_computation.6 | async-start | bytes 65536 | tf_op jit(solution)/shard_map/all_to_all | solution.py:197
  167.3 1.1 copy-start.7
  167.3 1.1 copy-start.8
  168.3 1.9 copy-start.16
  170.2 8.9 %all-to-all-start.7 = ((f32[4,1,8,256]{3,2,1,0:T(8,128)}), f32[4,1,8,256]{3,2,1,0:T(8,128)S(1)}, u32[]{:S(2)}, u32[]{:S(2)}) async-start(f32[4,1,8,256]{3,2,1,0:T(8,128)} %fusion.32), calls=%async_computation.7 | async-start | bytes 65536 | tf_op jit(solution)/shard_map/all_to_all | solution.py:222
  179.4 41.5 %copy-start.9 = (f32[64,128]{1,0:T(8,128)}, f32[64,128]{1,0:T(8,128)S(1)}, u32[]{:S(2)}) copy-start(f32[64,128]{1,0:T(8,128)S(1)} %select_n.630) | copy-start | bytes 98308
  (4 other events, 3.2 us)
where the time goes:
time: 223 us; the launch traced here: 221 us
  starting transfers between devices  60.7 us (27%)
  blocking collectives  49.1 us (22%)
  waiting for transfers between devices  41.9 us (19%)
  between operations  32.9 us (15%)
  matrix products  15.9 us (7%)
  local copies, waits for them, and re-layouts  15.3 us (7%)
  other arithmetic  5.14 us (2%)
    psum x1, blocking collectives, shards(): traces = lax.psum(jnp.stack(samples), ('grp', 'gx', 'gy'))  41.1 us
    ppermute x12, starting transfers between devices, passed_along(): lax.ppermute(value, axis, [(source, source + steps) for source in range(i...  33.7 us
    all_to_all x3, waiting for transfers between devices, shards(): lax.all_to_all(to_flat_tiles(new), 'gx', split_axis=2, concat_axis=0, til...  15.8 us
    ppermute x12, waiting for transfers between devices, passed_along(): lax.ppermute(value, axis, [(source, source + steps) for source in range(i...  11.2 us
    all_to_all x2, waiting for transfers between devices, shards(): back = lax.all_to_all(means, 'gx', split_axis=0, concat_axis=2, tiled=True)  10.7 us
    all_to_all x3, starting transfers between devices, shards(): lax.all_to_all(to_flat_tiles(new), 'gx', split_axis=2, concat_axis=0, til...  9.97 us
    dot_general x9, matrix products, fine_round(): jnp.dot(mixed, spread, precision=lax.Precision.HIGHEST, preferred_element...  9.19 us
    all_to_all x1, blocking collectives, shards(): back = lax.all_to_all(means, 'gx', split_axis=0, concat_axis=2, tiled=True)  8.01 us
  transfers between devices with their start and end apart: 19, of which 11 were waited for; matrix products, arithmetic and copies ran while one was open for 5% of the time, Pallas kernels for 0%

commit v1 on v0

--- a/solution.py
+++ b/solution.py
@@ -1,14 +1,476 @@
+import functools
+
 import jax
 import jax.numpy as jnp
 from jax import lax
+from jax.experimental import pallas as pl
+from jax.experimental.pallas import tpu as pltpu
 from jax.sharding import PartitionSpec as P
 
 TILE = 16
 STEPS = 3
-
+SUBSTEPS = 3
+LANES = 128
+FIELDS = 4
+WINDOW = 24
+BOX_ROW = FIELDS * WINDOW
+MESSAGE = BOX_ROW + 8
+PLANES = 9
 
 COURANT = 0.5
 HCOEF = 0.5
+F32 = jnp.float32
+BF16 = jnp.bfloat16
+I32 = jnp.int32
+COLS = ("grp", "gy")
+
+
+def iota(shape, axis):
+    return lax.broadcasted_iota(I32, shape, axis)
+
+
+def vmem():
+    return pl.BlockSpec(memory_space=pltpu.VMEM)
+
+
+def smem():
+    return pl.BlockSpec(memory_space=pltpu.SMEM)
+
+
+def params():
+    return pltpu.CompilerParams(vmem_limit_bytes=24 * 1024 * 1024)
+
+
+def cost(flops):
+    return pl.CostEstimate(flops=flops, bytes_accessed=1 << 20, transcendentals=0)
+
+
+def call(kernel, outs, ins, args, scratch=(), flops=1 << 20):
+    return pl.pallas_call(
+        kernel,
+        out_shape=outs,
+        in_specs=ins,
+        out_specs=jax.tree.map(lambda _: vmem(), outs),
+        scratch_shapes=list(scratch),
+        compiler_params=params(),
+        cost_estimate=cost(flops),
+    )(*args)
+
+
+def f32(*shape):
+    return jax.ShapeDtypeStruct(shape, F32)
+
+
+def ring(value, axis, steps):
+    count = lax.axis_size(axis)
+    return lax.ppermute(value, axis, [(k, (k + steps) % count) for k in range(count)])
+
+
+def pack_kernel(owners, ez, hx, hy, ids, boxes, *outs):
+    me = lax.axis_index("gx")
+    tiles = ez.shape[0] // 8
+    sub = iota((8, LANES), 0)
+    for d in range(owners):
+        g = lax.rem(me + d, owners)
+        here = pl.multiple_of(g * TILE, TILE)
+        after = pl.multiple_of(lax.rem(2 * g + 2, tiles) * 8, 8)
+        before = pl.multiple_of(lax.rem(2 * g + tiles - 1, tiles) * 8, 8)
+        for f, ref in enumerate((ez, hx, hy, ids)):
+            outs[d][f * WINDOW : f * WINDOW + TILE, :] = ref[pl.ds(here, TILE), :].astype(F32)
+            edge = jnp.where(sub < 4, ref[pl.ds(after, 8), :], ref[pl.ds(before, 8), :])
+            outs[d][f * WINDOW + TILE : (f + 1) * WINDOW, :] = edge.astype(F32)
+        outs[d][BOX_ROW:MESSAGE, :] = jnp.zeros((8, LANES), F32)
+        some = boxes[pl.ds(pl.multiple_of(g * 8, 8), 8), :]
+        outs[d][BOX_ROW:MESSAGE, 0:4] = some.astype(F32)
+
+
+def block_of(owners, d):
+    return lax.rem(lax.axis_index("gx") + owners - d, owners)
+
+
+def assemble(owners, received, store):
+    me = lax.axis_index("gx")
+    sub = iota((8, LANES), 0)
+    for d in range(owners):
+        store[block_of(owners, d)] = received[d][...]
+    for f in range(FIELDS):
+        at = f * WINDOW + TILE
+        edges = [store[a, at : at + 8, :] for a in range(owners)]
+        for a in range(owners):
+            before = jnp.where(me == 0, edges[max(a - 1, 0)], edges[a])
+            after = jnp.where(me == owners - 1, edges[min(a + 1, owners - 1)], edges[a])
+            store[a, at : at + 8, :] = jnp.where(sub < 4, after, before)
+
+
+def edges_kernel(owners, *refs):
+    received, out, store = refs[:owners], refs[owners], refs[owners + 1]
+    assemble(owners, received, store)
+    lane = iota((WINDOW, LANES), 1)
+    total = jnp.zeros((WINDOW, LANES), F32)
+    for a in range(owners):
+        for f in range(FIELDS):
+            at = 8 * (a * FIELDS + f)
+            moved = pltpu.roll(store[a, f * WINDOW : (f + 1) * WINDOW, :], at + 3, 1)
+            total = jnp.where((lane >= at) & (lane < at + 6), moved, total)
+    out[...] = total
+
+
+def source_lane(t):
+    plane = t >> 7
+    u = (plane * 11) >> 5
+    v = plane - 3 * u
+    return (3 * ((t >> 4) & 7) + u) * (3 * TILE) + 3 * (t & 15) + v
+
+
+def halves(x):
+    high = x.astype(BF16)
+    return high, (x - high.astype(F32)).astype(BF16)
+
+
+def materials(ids, eps, sig, ratio):
+    damp = jnp.zeros(ids.shape, F32)
+    gain = jnp.zeros(ids.shape, F32)
+    ones = jnp.ones((8, LANES), F32)
+    for m in range(eps.shape[0]):
+        e, s = ones * eps[m], ones * sig[m]
+        loss = s / (e * ratio)
+        d = (1.0 - loss) / (1.0 + loss)
+        g = COURANT / (e * (1.0 + loss))
+        hit = ids == float(m)
+        damp = jnp.where(hit, jnp.broadcast_to(d[0:1, 0:1], ids.shape), damp)
+        gain = jnp.where(hit, jnp.broadcast_to(g[0:1, 0:1], ids.shape), gain)
+    return damp, gain
+
+
+def spread_kernel(eps, sig, fez, fhx, fhy, ids, oez, ohx, ohy, odamp, ogain, left):
+    count = fez.shape[0]
+    rows = 2 * count
+    span = PLANES * LANES
+    for h in range(2):
+        lanes = slice(h * span, (h + 1) * span)
+        for f, ref in enumerate((fez, fhx, fhy)):
+            high, low = halves(ref[:, lanes])
+            left[2 * f * rows + h * count : 2 * f * rows + (h + 1) * count, :] = high
+            left[(2 * f + 1) * rows + h * count : (2 * f + 1) * rows + (h + 1) * count, :] = low
+        at = 6 * rows + h * count
+        left[at : at + count, :] = ids[:, lanes].astype(F32).astype(BF16)
+
+    def emit(plane, planes):
+        width = planes * LANES
+        want = source_lane(plane * LANES + iota((1, width), 1))
+        table = jnp.where(iota((span, width), 0) == want, 1.0, 0.0).astype(BF16)
+        got = jnp.dot(left[...], table, preferred_element_type=F32)
+        parts = [got[k * rows : (k + 1) * rows] for k in range(7)]
+        damp, gain = materials(parts[6], eps, sig, 3.0)
+        for ref, value in (
+            (oez, parts[0] + parts[1]),
+            (ohx, 2.0 * (parts[2] + parts[3])),
+            (ohy, 2.0 * (parts[4] + parts[5])),
+            (odamp, damp),
+            (ogain, 0.5 * gain),
+        ):
+            for k in range(planes):
+                ref[plane + k] = value[:, k * LANES : (k + 1) * LANES]
+
+    def pair(n, carry):
+        emit(2 * n, 2)
+        return carry
+
+    lax.fori_loop(0, PLANES // 2, pair, 0)
+    emit(PLANES - 1, 1)
+
+
+def gather_kernel(ez, hx, hy, oez, ohx, ohy, left):
+    rows = ez.shape[1]
+    count = rows // 2
+    span = PLANES * LANES
+    for f, ref in enumerate((ez, hx, hy)):
+        for p in range(PLANES):
+            high, low = halves(ref[p])
+            left[2 * f * rows : (2 * f + 1) * rows, p * LANES : (p + 1) * LANES] = high
+            left[(2 * f + 1) * rows : (2 * f + 2) * rows, p * LANES : (p + 1) * LANES] = low
+
+    def emit(at, width):
+        have = source_lane(iota((span, width), 0))
+        table = jnp.where(have == iota((span, width), 1) + at, 1.0, 0.0).astype(BF16)
+        got = jnp.dot(left[...], table, preferred_element_type=F32)
+        for f, ref in enumerate((oez, ohx, ohy)):
+            value = got[2 * f * rows : (2 * f + 1) * rows] + got[(2 * f + 1) * rows : (2 * f + 2) * rows]
+            for h in range(2):
+                start = pl.multiple_of(h * span + at, LANES)
+                ref[:, pl.ds(start, width)] = value[h * count : (h + 1) * count]
+
+    def pair(n, carry):
+        emit(pl.multiple_of(n * 2 * LANES, LANES), 2 * LANES)
+        return carry
+
+    lax.fori_loop(0, PLANES // 2, pair, 0)
+    emit((PLANES - 1) * LANES, LANES)
+
+
+def swap_blocks(x):
+    block = iota((8, LANES), 1) >> 4
+    sub = iota((8, LANES), 0)
+    x = jnp.take_along_axis(x, (block + sub) & 7, axis=0)
+    x = pltpu.roll(x, 0, 1, stride=TILE, stride_axis=0)
+    return jnp.take_along_axis(x, (block - sub) & 7, axis=0)
+
+
+def step_kernel(owners, all_rows, all_cols, *refs):
+    received = refs[:owners]
+    from_left, from_right, fez, fhx, fhy, fdamp, fgain = refs[owners : owners + 7]
+    eps, sig, src, wave, rcv = refs[owners + 7 : owners + 12]
+    at = owners + 12
+    oez, ohx, ohy = refs[at : at + 3]
+    back = refs[at + 3 : at + 3 + owners]
+    trace = refs[at + 3 + owners]
+    scratch = refs[at + 4 + owners :]
+    store, ez, hx, hy, damp, gain, half, drive, mid, cyc, box, held, mdamp, mgain = scratch
+    wide = 2 * LANES
+    me = lax.axis_index("gx")
+    column = lax.axis_index("grp") * lax.axis_size("gy") + lax.axis_index("gy")
+    rows = owners * TILE
+
+    assemble(owners, received, store)
+    lane = iota((WINDOW, LANES), 1)
+    row = iota((WINDOW, wide), 0)
+    row = jnp.where(row < 20, row, row - WINDOW)
+    col = iota((WINDOW, wide), 1)
+    col = jnp.where(col < LANES + 64, col, col - wide)
+    all_col = col + column * LANES
+    cells = []
+    for a in range(owners):
+        all_row = row + (a * rows + me * TILE)
+        valid = (all_row >= 0) & (all_row < all_rows) & (all_col >= 0) & (all_col < all_cols)
+        cells.append(jnp.where(valid, all_row * all_cols + all_col, -1))
+        fields = []
+        for f in range(FIELDS):
+            k = 8 * (a * FIELDS + f)
+            after = pltpu.roll(from_right[...], LANES - (k + 3), 1)
+            before = pltpu.roll(from_left[...], (LANES - 3 - k) % LANES, 1)
+            side = jnp.where(lane < 3, after, jnp.where(lane >= LANES - 3, before, 0.0))
+            main = store[a, f * WINDOW : (f + 1) * WINDOW, :]
+            both = jnp.concatenate([main, side], axis=1)
+            fields.append(jnp.where(valid, both, 0.0))
+        ez[a], hx[a], hy[a] = fields[:3]
+        d, g = materials(fields[3], eps, sig, 1.0)
+        damp[a] = jnp.where(valid, d, 0.0)
+        gain[a] = jnp.where(valid, g, 0.0)
+        half[a] = jnp.where(valid, HCOEF, 0.0)
+    for n in range(STEPS):
+        for a in range(owners):
+            total = jnp.zeros((WINDOW, wide), F32)
+            for k in range(src.shape[0]):
+                total = total + jnp.where(cells[a] == src[k], wave[n, k], 0.0)
+            drive[n, a] = total
+
+    tile_lane = iota((8, LANES), 1)
+    tile_col = (tile_lane & 15).astype(F32)
+    for a in range(owners):
+        sizes = store[a, BOX_ROW:MESSAGE, :]
+        low_i, low_j, size_i, size_j = (sizes[:, k : k + 1] for k in range(4))
+        high_i, high_j = low_i + size_i, low_j + size_j
+        for h in range(2):
+            i = (8 * h + (tile_lane >> 4)).astype(F32)
+            inside = (i >= low_i) & (i < high_i) & (tile_col >= low_j) & (tile_col < high_j)
+            middle = (i > low_i) & (i < high_i - 1) & (tile_col > low_j) & (tile_col < high_j - 1)
+            at_rows = slice((h * owners + a) * 8, (h * owners + a + 1) * 8)
+            mid[at_rows] = jnp.where(middle, 1.0, 0.0)
+            box[at_rows] = jnp.where(inside, 1.0, 0.0)
+            held[at_rows] = swap_blocks(ez[a, 8 * h : 8 * h + 8, 0:LANES])
+    for p in range(PLANES):
+        mdamp[p] = fdamp[p] * mid[...]
+        mgain[p] = fgain[p] * mid[...]
+        oez[p], ohx[p], ohy[p] = fez[p], fhx[p], fhy[p]
+
+    count = 8 * owners
+    lanes = iota((count, LANES), 1)
+    first, second = slice(0, count), slice(count, 2 * count)
+
+    def after_row(ref, p):
+        a, b = (pltpu.roll(ref[p, s], LANES - TILE, 1) for s in (first, second))
+        return jnp.where(lanes < LANES - TILE, a, b), b
+
+    def before_row(ref, p):
+        a, b = (pltpu.roll(ref[p, s], TILE, 1) for s in (first, second))
+        return a, jnp.where(lanes < TILE, a, b)
+
+    def substep(m, new_tiles):
+        weight = (m + 1).astype(F32) * (1.0 / SUBSTEPS)
+        cyc[...] = (box[...] - mid[...]) * ((1.0 - weight) * held[...] + weight * new_tiles)
+        down = [after_row(oez, v) for v in range(3)]
+        for u in range(3):
+            for v in range(3):
+                p = 3 * u + v
+                for h, s in enumerate((first, second)):
+                    e = oez[p, s]
+                    right = oez[p + 1, s] if v < 2 else pltpu.roll(oez[3 * u, s], LANES - 1, 1)
+                    below = oez[p + 3, s] if u < 2 else down[v][h]
+                    ohx[p, s] = ohx[p, s] - (right - e)
+                    ohy[p, s] = ohy[p, s] + (below - e)
+        up = [before_row(ohy, 6 + v) for v in range(3)]
+        for u in range(3):
+            for v in range(3):
+                p = 3 * u + v
+                for h, s in enumerate((first, second)):
+                    left = ohx[p - 1, s] if v > 0 else pltpu.roll(ohx[3 * u + 2, s], 1, 1)
+                    above = ohy[p - 3, s] if u > 0 else up[v][h]
+                    curl = (ohy[p, s] - above) - (ohx[p, s] - left)
+                    oez[p, s] = mdamp[p, s] * oez[p, s] + mgain[p, s] * curl + cyc[s]
+        return new_tiles
+
+    def step(n, carry):
+        for a in range(owners):
+            e = ez[a]
+            x = hx[a] - half[a] * (pltpu.roll(e, wide - 1, 1) - e)
+            y = hy[a] + half[a] * (pltpu.roll(e, WINDOW - 1, 0) - e)
+            curl = (y - pltpu.roll(y, 1, 0)) - (x - pltpu.roll(x, 1, 1))
+            hx[a], hy[a] = x, y
+            ez[a] = damp[a] * e + gain[a] * curl + drive[n, a]
+        new_tiles = jnp.concatenate(
+            [
+                swap_blocks(ez[a, 8 * h : 8 * h + 8, 0:LANES])
+                for h in range(2)
+                for a in range(owners)
+            ],
+            axis=0,
+        )
+        lax.fori_loop(0, SUBSTEPS, substep, new_tiles)
+        total = oez[0]
+        for p in range(1, PLANES):
+            total = total + oez[p]
+        now = jnp.where(mid[...] > 0.0, total / 9.0, new_tiles)
+        held[...] = now
+        picked = []
+        for a in range(owners):
+            for h in range(2):
+                image = swap_blocks(now[(h * owners + a) * 8 : (h * owners + a + 1) * 8])
+                ez[a, 8 * h : 8 * h + 8, 0:LANES] = image
+                picked.append(image)
+        image = jnp.concatenate(picked, axis=0)
+        block = iota((owners * TILE, LANES), 0)
+        image_row = (block >> 4) * rows + me * TILE + (block & 15)
+        row_hit = jnp.where(image_row == rcv[0:1, :], 1.0, 0.0)
+        col_hit = iota((LANES, rcv.shape[1]), 0) + column * LANES == rcv[1:2, :]
+        mixed = lax.dot_general(
+            image,
+            row_hit,
+            (((0,), (0,)), ((), ())),
+            precision=lax.Precision.HIGHEST,
+            preferred_element_type=F32,
+        )
+        trace[pl.ds(n, 1), :] = jnp.sum(jnp.where(col_hit, mixed, 0.0), axis=0, keepdims=True)
+        return carry
+
+    trace[...] = jnp.zeros(trace.shape, F32)
+    lax.fori_loop(0, STEPS, step, 0)
+    for p in range(PLANES):
+        ohx[p] = 0.5 * (ohx[p] * box[...])
+        ohy[p] = 0.5 * (ohy[p] * box[...])
+    for d in range(owners):
+        a = block_of(owners, d)
+        for f, ref in enumerate((ez, hx, hy)):
+            back[d][f * TILE : (f + 1) * TILE, :] = ref[a, 0:TILE, 0:LANES]
+
+
+def place_kernel(owners, *refs):
+    pieces = refs[:owners]
+    traces = refs[owners]
+    outs = refs[owners + 1 : owners + 4]
+    out_trace = refs[owners + 4]
+    me = lax.axis_index("gx")
+    for d in range(owners):
+        g = lax.rem(me + d, owners)
+        for f in range(3):
+            outs[f][pl.ds(pl.multiple_of(g * TILE, TILE), TILE), :] = pieces[d][f * TILE : (f + 1) * TILE, :]
+    out_trace[...] = jnp.sum(traces[...], axis=0)[0:STEPS]
+
+
+def fast_shards(
+    all_rows,
+    coarse_ez,
+    coarse_hx,
+    coarse_hy,
+    coarse_ids,
+    mat_eps,
+    mat_sig,
+    fine_ez,
+    fine_hx,
+    fine_hy,
+    fine_ids,
+    boxes,
+    src_cells,
+    src_wave,
+    rcv_cells,
+):
+    owners = lax.axis_size("gx")
+    rows, cols = coarse_ez.shape
+    all_cols = cols * lax.axis_size(COLS)
+    fine_shape = fine_ez.shape
+    count = fine_shape[0] * fine_shape[2]
+    receivers = rcv_cells.shape[0]
+    flat = [x.reshape(count, fine_shape[-1]) for x in (fine_ez, fine_hx, fine_hy, fine_ids)]
+    messages = call(
+        functools.partial(pack_kernel, owners),
+        tuple(f32(MESSAGE, cols) for _ in range(owners)),
+        [vmem()] * 5,
+        (coarse_ez, coarse_hx, coarse_hy, coarse_ids, boxes.reshape(boxes.shape[2:])),
+    )
+    received = [messages[0]] + [ring(messages[d], "gx", d) for d in range(1, owners)]
+    planes = call(
+        spread_kernel,
+        tuple(f32(PLANES, 2 * count, LANES) for _ in range(5)),
+        [smem()] * 2 + [vmem()] * 4,
+        (mat_eps, mat_sig, *flat),
+        [pltpu.VMEM((14 * count, PLANES * LANES), BF16)],
+        1 << 31,
+    )
+    edges = call(
+        functools.partial(edges_kernel, owners),
+        f32(WINDOW, LANES),
+        [vmem()] * owners,
+        received,
+        [pltpu.VMEM((owners, MESSAGE, LANES), F32)],
+    )
+    from_left = ring(edges, COLS, 1)
+    from_right = ring(edges, COLS, -1)
+    picks = jnp.stack([rcv_cells // all_cols, rcv_cells % all_cols])
+    window = (owners, WINDOW, 2 * LANES)
+    tiles = (2 * count, LANES)
+    results = call(
+        functools.partial(step_kernel, owners, all_rows, all_cols),
+        tuple(f32(PLANES, 2 * count, LANES) for _ in range(3))
+        + tuple(f32(3 * TILE, LANES) for _ in range(owners))
+        + (f32(8, receivers),),
+        [vmem()] * (owners + 7) + [smem()] * 4 + [vmem()],
+        (*received, from_left, from_right, *planes, mat_eps, mat_sig, src_cells, src_wave, picks),
+        [pltpu.VMEM((owners, MESSAGE, LANES), F32)]
+        + [pltpu.VMEM(window, F32)] * 6
+        + [pltpu.VMEM((STEPS,) + window, F32)]
+        + [pltpu.VMEM(tiles, F32)] * 4
+        + [pltpu.VMEM((PLANES,) + tiles, F32)] * 2,
+        1 << 30,
+    )
+    fine, back, trace = results[:3], results[3 : 3 + owners], results[3 + owners]
+    every = ("grp", "gx", "gy")
+    copies = jnp.broadcast_to(trace[None], (lax.axis_size(every),) + trace.shape)
+    traces = lax.all_to_all(copies, every, 0, 0)
+    pieces = [back[0]] + [ring(back[d], "gx", owners - d) for d in range(1, owners)]
+    finals = call(
+        gather_kernel,
+        tuple(f32(count, fine_shape[-1]) for _ in range(3)),
+        [vmem()] * 3,
+        fine,
+        [pltpu.VMEM((12 * count, PLANES * LANES), BF16)],
+        1 << 31,
+    )
+    ends = call(
+        functools.partial(place_kernel, owners),
+        tuple(f32(rows, cols) for _ in range(3)) + (f32(STEPS, receivers),),
+        [vmem()] * (owners + 1),
+        (*pieces, traces),
+    )
+    return (*ends[:3], *(x.reshape(fine_shape) for x in finals), ends[3])
 
 
 def passed_along(value, axis, steps):
@@ -254,8 +716,15 @@
         P(),
         P(),
     )
+    def body(*args):
+        rows, cols = args[0].shape
+        owned = args[6].shape[2] * TILE
+        if cols == LANES and owned == cols and rows == lax.axis_size("gx") * TILE:
+            return fast_shards(rows * lax.axis_size("gx"), *args)
+        return shards(*args)
+
     return jax.shard_map(
-        shards,
+        body,
         mesh=mesh,
         in_specs=placed,
         out_specs=(

time: 223 us -> 44.7 us (0.20)
  blocking collectives: 49.1 us -> 0 us
  starting transfers between devices: 60.7 us -> 16.8 us
  waiting for transfers between devices: 41.9 us -> 3.71 us
  between operations: 32.9 us -> 0.73 us
  matrix products: 15.9 us -> 0 us
  Pallas kernels: 0 us -> 13.1 us
  local copies, waits for them, and re-layouts: 15.3 us -> 9.66 us
  other arithmetic: 5.14 us -> 0.02 us
    psum x1 -> x0, blocking collectives: 41.1 us -> none  [shards(): traces = lax.psum(jnp.stack(samples), ('grp', 'gx', 'gy'))]
    all_to_all x7 -> x1, waiting for transfers between devices: 30.7 us -> 0.01 us  [fast_shards(): traces = lax.all_to_all(copies, every, 0, 0)]
    all_to_all x7 -> x1, starting transfers between devices: 27 us -> 2.96 us  [fast_shards(): traces = lax.all_to_all(copies, every, 0, 0)]
    ppermute x12 -> x8, starting transfers between devices: 33.7 us -> 13.9 us  [ring(): lax.ppermute(value, axis, [(k, (k + steps) % count) for k in range(count)])]
    dot_general x18 -> x0, matrix products: 15.9 us -> none  [the longest x9 9.19 us: fine_round(): jnp.dot(mixed, spread, precision=lax.Precision.HIGHEST, preferred_element...]
    pallas_call x0 -> x6, Pallas kernels: none -> 13.1 us  [call(): pl.pallas_call(kernel, out_shape=outs, in_specs=ins, out_specs=jax.tree.m...]
    all_to_all x1 -> x0, blocking collectives: 8.01 us -> none  [shards(): back = lax.all_to_all(means, 'gx', split_axis=0, concat_axis=2, tiled=True)]
    ppermute x12 -> x8, waiting for transfers between devices: 11.2 us -> 3.71 us  [ring(): lax.ppermute(value, axis, [(k, (k + steps) % count) for k in range(count)])]
  transfers between devices with their start and end apart: 19 -> 9, of which waited for: 11 -> 3; matrix products, arithmetic and copies ran while one was open for 5% -> 0% of each run, Pallas kernels for 0% -> 16%
where the time goes in v1:
time: 44.7 us; the launch traced here: 44.1 us
  starting transfers between devices  16.8 us (38%)
  Pallas kernels  13.1 us (29%)
  local copies, waits for them, and re-layouts  9.66 us (22%)
  waiting for transfers between devices  3.71 us (8%)
  between operations  0.73 us (2%)
    ppermute x8, starting transfers between devices, ring(): lax.ppermute(value, axis, [(k, (k + steps) % count) for k in range(count)])  13.9 us
    pallas_call x6, Pallas kernels, call(): pl.pallas_call(kernel, out_shape=outs, in_specs=ins, out_specs=jax.tree.m...  13.1 us
    unnamed x26, local copies, waits for them, and re-layouts  8.22 us
    ppermute x8, waiting for transfers between devices, ring(): lax.ppermute(value, axis, [(k, (k + steps) % count) for k in range(count)])  3.71 us
    all_to_all x1, starting transfers between devices, fast_shards(): traces = lax.all_to_all(copies, every, 0, 0)  2.96 us
  transfers between devices with their start and end apart: 9, of which 3 were waited for; matrix products, arithmetic and copies ran while one was open for 0% of the time, Pallas kernels for 16%

profile of v1, /device:TPU:0, one launch (start us, length us, event | category | flops | bytes accessed | tf_op | source)
XLA Modules:
  0.0 44.1 jit_solution(10962130962293642678)
XLA Ops:
  0.6 0.8 %copy.21.boxes = s32[32,4]{1,0:T(8,128)S(1)} copy(s32[32,4]{0,1:T(4,128)} %bitcast.22) | data formatting | bytes 1024 | tf_op jit(solution)/shard_map/reshape | solution.py:417
  1.4 0.8 %copy-done = f32[64,128]{1,0:T(8,128)S(1)} copy-done((f32[64,128]{1,0:T(8,128)S(1)}, f32[64,128]{1,0:T(8,128)}, u32[]{:S(2)}) %copy-start) | copy-done | bytes 32792
  2.2 0.8 %copy-done.1 = f32[64,128]{1,0:T(8,128)S(1)} copy-done((f32[64,128]{1,0:T(8,128)S(1)}, f32[64,128]{1,0:T(8,128)}, u32[]{:S(2)}) %copy-start.1) | copy-done | bytes 32792
  2.9 0.8 %copy-done.2 = f32[64,128]{1,0:T(8,128)S(1)} copy-done((f32[64,128]{1,0:T(8,128)S(1)}, f32[64,128]{1,0:T(8,128)}, u32[]{:S(2)}) %copy-start.2) | copy-done | bytes 32792
  3.7 0.8 %copy-done.3 = s32[64,128]{1,0:T(8,128)S(1)} copy-done((s32[64,128]{1,0:T(8,128)S(1)}, s32[64,128]{1,0:T(8,128)}, u32[]{:S(2)}) %copy-start.3) | copy-done | bytes 32792
  4.5 3.1 %collective-permute-start = (f32[104,128]{1,0:T(8,128)S(1)}, f32[104,128]{1,0:T(8,128)S(1)}, u32[]{:S(2)}, u32[]{:S(2)}) collective-permute-start(f32[104,128]{1,0:T(8,128)S(1)} %get-tuple-element.32), channel_id=1, source_target_pairs={{0,4},{4,8},{8,12},{12,0},{1,5},{5,9},{9,13},{13,1},{2,6},{6,10},{... | collective-permute-start | bytes 159752 | tf_op jit(solution)/shard_map/ppermute | solution.py:66
  7.6 2.6 %collective-permute-start.1 = (f32[104,128]{1,0:T(8,128)S(1)}, f32[104,128]{1,0:T(8,128)S(1)}, u32[]{:S(2)}, u32[]{:S(2)}) collective-permute-start(f32[104,128]{1,0:T(8,128)S(1)} %get-tuple-element.33), channel_id=1, source_target_pairs={{0,8},{4,12},{8,0},{12,4},{1,9},{5,13},{9,1},{13,5},{2,10},{6,14},... | collective-permute-start | bytes 159752 | tf_op jit(solution)/shard_map/ppermute | solution.py:66
  10.2 1.3 %collective-permute-start.2 = (f32[104,128]{1,0:T(8,128)S(1)}, f32[104,128]{1,0:T(8,128)S(1)}, u32[]{:S(2)}, u32[]{:S(2)}) collective-permute-start(f32[104,128]{1,0:T(8,128)S(1)} %get-tuple-element.34), channel_id=1, source_target_pairs={{0,12},{4,0},{8,4},{12,8},{1,13},{5,1},{9,5},{13,9},{2,14},{6,2},{... | collective-permute-start | bytes 159752 | tf_op jit(solution)/shard_map/ppermute | solution.py:66
  11.5 0.0 copy-start.9
  11.5 0.0 copy-start.10
  11.6 0.6 %copy-done.9 = f32[8]{0:T(128)S(1)} copy-done((f32[8]{0:T(128)S(1)}, f32[8]{0:T(128)}, u32[]{:S(2)}) %copy-start.9) | copy-done | bytes 56
  12.2 0.0 copy-done.10
  12.2 1.0 %copy-done.4 = f32[4,1,8,2304]{3,2,1,0:T(8,128)S(1)} copy-done((f32[4,1,8,2304]{3,2,1,0:T(8,128)S(1)}, f32[4,1,8,2304]{3,2,1,0:T(8,128)}, u32[]{:S(2)}) %copy-start.4) | copy-done | bytes 294936
  13.2 1.0 %copy-done.5 = f32[4,1,8,2304]{3,2,1,0:T(8,128)S(1)} copy-done((f32[4,1,8,2304]{3,2,1,0:T(8,128)S(1)}, f32[4,1,8,2304]{3,2,1,0:T(8,128)}, u32[]{:S(2)}) %copy-start.5) | copy-done | bytes 294936
  14.1 1.0 %copy-done.6 = f32[4,1,8,2304]{3,2,1,0:T(8,128)S(1)} copy-done((f32[4,1,8,2304]{3,2,1,0:T(8,128)S(1)}, f32[4,1,8,2304]{3,2,1,0:T(8,128)}, u32[]{:S(2)}) %copy-start.6) | copy-done | bytes 294936
  15.1 1.0 %copy-done.7 = s32[4,1,8,2304]{3,2,1,0:T(8,128)S(1)} copy-done((s32[4,1,8,2304]{3,2,1,0:T(8,128)S(1)}, s32[4,1,8,2304]{3,2,1,0:T(8,128)}, u32[]{:S(2)}) %copy-start.7) | copy-done | bytes 294936
  16.1 3.2 %shard_map.191 = (f32[9,64,128]{2,1,0:T(8,128)S(1)}, f32[9,64,128]{2,1,0:T(8,128)S(1)}, f32[9,64,128]{2,1,0:T(8,128)S(1)}, f32[9,64,128]{2,1,0:T(8,128)S(1)}, f32[9,64,128]{2,1,0:T(8,128)S(1)}) custom-call(f32[8]{0:T(128)S(1)} %copy-done.9, f32[8]{0:T(128)S(1)} %copy-done.10, f32[32,2304]{1,0:T(8,128)S(1)} %bitcast.18, f32[32,2304]{1,0:T(8,128)S(1)} %bitcast.19, ...), custom_call_target="tpu_custom_call" | custom-call | flops 2147483648 | bytes 1048576 | tf_op jit(solution)/shard_map/pallas_call | solution.py:49
  19.3 0.0 collective-permute-done.refs_1_
  19.3 0.1 shard_map.190
  19.5 1.1 %collective-permute-start.4 = (f32[24,128]{1,0:T(8,128)S(1)}, f32[24,128]{1,0:T(8,128)S(1)}, u32[]{:S(2)}, u32[]{:S(2)}) collective-permute-start(f32[24,128]{1,0:T(8,128)S(1)} %shard_map.190), channel_id=1, source_target_pairs={{0,19},{1,0},{2,1},{3,2},{16,3},{17,16},{18,17},{19,18},{4,23},{5,... | collective-permute-start | bytes 36872 | tf_op jit(solution)/shard_map/ppermute | solution.py:66
  20.6 1.0 %collective-permute-start.3 = (f32[24,128]{1,0:T(8,128)S(1)}, f32[24,128]{1,0:T(8,128)S(1)}, u32[]{:S(2)}, u32[]{:S(2)}) collective-permute-start(f32[24,128]{1,0:T(8,128)S(1)} %shard_map.190), channel_id=1, source_target_pairs={{0,1},{1,2},{2,3},{3,16},{16,17},{17,18},{18,19},{19,0},{4,5},{5,6... | collective-permute-start | bytes 36872 | tf_op jit(solution)/shard_map/ppermute | solution.py:66
  21.6 1.7 %collective-permute-done.4.refs_5_ = f32[24,128]{1,0:T(8,128)S(1)} collective-permute-done((f32[24,128]{1,0:T(8,128)S(1)}, f32[24,128]{1,0:T(8,128)S(1)}, u32[]{:S(2)}, u32[]{:S(2)}) %collective-permute-start.4) | collective-permute-done | bytes 12320 | tf_op jit(solution)/shard_map/ppermute | solution.py:66
  23.2 1.4 %collective-permute-done.3.refs_4_ = f32[24,128]{1,0:T(8,128)S(1)} collective-permute-done((f32[24,128]{1,0:T(8,128)S(1)}, f32[24,128]{1,0:T(8,128)S(1)}, u32[]{:S(2)}, u32[]{:S(2)}) %collective-permute-start.3) | collective-permute-done | bytes 12320 | tf_op jit(solution)/shard_map/ppermute | solution.py:66
  24.6 0.7 %copy-done.8 = f32[3,4]{1,0:T(4,128)S(1)} copy-done((f32[3,4]{1,0:T(4,128)S(1)}, f32[3,4]{1,0:T(4,128)}, u32[]{:S(2)}) %copy-start.8) | copy-done | bytes 72
  25.3 5.2 %shard_map.192 = (f32[9,64,128]{2,1,0:T(8,128)S(1)}, f32[9,64,128]{2,1,0:T(8,128)S(1)}, f32[9,64,128]{2,1,0:T(8,128)S(1)}, f32[48,128]{1,0:T(8,128)S(1)}, f32[48...) custom-call(f32[104,128]{1,0:T(8,128)S(1)} %get-tuple-element.31.refs_0_, ...), custom_call_target="tpu_custom_call" | custom-call | flops 1073741824 | bytes 1048576 | tf_op jit(solution)/shard_map/pallas_call | solution.py:49
  30.5 0.7 %broadcast_in_dim.2 = f32[32,8,128]{2,1,0:T(8,128)} broadcast(f32[8,128]{1,0:T(8,128)S(1)} %get-tuple-element.44), dimensions={1,2} | broadcast | bytes 135168 | tf_op jit(solution)/shard_map/broadcast_in_dim | solution.py:456
  31.1 3.0 %all-to-all-start = ((f32[32,8,128]{2,1,0:T(8,128)}), f32[32,8,128]{2,1,0:T(8,128)S(1)}, u32[]{:S(2)}, u32[]{:S(2)}) async-start(f32[32,8,128]{2,1,0:T(8,128)} %broadcast_in_dim.2), calls=%async_computation | async-start | bytes 262144 | tf_op jit(solution)/shard_map/all_to_all | solution.py:457
  34.1 3.7 %collective-permute-start.5 = (f32[48,128]{1,0:T(8,128)S(1)}, f32[48,128]{1,0:T(8,128)S(1)}, u32[]{:S(2)}, u32[]{:S(2)}) collective-permute-start(f32[48,128]{1,0:T(8,128)S(1)} %get-tuple-element.41), channel_id=1, source_target_pairs={{0,12},{4,0},{8,4},{12,8},{1,13},{5,1},{9,5},{13,9},{2,14},{6,2},{... | collective-permute-start | bytes 73736 | tf_op jit(solution)/shard_map/ppermute | solution.py:66
  37.8 1.1 %collective-permute-start.7 = (f32[48,128]{1,0:T(8,128)S(1)}, f32[48,128]{1,0:T(8,128)S(1)}, u32[]{:S(2)}, u32[]{:S(2)}) collective-permute-start(f32[48,128]{1,0:T(8,128)S(1)} %get-tuple-element.43), channel_id=1, source_target_pairs={{0,4},{4,8},{8,12},{12,0},{1,5},{5,9},{9,13},{13,1},{2,6},{6,10},{... | collective-permute-start | bytes 73736 | tf_op jit(solution)/shard_map/ppermute | solution.py:66
  38.8 3.9 %shard_map.194 = (f32[32,2304]{1,0:T(8,128)}, f32[32,2304]{1,0:T(8,128)}, f32[32,2304]{1,0:T(8,128)}) custom-call(f32[9,64,128]{2,1,0:T(8,128)S(1)} %get-tuple-element.48.ez, f32[9,64,128]{2,1,0:T(8,128)S(1)} %get-tuple-element.49.hx, f32[9,64,128]{2,1,0:T(8,128)S(1)} %get-tuple-element.50.hy), custom_call_target="tpu_custom_call" | custom-call | flops 2147483648 | bytes 1048576 | tf_op jit(solution)/shard_map/pallas_call | solution.py:49
  42.7 0.7 %collective-permute-done.7.refs_3_ = f32[48,128]{1,0:T(8,128)S(1)} collective-permute-done((f32[48,128]{1,0:T(8,128)S(1)}, f32[48,128]{1,0:T(8,128)S(1)}, u32[]{:S(2)}, u32[]{:S(2)}) %collective-permute-start.7) | collective-permute-done | bytes 24608 | tf_op jit(solution)/shard_map/ppermute | solution.py:66
  43.4 0.7 %shard_map.193 = (f32[64,128]{1,0:T(8,128)}, f32[64,128]{1,0:T(8,128)}, f32[64,128]{1,0:T(8,128)}, f32[3,128]{1,0:T(4,128)}) custom-call(f32[48,128]{1,0:T(8,128)S(1)} %get-tuple-element.40.refs_0_, f32[48,128]{1,0:T(8,128)S(1)} %collective-permute-done.5.refs_1_, f32[48,128]{1,0:T(8,128)S(1)} %collective-permute-done.6.refs_2_, ...), custom_call_target="tpu_custom_call" | custom-call | flops 1048576 | bytes 1048576 | tf_op jit(solution)/shard_map/pallas_call | solution.py:49
  (22 shorter events, 0.1 us)
Async XLA Ops:
  1.4 0.8 %copy-start = (f32[64,128]{1,0:T(8,128)S(1)}, f32[64,128]{1,0:T(8,128)}, u32[]{:S(2)}) copy-start(f32[64,128]{1,0:T(8,128)} %ez.1) | copy-start | bytes 98308
  2.2 0.8 %copy-start.1 = (f32[64,128]{1,0:T(8,128)S(1)}, f32[64,128]{1,0:T(8,128)}, u32[]{:S(2)}) copy-start(f32[64,128]{1,0:T(8,128)} %hx.1) | copy-start | bytes 98308
  2.9 0.8 %copy-start.2 = (f32[64,128]{1,0:T(8,128)S(1)}, f32[64,128]{1,0:T(8,128)}, u32[]{:S(2)}) copy-start(f32[64,128]{1,0:T(8,128)} %hy.1) | copy-start | bytes 98308
  3.7 0.8 %copy-start.3 = (s32[64,128]{1,0:T(8,128)S(1)}, s32[64,128]{1,0:T(8,128)}, u32[]{:S(2)}) copy-start(s32[64,128]{1,0:T(8,128)} %ids.1) | copy-start | bytes 98308
  4.5 14.8 %collective-permute-start = (f32[104,128]{1,0:T(8,128)S(1)}, f32[104,128]{1,0:T(8,128)S(1)}, u32[]{:S(2)}, u32[]{:S(2)}) collective-permute-start(f32[104,128]{1,0:T(8,128)S(1)} %get-tuple-element.32), channel_id=1, source_target_pairs={{0,4},{4,8},{8,12},{12,0},{1,5},{5,9},{9,13},{13,1},{2,6},{6,10},{... | collective-permute-start | bytes 159752 | tf_op jit(solution)/shard_map/ppermute | solution.py:66
  7.6 3.9 %copy-start.12 = (s32[128]{0:T(128)S(1)}, s32[128]{0:T(128)}, u32[]{:S(2)}) copy-start(s32[128]{0:T(128)} %param.27) | copy-start | bytes 1540
  7.6 11.7 %collective-permute-start.1 = (f32[104,128]{1,0:T(8,128)S(1)}, f32[104,128]{1,0:T(8,128)S(1)}, u32[]{:S(2)}, u32[]{:S(2)}) collective-permute-start(f32[104,128]{1,0:T(8,128)S(1)} %get-tuple-element.33), channel_id=1, source_target_pairs={{0,8},{4,12},{8,0},{12,4},{1,9},{5,13},{9,1},{13,5},{2,10},{6,14},... | collective-permute-start | bytes 159752 | tf_op jit(solution)/shard_map/ppermute | solution.py:66
  10.2 9.1 %collective-permute-start.2 = (f32[104,128]{1,0:T(8,128)S(1)}, f32[104,128]{1,0:T(8,128)S(1)}, u32[]{:S(2)}, u32[]{:S(2)}) collective-permute-start(f32[104,128]{1,0:T(8,128)S(1)} %get-tuple-element.34), channel_id=1, source_target_pairs={{0,12},{4,0},{8,4},{12,8},{1,13},{5,1},{9,5},{13,9},{2,14},{6,2},{... | collective-permute-start | bytes 159752 | tf_op jit(solution)/shard_map/ppermute | solution.py:66
  11.5 0.7 %copy-start.9 = (f32[8]{0:T(128)S(1)}, f32[8]{0:T(128)}, u32[]{:S(2)}) copy-start(f32[8]{0:T(128)} %refs_11_.1) | copy-start | bytes 100
  11.5 0.7 %copy-start.10 = (f32[8]{0:T(128)S(1)}, f32[8]{0:T(128)}, u32[]{:S(2)}) copy-start(f32[8]{0:T(128)} %refs_12_.1) | copy-start | bytes 100
  12.2 1.0 %copy-start.4 = (f32[4,1,8,2304]{3,2,1,0:T(8,128)S(1)}, f32[4,1,8,2304]{3,2,1,0:T(8,128)}, u32[]{:S(2)}) copy-start(f32[4,1,8,2304]{3,2,1,0:T(8,128)} %param.20) | copy-start | bytes 884740
  13.2 1.0 %copy-start.5 = (f32[4,1,8,2304]{3,2,1,0:T(8,128)S(1)}, f32[4,1,8,2304]{3,2,1,0:T(8,128)}, u32[]{:S(2)}) copy-start(f32[4,1,8,2304]{3,2,1,0:T(8,128)} %param.21) | copy-start | bytes 884740
  14.1 1.0 %copy-start.6 = (f32[4,1,8,2304]{3,2,1,0:T(8,128)S(1)}, f32[4,1,8,2304]{3,2,1,0:T(8,128)}, u32[]{:S(2)}) copy-start(f32[4,1,8,2304]{3,2,1,0:T(8,128)} %param.22) | copy-start | bytes 884740
  15.1 1.0 %copy-start.7 = (s32[4,1,8,2304]{3,2,1,0:T(8,128)S(1)}, s32[4,1,8,2304]{3,2,1,0:T(8,128)}, u32[]{:S(2)}) copy-start(s32[4,1,8,2304]{3,2,1,0:T(8,128)} %param.23) | copy-start | bytes 884740
  19.5 3.8 %collective-permute-start.4 = (f32[24,128]{1,0:T(8,128)S(1)}, f32[24,128]{1,0:T(8,128)S(1)}, u32[]{:S(2)}, u32[]{:S(2)}) collective-permute-start(f32[24,128]{1,0:T(8,128)S(1)} %shard_map.190), channel_id=1, source_target_pairs={{0,19},{1,0},{2,1},{3,2},{16,3},{17,16},{18,17},{19,18},{4,23},{5,... | collective-permute-start | bytes 36872 | tf_op jit(solution)/shard_map/ppermute | solution.py:66
  20.6 4.0 %collective-permute-start.3 = (f32[24,128]{1,0:T(8,128)S(1)}, f32[24,128]{1,0:T(8,128)S(1)}, u32[]{:S(2)}, u32[]{:S(2)}) collective-permute-start(f32[24,128]{1,0:T(8,128)S(1)} %shard_map.190), channel_id=1, source_target_pairs={{0,1},{1,2},{2,3},{3,16},{16,17},{17,18},{18,19},{19,0},{4,5},{5,6... | collective-permute-start | bytes 36872 | tf_op jit(solution)/shard_map/ppermute | solution.py:66
  24.6 0.7 %copy-start.8 = (f32[3,4]{1,0:T(4,128)S(1)}, f32[3,4]{1,0:T(4,128)}, u32[]{:S(2)}) copy-start(f32[3,4]{1,0:T(4,128)} %refs_14_.1) | copy-start | bytes 148
  24.6 0.7 %copy-start.11 = (s32[4]{0:T(128)S(1)}, s32[4]{0:T(128)}, u32[]{:S(2)}) copy-start(s32[4]{0:T(128)} %refs_13_.1) | copy-start | bytes 52
  31.1 12.3 %all-to-all-start = ((f32[32,8,128]{2,1,0:T(8,128)}), f32[32,8,128]{2,1,0:T(8,128)S(1)}, u32[]{:S(2)}, u32[]{:S(2)}) async-start(f32[32,8,128]{2,1,0:T(8,128)} %broadcast_in_dim.2), calls=%async_computation | async-start | bytes 262144 | tf_op jit(solution)/shard_map/all_to_all | solution.py:457
  34.1 8.6 %collective-permute-start.5 = (f32[48,128]{1,0:T(8,128)S(1)}, f32[48,128]{1,0:T(8,128)S(1)}, u32[]{:S(2)}, u32[]{:S(2)}) collective-permute-start(f32[48,128]{1,0:T(8,128)S(1)} %get-tuple-element.41), channel_id=1, source_target_pairs={{0,12},{4,0},{8,4},{12,8},{1,13},{5,1},{9,5},{13,9},{2,14},{6,2},{... | collective-permute-start | bytes 73736 | tf_op jit(solution)/shard_map/ppermute | solution.py:66
  37.8 5.0 %collective-permute-start.6 = (f32[48,128]{1,0:T(8,128)S(1)}, f32[48,128]{1,0:T(8,128)S(1)}, u32[]{:S(2)}, u32[]{:S(2)}) collective-permute-start(f32[48,128]{1,0:T(8,128)S(1)} %get-tuple-element.42), channel_id=1, source_target_pairs={{0,8},{4,12},{8,0},{12,4},{1,9},{5,13},{9,1},{13,5},{2,10},{6,14},... | collective-permute-start | bytes 73736 | tf_op jit(solution)/shard_map/ppermute | solution.py:66
  37.8 5.6 %collective-permute-start.7 = (f32[48,128]{1,0:T(8,128)S(1)}, f32[48,128]{1,0:T(8,128)S(1)}, u32[]{:S(2)}, u32[]{:S(2)}) collective-permute-start(f32[48,128]{1,0:T(8,128)S(1)} %get-tuple-element.43), channel_id=1, source_target_pairs={{0,4},{4,8},{8,12},{12,0},{1,5},{5,9},{9,13},{13,1},{2,6},{6,10},{... | collective-permute-start | bytes 73736 | tf_op jit(solution)/shard_map/ppermute | solution.py:66

commit v2 on v0

--- a/solution.py
+++ b/solution.py
@@ -1,14 +1,575 @@
+import functools
+
 import jax
 import jax.numpy as jnp
 from jax import lax
+from jax.experimental import pallas as pl
+from jax.experimental.pallas import tpu as pltpu
 from jax.sharding import PartitionSpec as P
 
 TILE = 16
 STEPS = 3
-
+SUBSTEPS = 3
+LANES = 128
+FIELDS = 4
+WINDOW = 24
+HALO = FIELDS * TILE
+MESSAGE = HALO + 24
+PLANES = 9
+WIDE = 2 * LANES
+GROUP = 6
 
 COURANT = 0.5
 HCOEF = 0.5
+F32 = jnp.float32
+BF16 = jnp.bfloat16
+I32 = jnp.int32
+COLS = ("grp", "gy")
+
+
+def iota(shape, axis):
+    return lax.broadcasted_iota(I32, shape, axis)
+
+
+def f32(*shape):
+    return jax.ShapeDtypeStruct(shape, F32)
+
+
+def kept(*shape, dtype=F32):
+    return pltpu.VMEM(shape, dtype)
+
+
+def call(kernel, outs, args, scratch=(), far=(), near=(), far_outs=(), flops=1 << 20):
+    vmem, hbm = (pl.BlockSpec(memory_space=m) for m in (pltpu.VMEM, pltpu.HBM))
+    args = [
+        pltpu.with_memory_space_constraint(x, pltpu.HBM)
+        if k in far
+        else pltpu.with_memory_space_constraint(x, pltpu.VMEM)
+        if k in near
+        else x
+        for k, x in enumerate(args)
+    ]
+    return pl.pallas_call(
+        kernel,
+        out_shape=outs,
+        in_specs=[hbm if k in far else vmem for k in range(len(args))],
+        out_specs=tuple(hbm if k in far_outs else vmem for k in range(len(outs))),
+        scratch_shapes=list(scratch),
+        compiler_params=pltpu.CompilerParams(vmem_limit_bytes=16 * 1024 * 1024),
+        cost_estimate=pl.CostEstimate(flops=flops, bytes_accessed=1 << 20, transcendentals=0),
+    )(*args)
+
+
+def copies(sources, targets, sems):
+    moves = [
+        pltpu.make_async_copy(source, target, sems.at[k])
+        for k, (source, target) in enumerate(zip(sources, targets))
+    ]
+    for move in moves:
+        move.start()
+    return moves
+
+
+def ring(value, axis, steps):
+    count = lax.axis_size(axis)
+    return lax.ppermute(value, axis, [(k, (k + steps) % count) for k in range(count)])
+
+
+def pack_kernel(owners, *refs):
+    sources, outs = refs[:11], refs[11 : 11 + owners]
+    coarse_kinds, fine_kinds = refs[11 + owners : 13 + owners]
+    fine, held = refs[13 + owners : 17 + owners], refs[17 + owners : 22 + owners]
+    kinds, sems = refs[22 + owners : 24 + owners], refs[24 + owners]
+    moves = copies(sources, (*held, *kinds, *fine), sems)
+    for move in moves[:7]:
+        move.wait()
+    count = kinds[0].shape[0]
+    for ref, ratio, scale in zip((coarse_kinds, fine_kinds), (1.0, 3.0), (1.0, 0.5)):
+        for m, (damp, gain) in enumerate(lists(*kinds, ratio)):
+            ref[m : m + 1, :] = damp
+            ref[count + m : count + m + 1, :] = scale * gain
+    ez, hx, hy, ids, boxes = held
+    me = lax.axis_index("gx")
+    tiles = ez.shape[0] // 8
+    count = boxes.shape[1]
+    sub = iota((8, LANES), 0)
+    lines = jnp.concatenate([boxes[...].astype(F32), jnp.zeros((4, LANES - count), F32)], axis=1)
+    low, high, left, top = (jnp.broadcast_to(lines[k : k + 1, :], (8, LANES)) for k in range(4))
+    for d in range(owners):
+        g = lax.rem(me + d, owners)
+        here = pl.multiple_of(g * TILE, TILE)
+        after = pl.multiple_of(lax.rem(2 * g + 2, tiles) * 8, 8)
+        before = pl.multiple_of(lax.rem(2 * g + tiles - 1, tiles) * 8, 8)
+        edges = []
+        for f, ref in enumerate((ez, hx, hy, ids)):
+            outs[d][f * TILE : (f + 1) * TILE, :] = ref[pl.ds(here, TILE), :].astype(F32)
+            edge = jnp.where(sub < 4, ref[pl.ds(after, 8), :], ref[pl.ds(before, 8), :])
+            edges.append(edge.astype(F32))
+        around_ez, around_hx, around_hy, around_ids = edges
+        outs[d][HALO : HALO + 8, :] = jnp.where(sub == 3, low, jnp.where(sub == 4, high, around_ez))
+        inner = jnp.where(sub < 4, pltpu.roll(around_ids, 2, 0), pltpu.roll(around_ids, 6, 0))
+        outs[d][HALO + 8 : HALO + 16, :] = jnp.where((sub >= 2) & (sub < 6), inner, around_hx)
+        outs[d][HALO + 16 : HALO + 24, :] = jnp.where(
+            sub == 2, left, jnp.where(sub == 3, top, around_hy)
+        )
+    for move in moves[7:]:
+        move.wait()
+
+
+def block_of(owners, d):
+    return lax.rem(lax.axis_index("gx") + owners - d, owners)
+
+
+def edges_kernel(owners, *refs):
+    received, table = refs[:owners], refs[owners]
+    out, windows, boxes, store = refs[owners + 1 :]
+    me = lax.axis_index("gx")
+    sub = iota((8, LANES), 0)
+    for d in range(owners):
+        store[block_of(owners, d)] = received[d][...]
+    around = [
+        [store[a, HALO + 8 * k : HALO + 8 * k + 8, :] for a in range(owners)] for k in range(3)
+    ]
+    row = iota((WINDOW, LANES), 0)
+    row = jnp.where(row < 20, row, row - WINDOW)
+    lane = iota((WINDOW, LANES), 1)
+    total = jnp.zeros((WINDOW, LANES), F32)
+    for a in range(owners):
+        for k, at in enumerate((3, 4, 18, 19)):
+            boxes[a, k : k + 1, :] = store[a, HALO + at : HALO + at + 1, :]
+        tiles = []
+        for tile in around:
+            after = jnp.where(me == owners - 1, tile[min(a + 1, owners - 1)], tile[a])
+            before = jnp.where(me == 0, tile[max(a - 1, 0)], tile[a])
+            tiles.append(jnp.where(sub < 4, after, before))
+        inner = jnp.where(sub < 4, pltpu.roll(tiles[1], 6, 0), pltpu.roll(tiles[1], 2, 0))
+        fields = [
+            jnp.concatenate([store[a, f * TILE : (f + 1) * TILE, :], tile], axis=0)
+            for f, tile in enumerate((*tiles, inner))
+        ]
+        all_row = row + (a * owners * TILE + me * TILE)
+        valid = (all_row >= 0) & (all_row < owners * owners * TILE)
+        damp = jnp.zeros((WINDOW, LANES), F32)
+        gain = jnp.zeros((WINDOW, LANES), F32)
+        kinds = table.shape[0] // 2
+        for m in range(kinds):
+            hit = fields[3] == float(m)
+            damp = jnp.where(hit, table[m : m + 1, :], damp)
+            gain = jnp.where(hit, table[kinds + m : kinds + m + 1, :], gain)
+        for f, value in enumerate((*fields[:3], damp, gain)):
+            value = jnp.where(valid, value, 0.0)
+            windows[f, a] = value
+            at = GROUP * (f * owners + a)
+            total = jnp.where((lane >= at) & (lane < at + GROUP), pltpu.roll(value, at + 3, 1), total)
+    out[...] = total
+
+
+def lane_of():
+    return iota((8, LANES), 1)
+
+
+def third_of(x, start):
+    return lax.rem(x + start, 3)
+
+
+def choose(parts, which):
+    return jnp.where(which == 0, parts[0], jnp.where(which == 1, parts[1], parts[2]))
+
+
+def take(x, lanes):
+    return jnp.take_along_axis(x, lanes & (LANES - 1), axis=1)
+
+
+def in_block(block):
+    return ((block & 7) << 4) | (lane_of() & 15)
+
+
+def halves(x):
+    high = x.astype(BF16)
+    return high, (x - high.astype(F32)).astype(BF16)
+
+
+def thirds(x):
+    high = x.astype(BF16)
+    rest = x - high.astype(F32)
+    return high, *halves(rest)
+
+
+def lists(eps, sig, ratio):
+    ones = jnp.ones((1, LANES), F32)
+    both = []
+    for m in range(eps.shape[0]):
+        e, s = ones * eps[m], ones * sig[m]
+        loss = s / (e * ratio)
+        both.append(((1.0 - loss) / (1.0 + loss), COURANT / (e * (1.0 + loss))))
+    return both
+
+
+def each_group(count, body):
+    def group(n, carry):
+        tiles = pl.ds(pl.multiple_of(8 * n, 8), 8)
+        for h in range(2):
+            body(h, tiles, pl.ds(pl.multiple_of(h * count + 8 * n, 8), 8))
+        return carry
+
+    lax.fori_loop(0, count // 8, group, 0)
+
+
+def spread_kernel(fez, fhx, fhy, ids, kinds, oez, ohx, ohy, odamp, ogain, rows):
+    count = fez.shape[0]
+    half = kinds.shape[0] // 2
+    lane, block = lane_of(), lane_of() >> 4
+    for v in range(3):
+
+        def by_column(h, tiles, at, v=v):
+            for f, ref in enumerate((fez, fhx, fhy, ids)):
+                for r in range(3):
+                    first = 9 * h + 3 * r
+                    parts = [ref[tiles, k * LANES : (k + 1) * LANES] for k in range(first, first + 3)]
+                    part = choose(parts, third_of(lane, 2 * v)).astype(F32)
+                    rows[f, v, r, at] = take(part, 3 * lane + v)
+
+        each_group(count, by_column)
+    for u in range(3):
+
+        def by_row(h, tiles, at, u=u):
+            for f in range(4):
+                for v in range(3):
+                    part = choose([rows[f, v, r, at] for r in range(3)], third_of(block, 2 * u))
+                    value = take(part, in_block(3 * block + u))
+                    if f == 0:
+                        oez[3 * u + v, at] = value
+                    elif f < 3:
+                        (ohx, ohy)[f - 1][3 * u + v, at] = 2.0 * value
+                    else:
+                        damp = jnp.zeros((8, LANES), F32)
+                        gain = jnp.zeros((8, LANES), F32)
+                        for m in range(half):
+                            hit = value == float(m)
+                            damp = jnp.where(hit, kinds[m : m + 1, :], damp)
+                            gain = jnp.where(hit, kinds[half + m : half + m + 1, :], gain)
+                        odamp[3 * u + v, at] = damp
+                        ogain[3 * u + v, at] = gain
+
+        each_group(count, by_row)
+
+
+def gather_kernel(ez, hx, hy, *refs):
+    outs, (flat, rows, cells, sems) = refs[:3], refs[3:]
+    count = ez.shape[1] // 2
+    lane, block = lane_of(), lane_of() >> 4
+    for u in range(3):
+
+        def by_row(h, tiles, at, u=u):
+            for f, ref in enumerate((ez, hx, hy)):
+                for v in range(3):
+                    rows[f, v, u, at] = take(ref[3 * u + v, at], in_block(3 * (block - u)))
+
+        each_group(count, by_row)
+    for v in range(3):
+
+        def by_column(h, tiles, at, v=v):
+            for f in range(3):
+                parts = [rows[f, v, u, at] for u in range(3)]
+                for r in range(3):
+                    part = choose(parts, third_of(block, 2 * r))
+                    cells[f, r, v, at] = take(part, 43 * (lane - v))
+
+        each_group(count, by_column)
+    moves = []
+    for f in range(3):
+
+        def join(h, tiles, at, f=f):
+            for r in range(3):
+                parts = [cells[f, r, v, at] for v in range(3)]
+                for k in range(3):
+                    place = 9 * h + 3 * r + k
+                    value = choose(parts, third_of(lane, 2 * k))
+                    flat[f, tiles, place * LANES : (place + 1) * LANES] = value
+
+        each_group(count, join)
+        moves.append(pltpu.make_async_copy(flat.at[f], outs[f], sems.at[f]))
+        moves[-1].start()
+    for move in moves:
+        move.wait()
+
+
+def swap_blocks(x):
+    block = iota((8, LANES), 1) >> 4
+    sub = iota((8, LANES), 0)
+    x = jnp.take_along_axis(x, (block + sub) & 7, axis=0)
+    x = pltpu.roll(x, 0, 1, stride=TILE, stride_axis=0)
+    return jnp.take_along_axis(x, (block - sub) & 7, axis=0)
+
+
+def rows_of(owners, h, a):
+    return slice((h * owners + a) * 8, (h * owners + a + 1) * 8)
+
+
+def column_of():
+    return lax.axis_index("grp") * lax.axis_size("gy") + lax.axis_index("gy")
+
+
+def ready_kernel(owners, all_cols, *refs):
+    windows, boxes, fdamp, fgain, far_src, far_wave, far_rcv = refs[:7]
+    mdamp, mgain, mid, box, held, half, drive, row_hit, col_hit = refs[7:16]
+    src, wave, rcv, sems = refs[16:]
+    moves = copies((far_src, far_wave, far_rcv), (src, wave, rcv), sems)
+    me = lax.axis_index("gx")
+    column = column_of()
+    rows = owners * TILE
+    lane = iota((8, LANES), 1)
+    sub = iota((8, LANES), 0)
+    tile_col = (lane & 15).astype(F32)
+    for a in range(owners):
+        mine = lane == 8 * me + sub
+        low_i, low_j, size_i, size_j = (
+            jnp.sum(jnp.where(mine, boxes[a, k : k + 1, :], 0.0), axis=1, keepdims=True)
+            for k in range(4)
+        )
+        high_i, high_j = low_i + size_i, low_j + size_j
+        for h in range(2):
+            i = (8 * h + (lane >> 4)).astype(F32)
+            inside = (i >= low_i) & (i < high_i) & (tile_col >= low_j) & (tile_col < high_j)
+            middle = (i > low_i) & (i < high_i - 1) & (tile_col > low_j) & (tile_col < high_j - 1)
+            at = rows_of(owners, h, a)
+            mid[at] = jnp.where(middle, 1.0, 0.0)
+            box[at] = jnp.where(inside, 1.0, 0.0)
+            held[at] = swap_blocks(windows[0, a, 8 * h : 8 * h + 8, :])
+    for p in range(PLANES):
+        mdamp[p] = fdamp[p] * mid[...]
+        mgain[p] = fgain[p] * mid[...]
+    for move in moves:
+        move.wait()
+    receivers = rcv[...]
+    at_row = lax.div(receivers, all_cols)
+    image = lax.rem(iota((3 * rows, LANES), 0), rows)
+    image_row = (image >> 4) * rows + me * TILE + (image & 15)
+    row_hit[...] = jnp.where(image_row == at_row, 1.0, 0.0).astype(BF16)
+    at_col = receivers - at_row * all_cols - column * LANES
+    col_hit[...] = jnp.where(iota((LANES, LANES), 0) == at_col, 1.0, 0.0)
+    row = iota((WINDOW, WIDE), 0)
+    row = jnp.where(row < 20, row, row - WINDOW)
+    col = iota((WINDOW, WIDE), 1)
+    col = jnp.where(col < LANES + 64, col, col - WIDE)
+    all_col = col + column * LANES
+    for a in range(owners):
+        all_row = row + (a * rows + me * TILE)
+        valid = (all_row >= 0) & (all_row < owners * rows) & (all_col >= 0) & (all_col < all_cols)
+        cells = jnp.where(valid, all_row * all_cols + all_col, -1)
+        half[a] = jnp.where(valid, HCOEF, 0.0)
+        for n in range(STEPS):
+            total = jnp.zeros((WINDOW, WIDE), F32)
+            for k in range(src.shape[0]):
+                total = total + jnp.where(cells == src[k], wave[n, k], 0.0)
+            drive[n, a] = total
+
+
+def step_kernel(owners, *refs):
+    (windows, from_left, from_right, fez, fhx, fhy, mdamp, mgain, mid, box, first_held, half, drive,
+     row_hit, col_hit) = refs[:15]
+    oez, ohx, ohy = refs[15:18]
+    back = refs[18 : 18 + owners]
+    traces = refs[18 + owners]
+    ez, hx, hy, damp, gain, held, fresh, picked = refs[19 + owners :]
+    column = column_of()
+    lane = iota((WINDOW, LANES), 1)
+    no_left = column == 0
+    no_right = column == lax.axis_size(COLS) - 1
+    right = jnp.where(no_right, 0.0, from_right[...])
+    left = jnp.where(no_left, 0.0, from_left[...])
+    for f, ref in enumerate((ez, hx, hy, damp, gain)):
+        for a in range(owners):
+            at = GROUP * (f * owners + a)
+            after = pltpu.roll(right, LANES - (at + 3), 1)
+            before = pltpu.roll(left, (LANES - 3 - at) % LANES, 1)
+            side = jnp.where(lane < 3, after, jnp.where(lane >= LANES - 3, before, 0.0))
+            ref[a, :, 0:LANES] = windows[f, a]
+            ref[a, :, LANES:WIDE] = side
+    held[...] = first_held[...]
+    for p in range(PLANES):
+        oez[p], ohx[p], ohy[p] = fez[p], fhx[p], fhy[p]
+    lanes = iota((8, LANES), 1)
+    places = [(u, v, h) for u in range(3) for v in range(3) for h in range(2)]
+
+    def substep(m, carry):
+        weight = (m + 1).astype(F32) * (1.0 / SUBSTEPS)
+        for a in range(owners):
+            at = [rows_of(owners, h, a) for h in range(2)]
+            cyc = [
+                (box[s] - mid[s]) * ((1.0 - weight) * held[s] + weight * fresh[s]) for s in at
+            ]
+            e = {(u, v, h): oez[3 * u + v, at[h]] for u, v, h in places}
+            x, y = {}, {}
+            down = {(v, h): pltpu.roll(e[0, v, h], LANES - TILE, 1) for v in range(3) for h in range(2)}
+            for v in range(3):
+                down[v, 0] = jnp.where(lanes < LANES - TILE, down[v, 0], down[v, 1])
+            for u, v, h in places:
+                p = 3 * u + v
+                beside = e[u, v + 1, h] if v < 2 else pltpu.roll(e[u, 0, h], LANES - 1, 1)
+                below = e[u + 1, v, h] if u < 2 else down[v, h]
+                x[u, v, h] = ohx[p, at[h]] - (beside - e[u, v, h])
+                y[u, v, h] = ohy[p, at[h]] + (below - e[u, v, h])
+                ohx[p, at[h]], ohy[p, at[h]] = x[u, v, h], y[u, v, h]
+            up = {(v, h): pltpu.roll(y[2, v, h], TILE, 1) for v in range(3) for h in range(2)}
+            for v in range(3):
+                up[v, 1] = jnp.where(lanes < TILE, up[v, 0], up[v, 1])
+            for u, v, h in places:
+                p = 3 * u + v
+                beside = x[u, v - 1, h] if v > 0 else pltpu.roll(x[u, 2, h], 1, 1)
+                above = y[u - 1, v, h] if u > 0 else up[v, h]
+                curl = (y[u, v, h] - above) - (x[u, v, h] - beside)
+                oez[p, at[h]] = mdamp[p, at[h]] * e[u, v, h] + mgain[p, at[h]] * curl + cyc[h]
+        return carry
+
+    def pick(n):
+        image = jnp.concatenate([ez[a, 0:TILE, 0:LANES] for a in range(owners)], axis=0)
+        mixed = lax.dot_general(
+            jnp.concatenate(thirds(image), axis=0),
+            row_hit[...],
+            (((0,), (0,)), ((), ())),
+            preferred_element_type=F32,
+        )
+        picked[pl.ds(n, 1), :] = jnp.sum(mixed * col_hit[...], axis=0, keepdims=True)
+
+    def step(n, carry):
+        pick(lax.rem(n + STEPS - 1, STEPS))
+        for a in range(owners):
+            e = ez[a]
+            x = hx[a] - half[a] * (pltpu.roll(e, WIDE - 1, 1) - e)
+            y = hy[a] + half[a] * (pltpu.roll(e, WINDOW - 1, 0) - e)
+            curl = (y - pltpu.roll(y, 1, 0)) - (x - pltpu.roll(x, 1, 1))
+            hx[a], hy[a] = x, y
+            new = damp[a] * e + gain[a] * curl + drive[n, a]
+            ez[a] = new
+            for h in range(2):
+                fresh[rows_of(owners, h, a)] = swap_blocks(new[8 * h : 8 * h + 8, 0:LANES])
+        lax.fori_loop(0, SUBSTEPS, substep, 0)
+        for a in range(owners):
+            for h in range(2):
+                s = rows_of(owners, h, a)
+                total = oez[0, s]
+                for p in range(1, PLANES):
+                    total = total + oez[p, s]
+                now = jnp.where(mid[s] > 0.0, total * (1.0 / PLANES), fresh[s])
+                held[s] = now
+                ez[a, 8 * h : 8 * h + 8, 0:LANES] = swap_blocks(now)
+        return carry
+
+    lax.fori_loop(0, STEPS, step, 0)
+    pick(STEPS - 1)
+    for p in range(PLANES):
+        ohx[p] = 0.5 * (ohx[p] * box[...])
+        ohy[p] = 0.5 * (ohy[p] * box[...])
+    for d in range(owners):
+        a = block_of(owners, d)
+        for f, ref in enumerate((ez, hx, hy)):
+            back[d][f * TILE : (f + 1) * TILE, :] = ref[a, 0:TILE, 0:LANES]
+    for k in range(traces.shape[0]):
+        traces[k] = picked[0:STEPS, :]
+
+
+def place_kernel(owners, *refs):
+    pieces = refs[:owners]
+    traces = refs[owners]
+    outs = refs[owners + 1 : owners + 4]
+    out_trace = refs[owners + 4]
+    me = lax.axis_index("gx")
+    for d in range(owners):
+        here = pl.multiple_of(lax.rem(me + d, owners) * TILE, TILE)
+        for f in range(3):
+            outs[f][pl.ds(here, TILE), :] = pieces[d][f * TILE : (f + 1) * TILE, :]
+    out_trace[...] = jnp.sum(traces[...], axis=0)
+
+
+def fast_shards(
+    coarse_ez, coarse_hx, coarse_hy, coarse_ids, mat_eps, mat_sig,
+    fine_ez, fine_hx, fine_hy, fine_ids, boxes, src_cells, src_wave, rcv_cells,
+):
+    owners = lax.axis_size("gx")
+    every = ("grp", "gx", "gy")
+    rows, cols = coarse_ez.shape
+    all_cols = cols * lax.axis_size(COLS)
+    fine_shape = fine_ez.shape
+    count = fine_shape[0] * fine_shape[2]
+    cells = fine_shape[-1]
+    flat = [x.reshape(count, cells) for x in (fine_ez, fine_hx, fine_hy, fine_ids)]
+    corners = boxes.reshape(boxes.shape[2:]).T
+    block = pltpu.VMEM((rows, cols), F32)
+    kinds = mat_eps.shape[0]
+    *messages, coarse_kinds, fine_kinds, tile_ez, tile_hx, tile_hy, tile_ids = call(
+        functools.partial(pack_kernel, owners),
+        tuple(f32(MESSAGE, cols) for _ in range(owners))
+        + (kept(2 * kinds, LANES),) * 2
+        + (kept(count, cells),) * 3
+        + (kept(count, cells, dtype=I32),),
+        (coarse_ez, coarse_hx, coarse_hy, coarse_ids, corners, mat_eps, mat_sig, *flat),
+        [block] * 3
+        + [pltpu.VMEM((rows, cols), I32), pltpu.VMEM(corners.shape, I32)]
+        + [pltpu.SMEM((kinds,), F32)] * 2
+        + [pltpu.SemaphoreType.DMA((11,))],
+        far=range(11),
+    )
+    received = [messages[0]] + [ring(messages[d], "gx", d) for d in range(1, owners)]
+    planes = kept(PLANES, 2 * count, LANES)
+    *fields, fdamp, fgain = call(
+        spread_kernel,
+        (planes,) * 5,
+        (tile_ez, tile_hx, tile_hy, tile_ids, fine_kinds),
+        [pltpu.VMEM((4, 3, 3, 2 * count, LANES), F32)],
+        flops=1 << 31,
+    )
+    edges, windows, lines = call(
+        functools.partial(edges_kernel, owners),
+        (f32(WINDOW, LANES), kept(5, owners, WINDOW, LANES), kept(owners, 8, LANES)),
+        (*received, coarse_kinds),
+        [pltpu.VMEM((owners, MESSAGE, LANES), F32)],
+    )
+    from_left = ring(edges, COLS, 1)
+    from_right = ring(edges, COLS, -1)
+    receivers = rcv_cells.shape[0]
+    window = (owners, WINDOW, WIDE)
+    tiles = kept(2 * count, LANES)
+    ready = call(
+        functools.partial(ready_kernel, owners, all_cols),
+        (planes, planes, tiles, tiles, tiles, kept(*window), kept(STEPS, *window))
+        + (kept(3 * owners * TILE, receivers, dtype=BF16), kept(LANES, receivers)),
+        (windows, lines, fdamp, fgain, src_cells, src_wave, rcv_cells.reshape(1, receivers)),
+        [pltpu.SMEM(src_cells.shape, I32), pltpu.SMEM(src_wave.shape, F32)]
+        + [pltpu.VMEM((1, receivers), I32), pltpu.SemaphoreType.DMA((3,))],
+        far=(4, 5, 6),
+        flops=1 << 30,
+    )
+    *results, traces = call(
+        functools.partial(step_kernel, owners),
+        (planes,) * 3
+        + tuple(f32(3 * TILE, LANES) for _ in range(owners))
+        + (f32(lax.axis_size(every), STEPS, receivers),),
+        (windows, from_left, from_right, *fields, *ready),
+        [pltpu.VMEM(window, F32)] * 5
+        + [pltpu.VMEM(tiles.shape, F32)] * 2
+        + [pltpu.VMEM((8, receivers), F32)],
+        flops=1 << 30,
+    )
+    fine, back = results[:3], results[3:]
+    traces = lax.all_to_all(traces, every, 0, 0)
+    pieces = [back[0]] + [ring(back[d], "gx", owners - d) for d in range(1, owners)]
+    finals = call(
+        gather_kernel,
+        (f32(count, cells),) * 3,
+        fine,
+        [pltpu.VMEM((3, count, cells), F32)]
+        + [pltpu.VMEM((3, 3, 3, 2 * count, LANES), F32)] * 2
+        + [pltpu.SemaphoreType.DMA((3,))],
+        far_outs=range(3),
+        flops=1 << 31,
+    )
+    ends = call(
+        functools.partial(place_kernel, owners),
+        (f32(rows, cols),) * 3 + (f32(STEPS, receivers),),
+        (*pieces, traces),
+    )
+    return (*ends[:3], *(x.reshape(fine_shape) for x in finals), ends[3])
 
 
 def passed_along(value, axis, steps):
@@ -254,8 +815,16 @@
         P(),
         P(),
     )
+    def body(*args):
+        rows, cols = args[0].shape
+        owners = lax.axis_size("gx")
+        strips = cols == LANES and args[6].shape[2] * TILE == cols and rows == owners * TILE
+        if strips and 5 * GROUP * owners <= LANES and args[13].shape[0] == LANES:
+            return fast_shards(*args)
+        return shards(*args)
+
     return jax.shard_map(
-        shards,
+        body,
         mesh=mesh,
         in_specs=placed,
         out_specs=(

time: 223 us -> 37 us (0.17)
  blocking collectives: 49.1 us -> 0 us
  starting transfers between devices: 60.7 us -> 19.5 us
  waiting for transfers between devices: 41.9 us -> 3.46 us
  between operations: 32.9 us -> 0.71 us
  matrix products: 15.9 us -> 0 us
  local copies, waits for them, and re-layouts: 15.3 us -> 0 us
  Pallas kernels: 0 us -> 13.1 us
  other arithmetic: 5.14 us -> 0 us
    psum x1 -> x0, blocking collectives: 41.1 us -> none  [shards(): traces = lax.psum(jnp.stack(samples), ('grp', 'gx', 'gy'))]
    all_to_all x7 -> x1, waiting for transfers between devices: 30.7 us -> 0.01 us  [fast_shards(): traces = lax.all_to_all(traces, every, 0, 0)]
    all_to_all x7 -> x1, starting transfers between devices: 27 us -> 5.59 us  [fast_shards(): traces = lax.all_to_all(traces, every, 0, 0)]
    ppermute x12 -> x8, starting transfers between devices: 33.7 us -> 13.9 us  [ring(): lax.ppermute(value, axis, [(k, (k + steps) % count) for k in range(count)])]
    dot_general x18 -> x0, matrix products: 15.9 us -> none  [the longest x9 9.19 us: fine_round(): jnp.dot(mixed, spread, precision=lax.Precision.HIGHEST, preferred_element...]
    pallas_call x0 -> x7, Pallas kernels: none -> 13.1 us  [call(): pl.pallas_call(kernel, out_shape=outs, in_specs=[hbm if k in far else vme...]
    all_to_all x1 -> x0, blocking collectives: 8.01 us -> none  [shards(): back = lax.all_to_all(means, 'gx', split_axis=0, concat_axis=2, tiled=True)]
    ppermute x12 -> x8, waiting for transfers between devices: 11.2 us -> 3.46 us  [ring(): lax.ppermute(value, axis, [(k, (k + steps) % count) for k in range(count)])]
  transfers between devices with their start and end apart: 19 -> 9, of which waited for: 11 -> 5; matrix products, arithmetic and copies ran while one was open for 5% -> 0% of each run, Pallas kernels for 0% -> 18%
where the time goes in v2:
time: 37 us; the launch traced here: 36.8 us
  starting transfers between devices  19.5 us (53%)
  Pallas kernels  13.1 us (35%)
  waiting for transfers between devices  3.46 us (9%)
  between operations  0.71 us (2%)
    ppermute x8, starting transfers between devices, ring(): lax.ppermute(value, axis, [(k, (k + steps) % count) for k in range(count)])  13.9 us
    pallas_call x7, Pallas kernels, call(): pl.pallas_call(kernel, out_shape=outs, in_specs=[hbm if k in far else vme...  13.1 us
    all_to_all x1, starting transfers between devices, fast_shards(): traces = lax.all_to_all(traces, every, 0, 0)  5.59 us
    ppermute x8, waiting for transfers between devices, ring(): lax.ppermute(value, axis, [(k, (k + steps) % count) for k in range(count)])  3.46 us
  transfers between devices with their start and end apart: 9, of which 5 were waited for; matrix products, arithmetic and copies ran while one was open for 0% of the time, Pallas kernels for 18%

profile of v2, /device:TPU:0, one launch (start us, length us, event | category | flops | bytes accessed | tf_op | source)
XLA Modules:
  0.0 36.8 jit_solution(15980401498202585153)
XLA Ops:
  0.6 1.4 %shard_map.189 = (f32[88,128]{1,0:T(8,128)S(1)}, f32[88,128]{1,0:T(8,128)S(1)}, f32[88,128]{1,0:T(8,128)S(1)}, f32[88,128]{1,0:T(8,128)S(1)}, f32[16,128]{1,0:T(...) custom-call(f32[64,128]{1,0:T(8,128)} %refs_0_.1, ...), custom_call_target="tpu_custom_call" | custom-call | flops 1048576 | bytes 1048576 | tf_op jit(solution)/shard_map/pallas_call | solution.py:52
  2.1 3.1 %collective-permute-start = (f32[88,128]{1,0:T(8,128)S(1)}, f32[88,128]{1,0:T(8,128)S(1)}, u32[]{:S(2)}, u32[]{:S(2)}) collective-permute-start(f32[88,128]{1,0:T(8,128)S(1)} %get-tuple-element.50), channel_id=1, source_target_pairs={{0,4},{4,8},{8,12},{12,0},{1,5},{5,9},{9,13},{13,1},{2,6},{6,10},{... | collective-permute-start | bytes 135176 | tf_op jit(solution)/shard_map/ppermute | solution.py:75
  5.2 2.6 %collective-permute-start.1 = (f32[88,128]{1,0:T(8,128)S(1)}, f32[88,128]{1,0:T(8,128)S(1)}, u32[]{:S(2)}, u32[]{:S(2)}) collective-permute-start(f32[88,128]{1,0:T(8,128)S(1)} %get-tuple-element.51), channel_id=1, source_target_pairs={{0,8},{4,12},{8,0},{12,4},{1,9},{5,13},{9,1},{13,5},{2,10},{6,14},... | collective-permute-start | bytes 135176 | tf_op jit(solution)/shard_map/ppermute | solution.py:75
  7.8 1.3 %collective-permute-start.2 = (f32[88,128]{1,0:T(8,128)S(1)}, f32[88,128]{1,0:T(8,128)S(1)}, u32[]{:S(2)}, u32[]{:S(2)}) collective-permute-start(f32[88,128]{1,0:T(8,128)S(1)} %get-tuple-element.52), channel_id=1, source_target_pairs={{0,12},{4,0},{8,4},{12,8},{1,13},{5,1},{9,5},{13,9},{2,14},{6,2},{... | collective-permute-start | bytes 135176 | tf_op jit(solution)/shard_map/ppermute | solution.py:75
  9.1 2.5 %shard_map.191 = (f32[9,64,128]{2,1,0:T(8,128)S(1)}, f32[9,64,128]{2,1,0:T(8,128)S(1)}, f32[9,64,128]{2,1,0:T(8,128)S(1)}, f32[9,64,128]{2,1,0:T(8,128)S(1)}, f32[9,64,128]{2,1,0:T(8,128)S(1)}) custom-call(f32[32,2304]{1,0:T(8,128)S(1)} %get-tuple-element.56.fez, f32[32,2304]{1,0:T(8,128)S(1)} %get-tuple-element.57.fhx, ...), custom_call_target="tpu_custom_call" | custom-call | flops 2147483648 | bytes 1048576 | tf_op jit(solution)/shard_map/pallas_call | solution.py:52
  11.6 0.0 collective-permute-done.refs_1_
  11.6 0.0 collective-permute-done.1.refs_2_
  11.6 0.2 collective-permute-done.2.refs_3_
  11.8 0.2 shard_map.190
  12.0 0.9 %collective-permute-start.4 = (f32[24,128]{1,0:T(8,128)S(1)}, f32[24,128]{1,0:T(8,128)S(1)}, u32[]{:S(2)}, u32[]{:S(2)}) collective-permute-start(f32[24,128]{1,0:T(8,128)S(1)} %get-tuple-element.55), channel_id=1, source_target_pairs={{0,19},{1,0},{2,1},{3,2},{16,3},{17,16},{18,17},{19,18},{4,23},{5,... | collective-permute-start | bytes 36872 | tf_op jit(solution)/shard_map/ppermute | solution.py:75
  12.9 1.1 %collective-permute-start.3 = (f32[24,128]{1,0:T(8,128)S(1)}, f32[24,128]{1,0:T(8,128)S(1)}, u32[]{:S(2)}, u32[]{:S(2)}) collective-permute-start(f32[24,128]{1,0:T(8,128)S(1)} %get-tuple-element.55), channel_id=1, source_target_pairs={{0,1},{1,2},{2,3},{3,16},{16,17},{17,18},{18,19},{19,0},{4,5},{5,6... | collective-permute-start | bytes 36872 | tf_op jit(solution)/shard_map/ppermute | solution.py:75
  14.1 0.9 %shard_map.192 = (f32[9,64,128]{2,1,0:T(8,128)S(1)}, f32[9,64,128]{2,1,0:T(8,128)S(1)}, f32[64,128]{1,0:T(8,128)S(1)}, f32[64,128]{1,0:T(8,128)S(1)}, f32[64,128...) custom-call(f32[5,4,24,128]{3,2,1,0:T(8,128)S(1)} %get-tuple-element, ...), custom_call_target="tpu_custom_call" | custom-call | flops 1073741824 | bytes 1048576 | tf_op jit(solution)/shard_map/pallas_call | solution.py:52
  15.0 0.9 %collective-permute-done.4.refs_2_ = f32[24,128]{1,0:T(8,128)S(1)} collective-permute-done((f32[24,128]{1,0:T(8,128)S(1)}, f32[24,128]{1,0:T(8,128)S(1)}, u32[]{:S(2)}, u32[]{:S(2)}) %collective-permute-start.4) | collective-permute-done | bytes 12320 | tf_op jit(solution)/shard_map/ppermute | solution.py:75
  15.8 1.1 %collective-permute-done.3.refs_1_ = f32[24,128]{1,0:T(8,128)S(1)} collective-permute-done((f32[24,128]{1,0:T(8,128)S(1)}, f32[24,128]{1,0:T(8,128)S(1)}, u32[]{:S(2)}, u32[]{:S(2)}) %collective-permute-start.3) | collective-permute-done | bytes 12320 | tf_op jit(solution)/shard_map/ppermute | solution.py:75
  16.9 4.2 %shard_map.193 = (f32[9,64,128]{2,1,0:T(8,128)S(1)}, f32[9,64,128]{2,1,0:T(8,128)S(1)}, f32[9,64,128]{2,1,0:T(8,128)S(1)}, f32[48,128]{1,0:T(8,128)S(1)}, f32[48...) custom-call(f32[5,4,24,128]{3,2,1,0:T(8,128)S(1)} %get-tuple-element.54.refs_0_, ...), custom_call_target="tpu_custom_call" | custom-call | flops 1073741824 | bytes 1048576 | tf_op jit(solution)/shard_map/pallas_call | solution.py:52
  21.2 5.6 %all-to-all-start = ((f32[32,3,128]{2,1,0:T(4,128)}), f32[32,3,128]{2,1,0:T(4,128)S(1)}, u32[]{:S(2)}, u32[]{:S(2)}) async-start(f32[32,3,128]{2,1,0:T(4,128)} %get-tuple-element.80), calls=%async_computation | async-start | bytes 131072 | tf_op jit(solution)/shard_map/all_to_all | solution.py:555
  26.8 3.7 %collective-permute-start.5 = (f32[48,128]{1,0:T(8,128)S(1)}, f32[48,128]{1,0:T(8,128)S(1)}, u32[]{:S(2)}, u32[]{:S(2)}) collective-permute-start(f32[48,128]{1,0:T(8,128)S(1)} %get-tuple-element.77), channel_id=1, source_target_pairs={{0,12},{4,0},{8,4},{12,8},{1,13},{5,1},{9,5},{13,9},{2,14},{6,2},{... | collective-permute-start | bytes 73736 | tf_op jit(solution)/shard_map/ppermute | solution.py:75
  30.5 0.0 collective-permute-start.6
  30.5 1.1 %collective-permute-start.7 = (f32[48,128]{1,0:T(8,128)S(1)}, f32[48,128]{1,0:T(8,128)S(1)}, u32[]{:S(2)}, u32[]{:S(2)}) collective-permute-start(f32[48,128]{1,0:T(8,128)S(1)} %get-tuple-element.79), channel_id=1, source_target_pairs={{0,4},{4,8},{8,12},{12,0},{1,5},{5,9},{9,13},{13,1},{2,6},{6,10},{... | collective-permute-start | bytes 73736 | tf_op jit(solution)/shard_map/ppermute | solution.py:75
  31.5 3.2 %shard_map.195 = (f32[32,2304]{1,0:T(8,128)}, f32[32,2304]{1,0:T(8,128)}, f32[32,2304]{1,0:T(8,128)}) custom-call(f32[9,64,128]{2,1,0:T(8,128)S(1)} %get-tuple-element.84.ez, f32[9,64,128]{2,1,0:T(8,128)S(1)} %get-tuple-element.85.hx, f32[9,64,128]{2,1,0:T(8,128)S(1)} %get-tuple-element.86.hy), custom_call_target="tpu_custom_call" | custom-call | flops 2147483648 | bytes 1048576 | tf_op jit(solution)/shard_map/pallas_call | solution.py:52
  34.8 0.0 collective-permute-done.5.refs_1_
  34.8 0.4 %collective-permute-done.6.refs_2_ = f32[48,128]{1,0:T(8,128)S(1)} collective-permute-done((f32[48,128]{1,0:T(8,128)S(1)}, f32[48,128]{1,0:T(8,128)S(1)}, u32[]{:S(2)}, u32[]{:S(2)}) %collective-permute-start.6) | collective-permute-done | bytes 24608 | tf_op jit(solution)/shard_map/ppermute | solution.py:75
  35.2 0.9 %collective-permute-done.7.refs_3_ = f32[48,128]{1,0:T(8,128)S(1)} collective-permute-done((f32[48,128]{1,0:T(8,128)S(1)}, f32[48,128]{1,0:T(8,128)S(1)}, u32[]{:S(2)}, u32[]{:S(2)}) %collective-permute-start.7) | collective-permute-done | bytes 24608 | tf_op jit(solution)/shard_map/ppermute | solution.py:75
  36.1 0.0 all-to-all-done.refs_4_
  36.1 0.7 %shard_map.194 = (f32[64,128]{1,0:T(8,128)}, f32[64,128]{1,0:T(8,128)}, f32[64,128]{1,0:T(8,128)}, f32[3,128]{1,0:T(4,128)}) custom-call(f32[48,128]{1,0:T(8,128)S(1)} %get-tuple-element.76.refs_0_, f32[48,128]{1,0:T(8,128)S(1)} %collective-permute-done.5.refs_1_, f32[48,128]{1,0:T(8,128)S(1)} %collective-permute-done.6.refs_2_, ...), custom_call_target="tpu_custom_call" | custom-call | flops 1048576 | bytes 1048576 | tf_op jit(solution)/shard_map/pallas_call | solution.py:52
Async XLA Ops:
  2.1 9.5 %collective-permute-start = (f32[88,128]{1,0:T(8,128)S(1)}, f32[88,128]{1,0:T(8,128)S(1)}, u32[]{:S(2)}, u32[]{:S(2)}) collective-permute-start(f32[88,128]{1,0:T(8,128)S(1)} %get-tuple-element.50), channel_id=1, source_target_pairs={{0,4},{4,8},{8,12},{12,0},{1,5},{5,9},{9,13},{13,1},{2,6},{6,10},{... | collective-permute-start | bytes 135176 | tf_op jit(solution)/shard_map/ppermute | solution.py:75
  5.2 6.5 %collective-permute-start.1 = (f32[88,128]{1,0:T(8,128)S(1)}, f32[88,128]{1,0:T(8,128)S(1)}, u32[]{:S(2)}, u32[]{:S(2)}) collective-permute-start(f32[88,128]{1,0:T(8,128)S(1)} %get-tuple-element.51), channel_id=1, source_target_pairs={{0,8},{4,12},{8,0},{12,4},{1,9},{5,13},{9,1},{13,5},{2,10},{6,14},... | collective-permute-start | bytes 135176 | tf_op jit(solution)/shard_map/ppermute | solution.py:75
  7.8 4.0 %collective-permute-start.2 = (f32[88,128]{1,0:T(8,128)S(1)}, f32[88,128]{1,0:T(8,128)S(1)}, u32[]{:S(2)}, u32[]{:S(2)}) collective-permute-start(f32[88,128]{1,0:T(8,128)S(1)} %get-tuple-element.52), channel_id=1, source_target_pairs={{0,12},{4,0},{8,4},{12,8},{1,13},{5,1},{9,5},{13,9},{2,14},{6,2},{... | collective-permute-start | bytes 135176 | tf_op jit(solution)/shard_map/ppermute | solution.py:75
  12.0 3.9 %collective-permute-start.4 = (f32[24,128]{1,0:T(8,128)S(1)}, f32[24,128]{1,0:T(8,128)S(1)}, u32[]{:S(2)}, u32[]{:S(2)}) collective-permute-start(f32[24,128]{1,0:T(8,128)S(1)} %get-tuple-element.55), channel_id=1, source_target_pairs={{0,19},{1,0},{2,1},{3,2},{16,3},{17,16},{18,17},{19,18},{4,23},{5,... | collective-permute-start | bytes 36872 | tf_op jit(solution)/shard_map/ppermute | solution.py:75
  12.9 4.0 %collective-permute-start.3 = (f32[24,128]{1,0:T(8,128)S(1)}, f32[24,128]{1,0:T(8,128)S(1)}, u32[]{:S(2)}, u32[]{:S(2)}) collective-permute-start(f32[24,128]{1,0:T(8,128)S(1)} %get-tuple-element.55), channel_id=1, source_target_pairs={{0,1},{1,2},{2,3},{3,16},{16,17},{17,18},{18,19},{19,0},{4,5},{5,6... | collective-permute-start | bytes 36872 | tf_op jit(solution)/shard_map/ppermute | solution.py:75
  21.2 14.9 %all-to-all-start = ((f32[32,3,128]{2,1,0:T(4,128)}), f32[32,3,128]{2,1,0:T(4,128)S(1)}, u32[]{:S(2)}, u32[]{:S(2)}) async-start(f32[32,3,128]{2,1,0:T(4,128)} %get-tuple-element.80), calls=%async_computation | async-start | bytes 131072 | tf_op jit(solution)/shard_map/all_to_all | solution.py:555
  26.8 8.0 %collective-permute-start.5 = (f32[48,128]{1,0:T(8,128)S(1)}, f32[48,128]{1,0:T(8,128)S(1)}, u32[]{:S(2)}, u32[]{:S(2)}) collective-permute-start(f32[48,128]{1,0:T(8,128)S(1)} %get-tuple-element.77), channel_id=1, source_target_pairs={{0,12},{4,0},{8,4},{12,8},{1,13},{5,1},{9,5},{13,9},{2,14},{6,2},{... | collective-permute-start | bytes 73736 | tf_op jit(solution)/shard_map/ppermute | solution.py:75
  30.5 4.8 %collective-permute-start.6 = (f32[48,128]{1,0:T(8,128)S(1)}, f32[48,128]{1,0:T(8,128)S(1)}, u32[]{:S(2)}, u32[]{:S(2)}) collective-permute-start(f32[48,128]{1,0:T(8,128)S(1)} %get-tuple-element.78), channel_id=1, source_target_pairs={{0,8},{4,12},{8,0},{12,4},{1,9},{5,13},{9,1},{13,5},{2,10},{6,14},... | collective-permute-start | bytes 73736 | tf_op jit(solution)/shard_map/ppermute | solution.py:75
  30.5 5.6 %collective-permute-start.7 = (f32[48,128]{1,0:T(8,128)S(1)}, f32[48,128]{1,0:T(8,128)S(1)}, u32[]{:S(2)}, u32[]{:S(2)}) collective-permute-start(f32[48,128]{1,0:T(8,128)S(1)} %get-tuple-element.79), channel_id=1, source_target_pairs={{0,4},{4,8},{8,12},{12,0},{1,5},{5,9},{9,13},{13,1},{2,6},{6,10},{... | collective-permute-start | bytes 73736 | tf_op jit(solution)/shard_map/ppermute | solution.py:75

commit v3 on v2

--- a/solution.py
+++ b/solution.py
@@ -76,18 +76,10 @@
 
 
 def pack_kernel(owners, *refs):
-    sources, outs = refs[:11], refs[11 : 11 + owners]
-    coarse_kinds, fine_kinds = refs[11 + owners : 13 + owners]
-    fine, held = refs[13 + owners : 17 + owners], refs[17 + owners : 22 + owners]
-    kinds, sems = refs[22 + owners : 24 + owners], refs[24 + owners]
-    moves = copies(sources, (*held, *kinds, *fine), sems)
-    for move in moves[:7]:
+    sources, outs = refs[:5], refs[5 : 5 + owners]
+    held, sems = refs[5 + owners : 10 + owners], refs[10 + owners]
+    for move in copies(sources, held, sems):
         move.wait()
-    count = kinds[0].shape[0]
-    for ref, ratio, scale in zip((coarse_kinds, fine_kinds), (1.0, 3.0), (1.0, 0.5)):
-        for m, (damp, gain) in enumerate(lists(*kinds, ratio)):
-            ref[m : m + 1, :] = damp
-            ref[count + m : count + m + 1, :] = scale * gain
     ez, hx, hy, ids, boxes = held
     me = lax.axis_index("gx")
     tiles = ez.shape[0] // 8
@@ -112,8 +104,6 @@
         outs[d][HALO + 16 : HALO + 24, :] = jnp.where(
             sub == 2, left, jnp.where(sub == 3, top, around_hy)
         )
-    for move in moves[7:]:
-        move.wait()
 
 
 def block_of(owners, d):
@@ -205,38 +195,50 @@
     return both
 
 
-def each_group(count, body):
-    def group(n, carry):
-        tiles = pl.ds(pl.multiple_of(8 * n, 8), 8)
+def turn(x, first, last):
+    block = lane_of() >> 4
+    sub = iota((8, LANES), 0)
+    x = jnp.take_along_axis(x, first(sub, block) & 7, axis=0)
+    x = pltpu.roll(x, 0, 1, stride=TILE, stride_axis=0)
+    return jnp.take_along_axis(x, last(sub, block) & 7, axis=0)
+
+
+def each_half(owners):
+    for a in range(owners):
         for h in range(2):
-            body(h, tiles, pl.ds(pl.multiple_of(h * count + 8 * n, 8), 8))
-        return carry
-
-    lax.fori_loop(0, count // 8, group, 0)
-
-
-def spread_kernel(fez, fhx, fhy, ids, kinds, oez, ohx, ohy, odamp, ogain, rows):
-    count = fez.shape[0]
-    half = kinds.shape[0] // 2
+            yield a, h, slice(8 * a, 8 * a + 8), slice(TILE * a + 8 * h, TILE * a + 8 * h + 8)
+
+
+def spread_kernel(*refs):
+    sources, (oez, ohx, ohy, odamp, ogain, coarse_kinds) = refs[:6], refs[6:12]
+    held, (kinds, rows, sems) = refs[12:18], refs[18:]
+    fez, fhx, fhy, ids, eps, sig = held
+    moves = copies(sources, held, sems)
+    half = eps.shape[0]
+    for move in moves[4:]:
+        move.wait()
+    for ref, ratio, scale in ((coarse_kinds, 1.0, 1.0), (kinds, 3.0, 0.5)):
+        for m, (damp, gain) in enumerate(lists(eps, sig, ratio)):
+            ref[m : m + 1, :] = damp
+            ref[half + m : half + m + 1, :] = scale * gain
+    for move in moves[:4]:
+        move.wait()
+    owners = fez.shape[0] // 8
     lane, block = lane_of(), lane_of() >> 4
     for v in range(3):
-
-        def by_column(h, tiles, at, v=v):
+        for a, h, tiles, at in each_half(owners):
             for f, ref in enumerate((fez, fhx, fhy, ids)):
                 for r in range(3):
                     first = 9 * h + 3 * r
                     parts = [ref[tiles, k * LANES : (k + 1) * LANES] for k in range(first, first + 3)]
                     part = choose(parts, third_of(lane, 2 * v)).astype(F32)
                     rows[f, v, r, at] = take(part, 3 * lane + v)
-
-        each_group(count, by_column)
     for u in range(3):
-
-        def by_row(h, tiles, at, u=u):
-            for f in range(4):
+        for a, h, tiles, at in each_half(owners):
+            for f in (3, 0, 1, 2):
                 for v in range(3):
                     part = choose([rows[f, v, r, at] for r in range(3)], third_of(block, 2 * u))
-                    value = take(part, in_block(3 * block + u))
+                    value = turn(part, lambda r, b: r + b, lambda i, c: c - 3 * i - u)
                     if f == 0:
                         oez[3 * u + v, at] = value
                     elif f < 3:
@@ -251,91 +253,67 @@
                         odamp[3 * u + v, at] = damp
                         ogain[3 * u + v, at] = gain
 
-        each_group(count, by_row)
-
 
 def gather_kernel(ez, hx, hy, *refs):
     outs, (flat, rows, cells, sems) = refs[:3], refs[3:]
-    count = ez.shape[1] // 2
+    owners = ez.shape[1] // TILE
     lane, block = lane_of(), lane_of() >> 4
     for u in range(3):
-
-        def by_row(h, tiles, at, u=u):
+        for a, h, tiles, at in each_half(owners):
             for f, ref in enumerate((ez, hx, hy)):
                 for v in range(3):
-                    rows[f, v, u, at] = take(ref[3 * u + v, at], in_block(3 * (block - u)))
-
-        each_group(count, by_row)
+                    rows[f, v, u, at] = turn(
+                        ref[3 * u + v, at], lambda r, b: 3 * (b + r - u), lambda c, b: b - c
+                    )
     for v in range(3):
-
-        def by_column(h, tiles, at, v=v):
+        for a, h, tiles, at in each_half(owners):
             for f in range(3):
                 parts = [rows[f, v, u, at] for u in range(3)]
                 for r in range(3):
                     part = choose(parts, third_of(block, 2 * r))
                     cells[f, r, v, at] = take(part, 43 * (lane - v))
-
-        each_group(count, by_column)
     moves = []
     for f in range(3):
-
-        def join(h, tiles, at, f=f):
+        for a, h, tiles, at in each_half(owners):
             for r in range(3):
                 parts = [cells[f, r, v, at] for v in range(3)]
                 for k in range(3):
                     place = 9 * h + 3 * r + k
                     value = choose(parts, third_of(lane, 2 * k))
                     flat[f, tiles, place * LANES : (place + 1) * LANES] = value
-
-        each_group(count, join)
         moves.append(pltpu.make_async_copy(flat.at[f], outs[f], sems.at[f]))
         moves[-1].start()
     for move in moves:
         move.wait()
 
 
-def swap_blocks(x):
-    block = iota((8, LANES), 1) >> 4
-    sub = iota((8, LANES), 0)
-    x = jnp.take_along_axis(x, (block + sub) & 7, axis=0)
-    x = pltpu.roll(x, 0, 1, stride=TILE, stride_axis=0)
-    return jnp.take_along_axis(x, (block - sub) & 7, axis=0)
-
-
-def rows_of(owners, h, a):
-    return slice((h * owners + a) * 8, (h * owners + a + 1) * 8)
-
-
 def column_of():
     return lax.axis_index("grp") * lax.axis_size("gy") + lax.axis_index("gy")
 
 
 def ready_kernel(owners, all_cols, *refs):
     windows, boxes, fdamp, fgain, far_src, far_wave, far_rcv = refs[:7]
-    mdamp, mgain, mid, box, held, half, drive, row_hit, col_hit = refs[7:16]
-    src, wave, rcv, sems = refs[16:]
+    mdamp, mgain, mid, box, half, drive, row_hit, col_hit = refs[7:15]
+    src, wave, rcv, sems = refs[15:]
     moves = copies((far_src, far_wave, far_rcv), (src, wave, rcv), sems)
     me = lax.axis_index("gx")
     column = column_of()
     rows = owners * TILE
-    lane = iota((8, LANES), 1)
-    sub = iota((8, LANES), 0)
+    lane = lane_of()
     tile_col = (lane & 15).astype(F32)
     for a in range(owners):
-        mine = lane == 8 * me + sub
         low_i, low_j, size_i, size_j = (
-            jnp.sum(jnp.where(mine, boxes[a, k : k + 1, :], 0.0), axis=1, keepdims=True)
+            take(jnp.broadcast_to(boxes[a, k : k + 1, :], (8, LANES)), 8 * me + (lane >> 4))
             for k in range(4)
         )
         high_i, high_j = low_i + size_i, low_j + size_j
         for h in range(2):
-            i = (8 * h + (lane >> 4)).astype(F32)
+            i = (8 * h + iota((8, LANES), 0)).astype(F32)
             inside = (i >= low_i) & (i < high_i) & (tile_col >= low_j) & (tile_col < high_j)
             middle = (i > low_i) & (i < high_i - 1) & (tile_col > low_j) & (tile_col < high_j - 1)
-            at = rows_of(owners, h, a)
+            at = slice(TILE * a + 8 * h, TILE * a + 8 * h + 8)
             mid[at] = jnp.where(middle, 1.0, 0.0)
             box[at] = jnp.where(inside, 1.0, 0.0)
-            held[at] = swap_blocks(windows[0, a, 8 * h : 8 * h + 8, :])
     for p in range(PLANES):
         mdamp[p] = fdamp[p] * mid[...]
         mgain[p] = fgain[p] * mid[...]
@@ -358,6 +336,7 @@
         valid = (all_row >= 0) & (all_row < owners * rows) & (all_col >= 0) & (all_col < all_cols)
         cells = jnp.where(valid, all_row * all_cols + all_col, -1)
         half[a] = jnp.where(valid, HCOEF, 0.0)
+        half[owners + a] = jnp.where(valid & (all_col > 0), HCOEF, 0.0)
         for n in range(STEPS):
             total = jnp.zeros((WINDOW, WIDE), F32)
             for k in range(src.shape[0]):
@@ -366,60 +345,71 @@
 
 
 def step_kernel(owners, *refs):
-    (windows, from_left, from_right, fez, fhx, fhy, mdamp, mgain, mid, box, first_held, half, drive,
-     row_hit, col_hit) = refs[:15]
-    oez, ohx, ohy = refs[15:18]
-    back = refs[18 : 18 + owners]
-    traces = refs[18 + owners]
-    ez, hx, hy, damp, gain, held, fresh, picked = refs[19 + owners :]
+    (windows, from_left, from_right, fez, fhx, fhy, mdamp, mgain, mid, box, half, drive,
+     row_hit, col_hit) = refs[:14]
+    oez, ohx, ohy = refs[14:17]
+    back = refs[17 : 17 + owners]
+    traces = refs[17 + owners]
+    ez, hx, hy, behind, damp, gain, held, beside, picked = refs[18 + owners :]
     column = column_of()
-    lane = iota((WINDOW, LANES), 1)
-    no_left = column == 0
-    no_right = column == lax.axis_size(COLS) - 1
-    right = jnp.where(no_right, 0.0, from_right[...])
-    left = jnp.where(no_left, 0.0, from_left[...])
+    place = lax.rem(iota((WINDOW, LANES), 1), GROUP)
+    right = jnp.where(column == lax.axis_size(COLS) - 1, 0.0, from_right[...])
+    left = jnp.where(column == 0, 0.0, from_left[...])
+    sides = jnp.where(place < 3, left, right)
     for f, ref in enumerate((ez, hx, hy, damp, gain)):
         for a in range(owners):
             at = GROUP * (f * owners + a)
-            after = pltpu.roll(right, LANES - (at + 3), 1)
-            before = pltpu.roll(left, (LANES - 3 - at) % LANES, 1)
-            side = jnp.where(lane < 3, after, jnp.where(lane >= LANES - 3, before, 0.0))
             ref[a, :, 0:LANES] = windows[f, a]
-            ref[a, :, LANES:WIDE] = side
-    held[...] = first_held[...]
+            ref[a, :, LANES:WIDE] = pltpu.roll(sides, (LANES - 3 - at) % LANES, 1)
     for p in range(PLANES):
         oez[p], ohx[p], ohy[p] = fez[p], fhx[p], fhy[p]
-    lanes = iota((8, LANES), 1)
+    for a in range(owners):
+        behind[a] = pltpu.roll(hx[a], 1, 1)
+    for u in range(3):
+        for k in range(2 * owners):
+            at = slice(8 * k, 8 * k + 8)
+            beside[u, at] = pltpu.roll(fhx[3 * u + 2, at], 1, 1)
+    sub = iota((8, LANES), 0)
     places = [(u, v, h) for u in range(3) for v in range(3) for h in range(2)]
 
     def substep(m, carry):
         weight = (m + 1).astype(F32) * (1.0 / SUBSTEPS)
         for a in range(owners):
-            at = [rows_of(owners, h, a) for h in range(2)]
-            cyc = [
-                (box[s] - mid[s]) * ((1.0 - weight) * held[s] + weight * fresh[s]) for s in at
-            ]
+            at = [slice(TILE * a + 8 * h, TILE * a + 8 * h + 8) for h in range(2)]
             e = {(u, v, h): oez[3 * u + v, at[h]] for u, v, h in places}
-            x, y = {}, {}
-            down = {(v, h): pltpu.roll(e[0, v, h], LANES - TILE, 1) for v in range(3) for h in range(2)}
-            for v in range(3):
-                down[v, 0] = jnp.where(lanes < LANES - TILE, down[v, 0], down[v, 1])
+            ahead = {(u, h): pltpu.roll(e[u, 0, h], LANES - 1, 1) for u in range(3) for h in range(2)}
+            back_e = {(u, h): pltpu.roll(e[u, 2, h], 1, 1) for u in range(3) for h in range(2)}
+            down = {(v, h): pltpu.roll(e[0, v, h], 7, 0) for v in range(3) for h in range(2)}
+            y = {}
             for u, v, h in places:
                 p = 3 * u + v
-                beside = e[u, v + 1, h] if v < 2 else pltpu.roll(e[u, 0, h], LANES - 1, 1)
-                below = e[u + 1, v, h] if u < 2 else down[v, h]
-                x[u, v, h] = ohx[p, at[h]] - (beside - e[u, v, h])
+                if u < 2:
+                    below = e[u + 1, v, h]
+                elif h == 0:
+                    below = jnp.where(sub < 7, down[v, 0], down[v, 1])
+                else:
+                    below = down[v, 1]
                 y[u, v, h] = ohy[p, at[h]] + (below - e[u, v, h])
-                ohx[p, at[h]], ohy[p, at[h]] = x[u, v, h], y[u, v, h]
-            up = {(v, h): pltpu.roll(y[2, v, h], TILE, 1) for v in range(3) for h in range(2)}
+                ohy[p, at[h]] = y[u, v, h]
+            up = {(v, h): pltpu.roll(y[2, v, h], 1, 0) for v in range(3) for h in range(2)}
             for v in range(3):
-                up[v, 1] = jnp.where(lanes < TILE, up[v, 0], up[v, 1])
-            for u, v, h in places:
-                p = 3 * u + v
-                beside = x[u, v - 1, h] if v > 0 else pltpu.roll(x[u, 2, h], 1, 1)
-                above = y[u - 1, v, h] if u > 0 else up[v, h]
-                curl = (y[u, v, h] - above) - (x[u, v, h] - beside)
-                oez[p, at[h]] = mdamp[p, at[h]] * e[u, v, h] + mgain[p, at[h]] * curl + cyc[h]
+                up[v, 1] = jnp.where(sub < 1, up[v, 0], up[v, 1])
+            for h in range(2):
+                now = ez[a, 8 * h : 8 * h + 8, 0:LANES]
+                cyc = (box[at[h]] - mid[at[h]]) * ((1.0 - weight) * held[at[h]] + weight * now)
+                for u in range(3):
+                    before = beside[u, at[h]] - (e[u, 0, h] - back_e[u, h])
+                    beside[u, at[h]] = before
+                    for v in range(3):
+                        p = 3 * u + v
+                        after = e[u, v + 1, h] if v < 2 else ahead[u, h]
+                        x = ohx[p, at[h]] - (after - e[u, v, h])
+                        ohx[p, at[h]] = x
+                        above = y[u - 1, v, h] if u > 0 else up[v, h]
+                        curl = (y[u, v, h] - above) - (x - before)
+                        inner = mdamp[p, at[h]] * e[u, v, h] + mgain[p, at[h]] * curl
+                        oez[p, at[h]] = inner + cyc
+                        before = x
         return carry
 
     def pick(n):
@@ -436,26 +426,26 @@
         pick(lax.rem(n + STEPS - 1, STEPS))
         for a in range(owners):
             e = ez[a]
-            x = hx[a] - half[a] * (pltpu.roll(e, WIDE - 1, 1) - e)
-            y = hy[a] + half[a] * (pltpu.roll(e, WINDOW - 1, 0) - e)
-            curl = (y - pltpu.roll(y, 1, 0)) - (x - pltpu.roll(x, 1, 1))
-            hx[a], hy[a] = x, y
-            new = damp[a] * e + gain[a] * curl + drive[n, a]
-            ez[a] = new
-            for h in range(2):
-                fresh[rows_of(owners, h, a)] = swap_blocks(new[8 * h : 8 * h + 8, 0:LANES])
+            held[TILE * a : TILE * a + TILE] = e[0:TILE, 0:LANES]
+            scale = half[a]
+            x = hx[a] - scale * (pltpu.roll(e, WIDE - 1, 1) - e)
+            before = behind[a] - half[owners + a] * (e - pltpu.roll(e, 1, 1))
+            y = hy[a] + scale * (pltpu.roll(e, WINDOW - 1, 0) - e)
+            hx[a], hy[a], behind[a] = x, y, before
+            curl = (y - pltpu.roll(y, 1, 0)) - (x - before)
+            ez[a] = damp[a] * e + gain[a] * curl + drive[n, a]
         lax.fori_loop(0, SUBSTEPS, substep, 0)
         for a in range(owners):
             for h in range(2):
-                s = rows_of(owners, h, a)
-                total = oez[0, s]
+                at = slice(TILE * a + 8 * h, TILE * a + 8 * h + 8)
+                total = oez[0, at]
                 for p in range(1, PLANES):
-                    total = total + oez[p, s]
-                now = jnp.where(mid[s] > 0.0, total * (1.0 / PLANES), fresh[s])
-                held[s] = now
-                ez[a, 8 * h : 8 * h + 8, 0:LANES] = swap_blocks(now)
+                    total = total + oez[p, at]
+                here = (a, slice(8 * h, 8 * h + 8), slice(0, LANES))
+                ez[here] = jnp.where(mid[at] > 0.0, total * (1.0 / PLANES), ez[here])
         return carry
 
+    picked[...] = jnp.zeros(picked.shape, F32)
     lax.fori_loop(0, STEPS, step, 0)
     pick(STEPS - 1)
     for p in range(PLANES):
@@ -496,27 +486,28 @@
     flat = [x.reshape(count, cells) for x in (fine_ez, fine_hx, fine_hy, fine_ids)]
     corners = boxes.reshape(boxes.shape[2:]).T
     block = pltpu.VMEM((rows, cols), F32)
-    kinds = mat_eps.shape[0]
-    *messages, coarse_kinds, fine_kinds, tile_ez, tile_hx, tile_hy, tile_ids = call(
+    messages = call(
         functools.partial(pack_kernel, owners),
-        tuple(f32(MESSAGE, cols) for _ in range(owners))
-        + (kept(2 * kinds, LANES),) * 2
-        + (kept(count, cells),) * 3
-        + (kept(count, cells, dtype=I32),),
-        (coarse_ez, coarse_hx, coarse_hy, coarse_ids, corners, mat_eps, mat_sig, *flat),
+        tuple(f32(MESSAGE, cols) for _ in range(owners)),
+        (coarse_ez, coarse_hx, coarse_hy, coarse_ids, corners),
         [block] * 3
         + [pltpu.VMEM((rows, cols), I32), pltpu.VMEM(corners.shape, I32)]
-        + [pltpu.SMEM((kinds,), F32)] * 2
-        + [pltpu.SemaphoreType.DMA((11,))],
-        far=range(11),
+        + [pltpu.SemaphoreType.DMA((5,))],
+        far=range(5),
     )
     received = [messages[0]] + [ring(messages[d], "gx", d) for d in range(1, owners)]
     planes = kept(PLANES, 2 * count, LANES)
-    *fields, fdamp, fgain = call(
+    kinds = mat_eps.shape[0]
+    *fields, fdamp, fgain, coarse_kinds = call(
         spread_kernel,
-        (planes,) * 5,
-        (tile_ez, tile_hx, tile_hy, tile_ids, fine_kinds),
-        [pltpu.VMEM((4, 3, 3, 2 * count, LANES), F32)],
+        (planes,) * 5 + (kept(2 * kinds, LANES),),
+        (*flat, mat_eps, mat_sig),
+        [pltpu.VMEM((count, cells), F32)] * 3
+        + [pltpu.VMEM((count, cells), I32)]
+        + [pltpu.SMEM((kinds,), F32)] * 2
+        + [pltpu.VMEM((2 * kinds, LANES), F32), pltpu.VMEM((4, 3, 3, 2 * count, LANES), F32)]
+        + [pltpu.SemaphoreType.DMA((6,))],
+        far=range(6),
         flops=1 << 31,
     )
     edges, windows, lines = call(
@@ -532,7 +523,7 @@
     tiles = kept(2 * count, LANES)
     ready = call(
         functools.partial(ready_kernel, owners, all_cols),
-        (planes, planes, tiles, tiles, tiles, kept(*window), kept(STEPS, *window))
+        (planes, planes, tiles, tiles, kept(2 * owners, *window[1:]), kept(STEPS, *window))
         + (kept(3 * owners * TILE, receivers, dtype=BF16), kept(LANES, receivers)),
         (windows, lines, fdamp, fgain, src_cells, src_wave, rcv_cells.reshape(1, receivers)),
         [pltpu.SMEM(src_cells.shape, I32), pltpu.SMEM(src_wave.shape, F32)]
@@ -544,10 +535,10 @@
         functools.partial(step_kernel, owners),
         (planes,) * 3
         + tuple(f32(3 * TILE, LANES) for _ in range(owners))
-        + (f32(lax.axis_size(every), STEPS, receivers),),
+        + (kept(lax.axis_size(every), STEPS, receivers),),
         (windows, from_left, from_right, *fields, *ready),
-        [pltpu.VMEM(window, F32)] * 5
-        + [pltpu.VMEM(tiles.shape, F32)] * 2
+        [pltpu.VMEM(window, F32)] * 6
+        + [pltpu.VMEM(tiles.shape, F32), pltpu.VMEM((3, *tiles.shape), F32)]
         + [pltpu.VMEM((8, receivers), F32)],
         flops=1 << 30,
     )

time: 37 us -> 35.8 us (0.968)
  Pallas kernels: 13.1 us -> 9.63 us
  waiting for transfers between devices: 3.46 us -> 5.64 us
    pallas_call x7, Pallas kernels: 13.1 us -> 9.63 us  [call(): pl.pallas_call(kernel, out_shape=outs, in_specs=[hbm if k in far else vme...]
    ppermute x8, waiting for transfers between devices: 3.46 us -> 5.64 us  [ring(): lax.ppermute(value, axis, [(k, (k + steps) % count) for k in range(count)])]
  transfers between devices with their start and end apart: 9 -> 9, of which waited for: 5 -> 5; matrix products, arithmetic and copies ran while one was open for 0% -> 0% of each run, Pallas kernels for 18% -> 12%
where the time goes in v3:
time: 35.8 us; the launch traced here: 35.5 us
  starting transfers between devices  19.6 us (55%)
  Pallas kernels  9.63 us (27%)
  waiting for transfers between devices  5.64 us (16%)
  between operations  0.71 us (2%)
    ppermute x8, starting transfers between devices, ring(): lax.ppermute(value, axis, [(k, (k + steps) % count) for k in range(count)])  13.9 us
    pallas_call x7, Pallas kernels, call(): pl.pallas_call(kernel, out_shape=outs, in_specs=[hbm if k in far else vme...  9.63 us
    all_to_all x1, starting transfers between devices, fast_shards(): traces = lax.all_to_all(traces, every, 0, 0)  5.68 us
    ppermute x8, waiting for transfers between devices, ring(): lax.ppermute(value, axis, [(k, (k + steps) % count) for k in range(count)])  5.64 us
  transfers between devices with their start and end apart: 9, of which 5 were waited for; matrix products, arithmetic and copies ran while one was open for 0% of the time, Pallas kernels for 12%

profile of v3, /device:TPU:0, one launch (start us, length us, event | category | flops | bytes accessed | tf_op | source)
XLA Modules:
  0.0 35.5 jit_solution(5310731840774567289)
XLA Ops:
  0.6 0.9 %shard_map.189 = (f32[88,128]{1,0:T(8,128)S(1)}, f32[88,128]{1,0:T(8,128)S(1)}, f32[88,128]{1,0:T(8,128)S(1)}, f32[88,128]{1,0:T(8,128)S(1)}) custom-call(f32[64,128]{1,0:T(8,128)} %refs_0_.1, f32[64,128]{1,0:T(8,128)} %refs_1_.1, f32[64,128]{1,0:T(8,128)} %refs_2_.1, s32[64,128]{1,0:T(8,128)} %refs_3_.1, s32[4,32]{1,0:T(4,128)} %bitcast.17), custom_call_target="tpu_custom_call" | custom-call | flops 1048576 | bytes 1048576 | tf_op jit(solution)/shard_map/pallas_call | solution.py:52
  1.5 3.1 %collective-permute-start = (f32[88,128]{1,0:T(8,128)S(1)}, f32[88,128]{1,0:T(8,128)S(1)}, u32[]{:S(2)}, u32[]{:S(2)}) collective-permute-start(f32[88,128]{1,0:T(8,128)S(1)} %get-tuple-element.44), channel_id=1, source_target_pairs={{0,4},{4,8},{8,12},{12,0},{1,5},{5,9},{9,13},{13,1},{2,6},{6,10},{... | collective-permute-start | bytes 135176 | tf_op jit(solution)/shard_map/ppermute | solution.py:75
  4.6 2.6 %collective-permute-start.1 = (f32[88,128]{1,0:T(8,128)S(1)}, f32[88,128]{1,0:T(8,128)S(1)}, u32[]{:S(2)}, u32[]{:S(2)}) collective-permute-start(f32[88,128]{1,0:T(8,128)S(1)} %get-tuple-element.45), channel_id=1, source_target_pairs={{0,8},{4,12},{8,0},{12,4},{1,9},{5,13},{9,1},{13,5},{2,10},{6,14},... | collective-permute-start | bytes 135176 | tf_op jit(solution)/shard_map/ppermute | solution.py:75
  7.2 1.3 %collective-permute-start.2 = (f32[88,128]{1,0:T(8,128)S(1)}, f32[88,128]{1,0:T(8,128)S(1)}, u32[]{:S(2)}, u32[]{:S(2)}) collective-permute-start(f32[88,128]{1,0:T(8,128)S(1)} %get-tuple-element.46), channel_id=1, source_target_pairs={{0,12},{4,0},{8,4},{12,8},{1,13},{5,1},{9,5},{13,9},{2,14},{6,2},{... | collective-permute-start | bytes 135176 | tf_op jit(solution)/shard_map/ppermute | solution.py:75
  8.6 2.0 %shard_map.190 = (f32[9,64,128]{2,1,0:T(8,128)S(1)}, f32[9,64,128]{2,1,0:T(8,128)S(1)}, f32[9,64,128]{2,1,0:T(8,128)S(1)}, f32[9,64,128]{2,1,0:T(8,128)S(1)}, f3...) custom-call(f32[32,2304]{1,0:T(8,128)} %bitcast.18, f32[32,2304]{1,0:T(8,128)} %bitcast.19, f32[32,2304]{1,0:T(8,128)} %bitcast.20, ...), custom_call_target="tpu_custom_call" | custom-call | flops 2147483648 | bytes 1048576 | tf_op jit(solution)/shard_map/pallas_call | solution.py:52
  10.6 0.0 collective-permute-done.refs_1_
  10.6 0.0 collective-permute-done.1.refs_2_
  10.6 0.7 %collective-permute-done.2.refs_3_ = f32[88,128]{1,0:T(8,128)S(1)} collective-permute-done((f32[88,128]{1,0:T(8,128)S(1)}, f32[88,128]{1,0:T(8,128)S(1)}, u32[]{:S(2)}, u32[]{:S(2)}) %collective-permute-start.2) | collective-permute-done | bytes 45088 | tf_op jit(solution)/shard_map/ppermute | solution.py:75
  11.3 0.2 shard_map.191
  11.4 0.7 %collective-permute-start.4 = (f32[24,128]{1,0:T(8,128)S(1)}, f32[24,128]{1,0:T(8,128)S(1)}, u32[]{:S(2)}, u32[]{:S(2)}) collective-permute-start(f32[24,128]{1,0:T(8,128)S(1)} %get-tuple-element.49), channel_id=1, source_target_pairs={{0,19},{1,0},{2,1},{3,2},{16,3},{17,16},{18,17},{19,18},{4,23},{5,... | collective-permute-start | bytes 36872 | tf_op jit(solution)/shard_map/ppermute | solution.py:75
  12.2 1.4 %collective-permute-start.3 = (f32[24,128]{1,0:T(8,128)S(1)}, f32[24,128]{1,0:T(8,128)S(1)}, u32[]{:S(2)}, u32[]{:S(2)}) collective-permute-start(f32[24,128]{1,0:T(8,128)S(1)} %get-tuple-element.49), channel_id=1, source_target_pairs={{0,1},{1,2},{2,3},{3,16},{16,17},{17,18},{18,19},{19,0},{4,5},{5,6... | collective-permute-start | bytes 36872 | tf_op jit(solution)/shard_map/ppermute | solution.py:75
  13.5 0.9 %shard_map.192 = (f32[9,64,128]{2,1,0:T(8,128)S(1)}, f32[9,64,128]{2,1,0:T(8,128)S(1)}, f32[64,128]{1,0:T(8,128)S(1)}, f32[64,128]{1,0:T(8,128)S(1)}, f32[8,24,2...) custom-call(f32[5,4,24,128]{3,2,1,0:T(8,128)S(1)} %get-tuple-element.48., ...), custom_call_target="tpu_custom_call" | custom-call | flops 1073741824 | bytes 1048576 | tf_op jit(solution)/shard_map/pallas_call | solution.py:52
  14.4 0.8 %collective-permute-done.4.refs_2_ = f32[24,128]{1,0:T(8,128)S(1)} collective-permute-done((f32[24,128]{1,0:T(8,128)S(1)}, f32[24,128]{1,0:T(8,128)S(1)}, u32[]{:S(2)}, u32[]{:S(2)}) %collective-permute-start.4) | collective-permute-done | bytes 12320 | tf_op jit(solution)/shard_map/ppermute | solution.py:75
  15.2 1.1 %collective-permute-done.3.refs_1_ = f32[24,128]{1,0:T(8,128)S(1)} collective-permute-done((f32[24,128]{1,0:T(8,128)S(1)}, f32[24,128]{1,0:T(8,128)S(1)}, u32[]{:S(2)}, u32[]{:S(2)}) %collective-permute-start.3) | collective-permute-done | bytes 12320 | tf_op jit(solution)/shard_map/ppermute | solution.py:75
  16.3 3.6 %shard_map.193 = (f32[9,64,128]{2,1,0:T(8,128)S(1)}, f32[9,64,128]{2,1,0:T(8,128)S(1)}, f32[9,64,128]{2,1,0:T(8,128)S(1)}, f32[48,128]{1,0:T(8,128)S(1)}, f32[48...) custom-call(f32[5,4,24,128]{3,2,1,0:T(8,128)S(1)} %get-tuple-element.48.refs_0_, ...), custom_call_target="tpu_custom_call" | custom-call | flops 1073741824 | bytes 1048576 | tf_op jit(solution)/shard_map/pallas_call | solution.py:52
  19.9 5.7 %all-to-all-start = ((f32[32,3,128]{2,1,0:T(4,128)}), f32[32,3,128]{2,1,0:T(4,128)S(1)}, u32[]{:S(2)}, u32[]{:S(2)}) async-start(f32[32,3,128]{2,1,0:T(4,128)} %get-tuple-element.68), calls=%async_computation | async-start | bytes 131072 | tf_op jit(solution)/shard_map/all_to_all | solution.py:546
  25.6 3.7 %collective-permute-start.5 = (f32[48,128]{1,0:T(8,128)S(1)}, f32[48,128]{1,0:T(8,128)S(1)}, u32[]{:S(2)}, u32[]{:S(2)}) collective-permute-start(f32[48,128]{1,0:T(8,128)S(1)} %get-tuple-element.65), channel_id=1, source_target_pairs={{0,12},{4,0},{8,4},{12,8},{1,13},{5,1},{9,5},{13,9},{2,14},{6,2},{... | collective-permute-start | bytes 73736 | tf_op jit(solution)/shard_map/ppermute | solution.py:75
  29.3 0.0 collective-permute-start.6
  29.3 1.1 %collective-permute-start.7 = (f32[48,128]{1,0:T(8,128)S(1)}, f32[48,128]{1,0:T(8,128)S(1)}, u32[]{:S(2)}, u32[]{:S(2)}) collective-permute-start(f32[48,128]{1,0:T(8,128)S(1)} %get-tuple-element.67), channel_id=1, source_target_pairs={{0,4},{4,8},{8,12},{12,0},{1,5},{5,9},{9,13},{13,1},{2,6},{6,10},{... | collective-permute-start | bytes 73736 | tf_op jit(solution)/shard_map/ppermute | solution.py:75
  30.3 1.5 %shard_map.195 = (f32[32,2304]{1,0:T(8,128)}, f32[32,2304]{1,0:T(8,128)}, f32[32,2304]{1,0:T(8,128)}) custom-call(f32[9,64,128]{2,1,0:T(8,128)S(1)} %get-tuple-element.72.ez, f32[9,64,128]{2,1,0:T(8,128)S(1)} %get-tuple-element.73.hx, f32[9,64,128]{2,1,0:T(8,128)S(1)} %get-tuple-element.74.hy), custom_call_target="tpu_custom_call" | custom-call | flops 2147483648 | bytes 1048576 | tf_op jit(solution)/shard_map/pallas_call | solution.py:52
  31.8 0.0 collective-permute-done.5.refs_1_
  31.8 2.2 %collective-permute-done.6.refs_2_ = f32[48,128]{1,0:T(8,128)S(1)} collective-permute-done((f32[48,128]{1,0:T(8,128)S(1)}, f32[48,128]{1,0:T(8,128)S(1)}, u32[]{:S(2)}, u32[]{:S(2)}) %collective-permute-start.6) | collective-permute-done | bytes 24608 | tf_op jit(solution)/shard_map/ppermute | solution.py:75
  34.0 0.9 %collective-permute-done.7.refs_3_ = f32[48,128]{1,0:T(8,128)S(1)} collective-permute-done((f32[48,128]{1,0:T(8,128)S(1)}, f32[48,128]{1,0:T(8,128)S(1)}, u32[]{:S(2)}, u32[]{:S(2)}) %collective-permute-start.7) | collective-permute-done | bytes 24608 | tf_op jit(solution)/shard_map/ppermute | solution.py:75
  34.9 0.0 all-to-all-done.refs_4_
  34.9 0.7 %shard_map.194 = (f32[64,128]{1,0:T(8,128)}, f32[64,128]{1,0:T(8,128)}, f32[64,128]{1,0:T(8,128)}, f32[3,128]{1,0:T(4,128)}) custom-call(f32[48,128]{1,0:T(8,128)S(1)} %get-tuple-element.64.refs_0_, f32[48,128]{1,0:T(8,128)S(1)} %collective-permute-done.5.refs_1_, f32[48,128]{1,0:T(8,128)S(1)} %collective-permute-done.6.refs_2_, ...), custom_call_target="tpu_custom_call" | custom-call | flops 1048576 | bytes 1048576 | tf_op jit(solution)/shard_map/pallas_call | solution.py:52
Async XLA Ops:
  1.5 9.0 %collective-permute-start = (f32[88,128]{1,0:T(8,128)S(1)}, f32[88,128]{1,0:T(8,128)S(1)}, u32[]{:S(2)}, u32[]{:S(2)}) collective-permute-start(f32[88,128]{1,0:T(8,128)S(1)} %get-tuple-element.44), channel_id=1, source_target_pairs={{0,4},{4,8},{8,12},{12,0},{1,5},{5,9},{9,13},{13,1},{2,6},{6,10},{... | collective-permute-start | bytes 135176 | tf_op jit(solution)/shard_map/ppermute | solution.py:75
  4.6 6.0 %collective-permute-start.1 = (f32[88,128]{1,0:T(8,128)S(1)}, f32[88,128]{1,0:T(8,128)S(1)}, u32[]{:S(2)}, u32[]{:S(2)}) collective-permute-start(f32[88,128]{1,0:T(8,128)S(1)} %get-tuple-element.45), channel_id=1, source_target_pairs={{0,8},{4,12},{8,0},{12,4},{1,9},{5,13},{9,1},{13,5},{2,10},{6,14},... | collective-permute-start | bytes 135176 | tf_op jit(solution)/shard_map/ppermute | solution.py:75
  7.2 4.0 %collective-permute-start.2 = (f32[88,128]{1,0:T(8,128)S(1)}, f32[88,128]{1,0:T(8,128)S(1)}, u32[]{:S(2)}, u32[]{:S(2)}) collective-permute-start(f32[88,128]{1,0:T(8,128)S(1)} %get-tuple-element.46), channel_id=1, source_target_pairs={{0,12},{4,0},{8,4},{12,8},{1,13},{5,1},{9,5},{13,9},{2,14},{6,2},{... | collective-permute-start | bytes 135176 | tf_op jit(solution)/shard_map/ppermute | solution.py:75
  11.4 3.8 %collective-permute-start.4 = (f32[24,128]{1,0:T(8,128)S(1)}, f32[24,128]{1,0:T(8,128)S(1)}, u32[]{:S(2)}, u32[]{:S(2)}) collective-permute-start(f32[24,128]{1,0:T(8,128)S(1)} %get-tuple-element.49), channel_id=1, source_target_pairs={{0,19},{1,0},{2,1},{3,2},{16,3},{17,16},{18,17},{19,18},{4,23},{5,... | collective-permute-start | bytes 36872 | tf_op jit(solution)/shard_map/ppermute | solution.py:75
  12.2 4.1 %collective-permute-start.3 = (f32[24,128]{1,0:T(8,128)S(1)}, f32[24,128]{1,0:T(8,128)S(1)}, u32[]{:S(2)}, u32[]{:S(2)}) collective-permute-start(f32[24,128]{1,0:T(8,128)S(1)} %get-tuple-element.49), channel_id=1, source_target_pairs={{0,1},{1,2},{2,3},{3,16},{16,17},{17,18},{18,19},{19,0},{4,5},{5,6... | collective-permute-start | bytes 36872 | tf_op jit(solution)/shard_map/ppermute | solution.py:75
  19.9 15.0 %all-to-all-start = ((f32[32,3,128]{2,1,0:T(4,128)}), f32[32,3,128]{2,1,0:T(4,128)S(1)}, u32[]{:S(2)}, u32[]{:S(2)}) async-start(f32[32,3,128]{2,1,0:T(4,128)} %get-tuple-element.68), calls=%async_computation | async-start | bytes 131072 | tf_op jit(solution)/shard_map/all_to_all | solution.py:546
  25.6 6.2 %collective-permute-start.5 = (f32[48,128]{1,0:T(8,128)S(1)}, f32[48,128]{1,0:T(8,128)S(1)}, u32[]{:S(2)}, u32[]{:S(2)}) collective-permute-start(f32[48,128]{1,0:T(8,128)S(1)} %get-tuple-element.65), channel_id=1, source_target_pairs={{0,12},{4,0},{8,4},{12,8},{1,13},{5,1},{9,5},{13,9},{2,14},{6,2},{... | collective-permute-start | bytes 73736 | tf_op jit(solution)/shard_map/ppermute | solution.py:75
  29.3 4.8 %collective-permute-start.6 = (f32[48,128]{1,0:T(8,128)S(1)}, f32[48,128]{1,0:T(8,128)S(1)}, u32[]{:S(2)}, u32[]{:S(2)}) collective-permute-start(f32[48,128]{1,0:T(8,128)S(1)} %get-tuple-element.66), channel_id=1, source_target_pairs={{0,8},{4,12},{8,0},{12,4},{1,9},{5,13},{9,1},{13,5},{2,10},{6,14},... | collective-permute-start | bytes 73736 | tf_op jit(solution)/shard_map/ppermute | solution.py:75
  29.3 5.6 %collective-permute-start.7 = (f32[48,128]{1,0:T(8,128)S(1)}, f32[48,128]{1,0:T(8,128)S(1)}, u32[]{:S(2)}, u32[]{:S(2)}) collective-permute-start(f32[48,128]{1,0:T(8,128)S(1)} %get-tuple-element.67), channel_id=1, source_target_pairs={{0,4},{4,8},{8,12},{12,0},{1,5},{5,9},{9,13},{13,1},{2,6},{6,10},{... | collective-permute-start | bytes 73736 | tf_op jit(solution)/shard_map/ppermute | solution.py:75

commit v4 on v3

--- a/solution.py
+++ b/solution.py
@@ -39,13 +39,11 @@
     return pltpu.VMEM(shape, dtype)
 
 
-def call(kernel, outs, args, scratch=(), far=(), near=(), far_outs=(), flops=1 << 20):
+def call(kernel, outs, args, scratch=(), far=(), far_outs=(), aliases=None, flops=1 << 20):
     vmem, hbm = (pl.BlockSpec(memory_space=m) for m in (pltpu.VMEM, pltpu.HBM))
     args = [
         pltpu.with_memory_space_constraint(x, pltpu.HBM)
         if k in far
-        else pltpu.with_memory_space_constraint(x, pltpu.VMEM)
-        if k in near
         else x
         for k, x in enumerate(args)
     ]
@@ -55,6 +53,7 @@
         in_specs=[hbm if k in far else vmem for k in range(len(args))],
         out_specs=tuple(hbm if k in far_outs else vmem for k in range(len(outs))),
         scratch_shapes=list(scratch),
+        input_output_aliases=aliases or {},
         compiler_params=pltpu.CompilerParams(vmem_limit_bytes=16 * 1024 * 1024),
         cost_estimate=pl.CostEstimate(flops=flops, bytes_accessed=1 << 20, transcendentals=0),
     )(*args)
@@ -254,7 +253,7 @@
                         ogain[3 * u + v, at] = gain
 
 
-def gather_kernel(ez, hx, hy, *refs):
+def gather_kernel(ez, hx, hy, box, *refs):
     outs, (flat, rows, cells, sems) = refs[:3], refs[3:]
     owners = ez.shape[1] // TILE
     lane, block = lane_of(), lane_of() >> 4
@@ -262,8 +261,10 @@
         for a, h, tiles, at in each_half(owners):
             for f, ref in enumerate((ez, hx, hy)):
                 for v in range(3):
+                    part = ref[3 * u + v, at]
+                    part = part if f == 0 else 0.5 * (part * box[at])
                     rows[f, v, u, at] = turn(
-                        ref[3 * u + v, at], lambda r, b: 3 * (b + r - u), lambda c, b: b - c
+                        part, lambda r, b: 3 * (b + r - u), lambda c, b: b - c
                     )
     for v in range(3):
         for a, h, tiles, at in each_half(owners):
@@ -345,12 +346,12 @@
 
 
 def step_kernel(owners, *refs):
-    (windows, from_left, from_right, fez, fhx, fhy, mdamp, mgain, mid, box, half, drive,
-     row_hit, col_hit) = refs[:14]
+    windows, from_left, from_right = refs[:3]
+    mdamp, mgain, mid, box, half, drive, row_hit, col_hit = refs[6:14]
     oez, ohx, ohy = refs[14:17]
     back = refs[17 : 17 + owners]
-    traces = refs[17 + owners]
-    ez, hx, hy, behind, damp, gain, held, beside, picked = refs[18 + owners :]
+    far_traces = refs[17 + owners]
+    ez, hx, hy, behind, damp, gain, held, beside, picked, traces, sem = refs[18 + owners :]
     column = column_of()
     place = lax.rem(iota((WINDOW, LANES), 1), GROUP)
     right = jnp.where(column == lax.axis_size(COLS) - 1, 0.0, from_right[...])
@@ -361,19 +362,17 @@
             at = GROUP * (f * owners + a)
             ref[a, :, 0:LANES] = windows[f, a]
             ref[a, :, LANES:WIDE] = pltpu.roll(sides, (LANES - 3 - at) % LANES, 1)
-    for p in range(PLANES):
-        oez[p], ohx[p], ohy[p] = fez[p], fhx[p], fhy[p]
     for a in range(owners):
         behind[a] = pltpu.roll(hx[a], 1, 1)
     for u in range(3):
         for k in range(2 * owners):
             at = slice(8 * k, 8 * k + 8)
-            beside[u, at] = pltpu.roll(fhx[3 * u + 2, at], 1, 1)
+            beside[u, at] = pltpu.roll(ohx[3 * u + 2, at], 1, 1)
     sub = iota((8, LANES), 0)
     places = [(u, v, h) for u in range(3) for v in range(3) for h in range(2)]
 
     def substep(m, carry):
-        weight = (m + 1).astype(F32) * (1.0 / SUBSTEPS)
+        weight = (m + 1) / SUBSTEPS
         for a in range(owners):
             at = [slice(TILE * a + 8 * h, TILE * a + 8 * h + 8) for h in range(2)]
             e = {(u, v, h): oez[3 * u + v, at[h]] for u, v, h in places}
@@ -420,10 +419,11 @@
             (((0,), (0,)), ((), ())),
             preferred_element_type=F32,
         )
-        picked[pl.ds(n, 1), :] = jnp.sum(mixed * col_hit[...], axis=0, keepdims=True)
+        picked[n : n + 1, :] = jnp.sum(mixed * col_hit[...], axis=0, keepdims=True)
 
     def step(n, carry):
-        pick(lax.rem(n + STEPS - 1, STEPS))
+        if n > 0:
+            pick(n - 1)
         for a in range(owners):
             e = ez[a]
             held[TILE * a : TILE * a + TILE] = e[0:TILE, 0:LANES]
@@ -434,7 +434,8 @@
             hx[a], hy[a], behind[a] = x, y, before
             curl = (y - pltpu.roll(y, 1, 0)) - (x - before)
             ez[a] = damp[a] * e + gain[a] * curl + drive[n, a]
-        lax.fori_loop(0, SUBSTEPS, substep, 0)
+        for m in range(SUBSTEPS):
+            substep(m, 0)
         for a in range(owners):
             for h in range(2):
                 at = slice(TILE * a + 8 * h, TILE * a + 8 * h + 8)
@@ -446,17 +447,18 @@
         return carry
 
     picked[...] = jnp.zeros(picked.shape, F32)
-    lax.fori_loop(0, STEPS, step, 0)
+    for n in range(STEPS):
+        step(n, 0)
     pick(STEPS - 1)
-    for p in range(PLANES):
-        ohx[p] = 0.5 * (ohx[p] * box[...])
-        ohy[p] = 0.5 * (ohy[p] * box[...])
+    for k in range(traces.shape[0]):
+        traces[k] = picked[0:STEPS, :]
+    move = pltpu.make_async_copy(traces, far_traces, sem)
+    move.start()
     for d in range(owners):
         a = block_of(owners, d)
         for f, ref in enumerate((ez, hx, hy)):
             back[d][f * TILE : (f + 1) * TILE, :] = ref[a, 0:TILE, 0:LANES]
-    for k in range(traces.shape[0]):
-        traces[k] = picked[0:STEPS, :]
+    move.wait()
 
 
 def place_kernel(owners, *refs):
@@ -535,11 +537,14 @@
         functools.partial(step_kernel, owners),
         (planes,) * 3
         + tuple(f32(3 * TILE, LANES) for _ in range(owners))
-        + (kept(lax.axis_size(every), STEPS, receivers),),
+        + (f32(lax.axis_size(every), STEPS, receivers),),
         (windows, from_left, from_right, *fields, *ready),
         [pltpu.VMEM(window, F32)] * 6
         + [pltpu.VMEM(tiles.shape, F32), pltpu.VMEM((3, *tiles.shape), F32)]
-        + [pltpu.VMEM((8, receivers), F32)],
+        + [pltpu.VMEM((8, receivers), F32)]
+        + [pltpu.VMEM((lax.axis_size(every), STEPS, receivers), F32), pltpu.SemaphoreType.DMA],
+        far_outs=(3 + owners,),
+        aliases={3: 0, 4: 1, 5: 2},
         flops=1 << 30,
     )
     fine, back = results[:3], results[3:]
@@ -548,7 +553,7 @@
     finals = call(
         gather_kernel,
         (f32(count, cells),) * 3,
-        fine,
+        (*fine, ready[3]),
         [pltpu.VMEM((3, count, cells), F32)]
         + [pltpu.VMEM((3, 3, 3, 2 * count, LANES), F32)] * 2
         + [pltpu.SemaphoreType.DMA((3,))],

time: 35.8 us -> 35.2 us (0.983)
  Pallas kernels: 9.63 us -> 9.03 us
    pallas_call x7, Pallas kernels: 9.63 us -> 9.03 us  [call(): pl.pallas_call(kernel, out_shape=outs, in_specs=[hbm if k in far else vme...]
where the time goes in v4:
time: 35.2 us; the launch traced here: 35 us
  starting transfers between devices  19.6 us (56%)
  Pallas kernels  9.03 us (26%)
  waiting for transfers between devices  5.64 us (16%)
  between operations  0.72 us (2%)
    ppermute x8, starting transfers between devices, ring(): lax.ppermute(value, axis, [(k, (k + steps) % count) for k in range(count)])  13.9 us
    pallas_call x7, Pallas kernels, call(): pl.pallas_call(kernel, out_shape=outs, in_specs=[hbm if k in far else vme...  9.03 us
    all_to_all x1, starting transfers between devices, fast_shards(): traces = lax.all_to_all(traces, every, 0, 0)  5.7 us
    ppermute x8, waiting for transfers between devices, ring(): lax.ppermute(value, axis, [(k, (k + steps) % count) for k in range(count)])  5.64 us
  transfers between devices with their start and end apart: 9, of which 5 were waited for; matrix products, arithmetic and copies ran while one was open for 0% of the time, Pallas kernels for 12%

profile of v4, /device:TPU:0, one launch (start us, length us, event | category | flops | bytes accessed | tf_op | source)
XLA Modules:
  0.0 35.0 jit_solution(3771311451410560094)
XLA Ops:
  0.6 0.9 %shard_map.189 = (f32[88,128]{1,0:T(8,128)S(1)}, f32[88,128]{1,0:T(8,128)S(1)}, f32[88,128]{1,0:T(8,128)S(1)}, f32[88,128]{1,0:T(8,128)S(1)}) custom-call(f32[64,128]{1,0:T(8,128)} %refs_0_.1, f32[64,128]{1,0:T(8,128)} %refs_1_.1, f32[64,128]{1,0:T(8,128)} %refs_2_.1, s32[64,128]{1,0:T(8,128)} %refs_3_.1, s32[4,32]{1,0:T(4,128)} %bitcast.17), custom_call_target="tpu_custom_call" | custom-call | flops 1048576 | bytes 1048576 | tf_op jit(solution)/shard_map/pallas_call | solution.py:50
  1.5 3.1 %collective-permute-start = (f32[88,128]{1,0:T(8,128)S(1)}, f32[88,128]{1,0:T(8,128)S(1)}, u32[]{:S(2)}, u32[]{:S(2)}) collective-permute-start(f32[88,128]{1,0:T(8,128)S(1)} %get-tuple-element.44), channel_id=1, source_target_pairs={{0,4},{4,8},{8,12},{12,0},{1,5},{5,9},{9,13},{13,1},{2,6},{6,10},{... | collective-permute-start | bytes 135176 | tf_op jit(solution)/shard_map/ppermute | solution.py:74
  4.6 2.6 %collective-permute-start.1 = (f32[88,128]{1,0:T(8,128)S(1)}, f32[88,128]{1,0:T(8,128)S(1)}, u32[]{:S(2)}, u32[]{:S(2)}) collective-permute-start(f32[88,128]{1,0:T(8,128)S(1)} %get-tuple-element.45), channel_id=1, source_target_pairs={{0,8},{4,12},{8,0},{12,4},{1,9},{5,13},{9,1},{13,5},{2,10},{6,14},... | collective-permute-start | bytes 135176 | tf_op jit(solution)/shard_map/ppermute | solution.py:74
  7.2 1.3 %collective-permute-start.2 = (f32[88,128]{1,0:T(8,128)S(1)}, f32[88,128]{1,0:T(8,128)S(1)}, u32[]{:S(2)}, u32[]{:S(2)}) collective-permute-start(f32[88,128]{1,0:T(8,128)S(1)} %get-tuple-element.46), channel_id=1, source_target_pairs={{0,12},{4,0},{8,4},{12,8},{1,13},{5,1},{9,5},{13,9},{2,14},{6,2},{... | collective-permute-start | bytes 135176 | tf_op jit(solution)/shard_map/ppermute | solution.py:74
  8.6 2.0 %shard_map.190 = (f32[9,64,128]{2,1,0:T(8,128)S(1)}, f32[9,64,128]{2,1,0:T(8,128)S(1)}, f32[9,64,128]{2,1,0:T(8,128)S(1)}, f32[9,64,128]{2,1,0:T(8,128)S(1)}, f3...) custom-call(f32[32,2304]{1,0:T(8,128)} %bitcast.18, f32[32,2304]{1,0:T(8,128)} %bitcast.19, f32[32,2304]{1,0:T(8,128)} %bitcast.20, ...), custom_call_target="tpu_custom_call" | custom-call | flops 2147483648 | bytes 1048576 | tf_op jit(solution)/shard_map/pallas_call | solution.py:50
  10.6 0.0 collective-permute-done.refs_1_
  10.6 0.0 collective-permute-done.1.refs_2_
  10.6 0.7 %collective-permute-done.2.refs_3_ = f32[88,128]{1,0:T(8,128)S(1)} collective-permute-done((f32[88,128]{1,0:T(8,128)S(1)}, f32[88,128]{1,0:T(8,128)S(1)}, u32[]{:S(2)}, u32[]{:S(2)}) %collective-permute-start.2) | collective-permute-done | bytes 45088 | tf_op jit(solution)/shard_map/ppermute | solution.py:74
  11.3 0.2 shard_map.191
  11.4 0.7 %collective-permute-start.4 = (f32[24,128]{1,0:T(8,128)S(1)}, f32[24,128]{1,0:T(8,128)S(1)}, u32[]{:S(2)}, u32[]{:S(2)}) collective-permute-start(f32[24,128]{1,0:T(8,128)S(1)} %get-tuple-element.49), channel_id=1, source_target_pairs={{0,19},{1,0},{2,1},{3,2},{16,3},{17,16},{18,17},{19,18},{4,23},{5,... | collective-permute-start | bytes 36872 | tf_op jit(solution)/shard_map/ppermute | solution.py:74
  12.2 1.4 %collective-permute-start.3 = (f32[24,128]{1,0:T(8,128)S(1)}, f32[24,128]{1,0:T(8,128)S(1)}, u32[]{:S(2)}, u32[]{:S(2)}) collective-permute-start(f32[24,128]{1,0:T(8,128)S(1)} %get-tuple-element.49), channel_id=1, source_target_pairs={{0,1},{1,2},{2,3},{3,16},{16,17},{17,18},{18,19},{19,0},{4,5},{5,6... | collective-permute-start | bytes 36872 | tf_op jit(solution)/shard_map/ppermute | solution.py:74
  13.5 0.9 %shard_map.192 = (f32[9,64,128]{2,1,0:T(8,128)S(1)}, f32[9,64,128]{2,1,0:T(8,128)S(1)}, f32[64,128]{1,0:T(8,128)S(1)}, f32[64,128]{1,0:T(8,128)S(1)}, f32[8,24,2...) custom-call(f32[5,4,24,128]{3,2,1,0:T(8,128)S(1)} %get-tuple-element.48., ...), custom_call_target="tpu_custom_call" | custom-call | flops 1073741824 | bytes 1048576 | tf_op jit(solution)/shard_map/pallas_call | solution.py:50
  14.4 0.8 %collective-permute-done.4.refs_2_ = f32[24,128]{1,0:T(8,128)S(1)} collective-permute-done((f32[24,128]{1,0:T(8,128)S(1)}, f32[24,128]{1,0:T(8,128)S(1)}, u32[]{:S(2)}, u32[]{:S(2)}) %collective-permute-start.4) | collective-permute-done | bytes 12320 | tf_op jit(solution)/shard_map/ppermute | solution.py:74
  15.2 1.1 %collective-permute-done.3.refs_1_ = f32[24,128]{1,0:T(8,128)S(1)} collective-permute-done((f32[24,128]{1,0:T(8,128)S(1)}, f32[24,128]{1,0:T(8,128)S(1)}, u32[]{:S(2)}, u32[]{:S(2)}) %collective-permute-start.3) | collective-permute-done | bytes 12320 | tf_op jit(solution)/shard_map/ppermute | solution.py:74
  16.3 3.0 %shard_map.193 = (f32[9,64,128]{2,1,0:T(8,128)S(1)}, f32[9,64,128]{2,1,0:T(8,128)S(1)}, f32[9,64,128]{2,1,0:T(8,128)S(1)}, f32[48,128]{1,0:T(8,128)S(1)}, f32[48...) custom-call(f32[5,4,24,128]{3,2,1,0:T(8,128)S(1)} %get-tuple-element, ...), custom_call_target="tpu_custom_call", output_to_operand_aliasing={{0}: (3, {}), {1}: (4, {}), {2}: (5, {})} | custom-call | flops 1073741824 | bytes 1048576 | tf_op jit(solution)/shard_map/pallas_call | solution.py:50
  19.3 5.7 %all-to-all-start = ((f32[32,3,128]{2,1,0:T(4,128)}), f32[32,3,128]{2,1,0:T(4,128)S(1)}, u32[]{:S(2)}, u32[]{:S(2)}) async-start(f32[32,3,128]{2,1,0:T(4,128)} %get-tuple-element.68), calls=%async_computation | async-start | bytes 131072 | tf_op jit(solution)/shard_map/all_to_all | solution.py:551
  25.0 3.7 %collective-permute-start.5 = (f32[48,128]{1,0:T(8,128)S(1)}, f32[48,128]{1,0:T(8,128)S(1)}, u32[]{:S(2)}, u32[]{:S(2)}) collective-permute-start(f32[48,128]{1,0:T(8,128)S(1)} %get-tuple-element.65), channel_id=1, source_target_pairs={{0,12},{4,0},{8,4},{12,8},{1,13},{5,1},{9,5},{13,9},{2,14},{6,2},{... | collective-permute-start | bytes 73736 | tf_op jit(solution)/shard_map/ppermute | solution.py:74
  28.7 0.0 collective-permute-start.6
  28.7 1.1 %collective-permute-start.7 = (f32[48,128]{1,0:T(8,128)S(1)}, f32[48,128]{1,0:T(8,128)S(1)}, u32[]{:S(2)}, u32[]{:S(2)}) collective-permute-start(f32[48,128]{1,0:T(8,128)S(1)} %get-tuple-element.67), channel_id=1, source_target_pairs={{0,4},{4,8},{8,12},{12,0},{1,5},{5,9},{9,13},{13,1},{2,6},{6,10},{... | collective-permute-start | bytes 73736 | tf_op jit(solution)/shard_map/ppermute | solution.py:74
  29.8 1.5 %shard_map.195 = (f32[32,2304]{1,0:T(8,128)}, f32[32,2304]{1,0:T(8,128)}, f32[32,2304]{1,0:T(8,128)}) custom-call(f32[9,64,128]{2,1,0:T(8,128)S(1)} %get-tuple-element.72.ez, f32[9,64,128]{2,1,0:T(8,128)S(1)} %get-tuple-element.73.hx, f32[9,64,128]{2,1,0:T(8,128)S(1)} %get-tuple-element.74.hy, f32[64,128]{1,0:T(8,128)S(1)} %get-tuple-element.59.refs_9_.box), custom_call_target="tpu_custom_call" | custom-call | flops 2147483648 | bytes 1048576 | tf_op jit(solution)/shard_map/pallas_call | solution.py:50
  31.2 0.0 collective-permute-done.5.refs_1_
  31.2 2.2 %collective-permute-done.6.refs_2_ = f32[48,128]{1,0:T(8,128)S(1)} collective-permute-done((f32[48,128]{1,0:T(8,128)S(1)}, f32[48,128]{1,0:T(8,128)S(1)}, u32[]{:S(2)}, u32[]{:S(2)}) %collective-permute-start.6) | collective-permute-done | bytes 24608 | tf_op jit(solution)/shard_map/ppermute | solution.py:74
  33.4 0.9 %collective-permute-done.7.refs_3_ = f32[48,128]{1,0:T(8,128)S(1)} collective-permute-done((f32[48,128]{1,0:T(8,128)S(1)}, f32[48,128]{1,0:T(8,128)S(1)}, u32[]{:S(2)}, u32[]{:S(2)}) %collective-permute-start.7) | collective-permute-done | bytes 24608 | tf_op jit(solution)/shard_map/ppermute | solution.py:74
  34.3 0.0 all-to-all-done.refs_4_
  34.3 0.7 %shard_map.194 = (f32[64,128]{1,0:T(8,128)}, f32[64,128]{1,0:T(8,128)}, f32[64,128]{1,0:T(8,128)}, f32[3,128]{1,0:T(4,128)}) custom-call(f32[48,128]{1,0:T(8,128)S(1)} %get-tuple-element.64.refs_0_, f32[48,128]{1,0:T(8,128)S(1)} %collective-permute-done.5.refs_1_, f32[48,128]{1,0:T(8,128)S(1)} %collective-permute-done.6.refs_2_, ...), custom_call_target="tpu_custom_call" | custom-call | flops 1048576 | bytes 1048576 | tf_op jit(solution)/shard_map/pallas_call | solution.py:50
Async XLA Ops:
  1.5 9.0 %collective-permute-start = (f32[88,128]{1,0:T(8,128)S(1)}, f32[88,128]{1,0:T(8,128)S(1)}, u32[]{:S(2)}, u32[]{:S(2)}) collective-permute-start(f32[88,128]{1,0:T(8,128)S(1)} %get-tuple-element.44), channel_id=1, source_target_pairs={{0,4},{4,8},{8,12},{12,0},{1,5},{5,9},{9,13},{13,1},{2,6},{6,10},{... | collective-permute-start | bytes 135176 | tf_op jit(solution)/shard_map/ppermute | solution.py:74
  4.6 6.0 %collective-permute-start.1 = (f32[88,128]{1,0:T(8,128)S(1)}, f32[88,128]{1,0:T(8,128)S(1)}, u32[]{:S(2)}, u32[]{:S(2)}) collective-permute-start(f32[88,128]{1,0:T(8,128)S(1)} %get-tuple-element.45), channel_id=1, source_target_pairs={{0,8},{4,12},{8,0},{12,4},{1,9},{5,13},{9,1},{13,5},{2,10},{6,14},... | collective-permute-start | bytes 135176 | tf_op jit(solution)/shard_map/ppermute | solution.py:74
  7.2 4.0 %collective-permute-start.2 = (f32[88,128]{1,0:T(8,128)S(1)}, f32[88,128]{1,0:T(8,128)S(1)}, u32[]{:S(2)}, u32[]{:S(2)}) collective-permute-start(f32[88,128]{1,0:T(8,128)S(1)} %get-tuple-element.46), channel_id=1, source_target_pairs={{0,12},{4,0},{8,4},{12,8},{1,13},{5,1},{9,5},{13,9},{2,14},{6,2},{... | collective-permute-start | bytes 135176 | tf_op jit(solution)/shard_map/ppermute | solution.py:74
  11.4 3.8 %collective-permute-start.4 = (f32[24,128]{1,0:T(8,128)S(1)}, f32[24,128]{1,0:T(8,128)S(1)}, u32[]{:S(2)}, u32[]{:S(2)}) collective-permute-start(f32[24,128]{1,0:T(8,128)S(1)} %get-tuple-element.49), channel_id=1, source_target_pairs={{0,19},{1,0},{2,1},{3,2},{16,3},{17,16},{18,17},{19,18},{4,23},{5,... | collective-permute-start | bytes 36872 | tf_op jit(solution)/shard_map/ppermute | solution.py:74
  12.2 4.1 %collective-permute-start.3 = (f32[24,128]{1,0:T(8,128)S(1)}, f32[24,128]{1,0:T(8,128)S(1)}, u32[]{:S(2)}, u32[]{:S(2)}) collective-permute-start(f32[24,128]{1,0:T(8,128)S(1)} %get-tuple-element.49), channel_id=1, source_target_pairs={{0,1},{1,2},{2,3},{3,16},{16,17},{17,18},{18,19},{19,0},{4,5},{5,6... | collective-permute-start | bytes 36872 | tf_op jit(solution)/shard_map/ppermute | solution.py:74
  19.3 15.0 %all-to-all-start = ((f32[32,3,128]{2,1,0:T(4,128)}), f32[32,3,128]{2,1,0:T(4,128)S(1)}, u32[]{:S(2)}, u32[]{:S(2)}) async-start(f32[32,3,128]{2,1,0:T(4,128)} %get-tuple-element.68), calls=%async_computation | async-start | bytes 131072 | tf_op jit(solution)/shard_map/all_to_all | solution.py:551
  25.0 6.2 %collective-permute-start.5 = (f32[48,128]{1,0:T(8,128)S(1)}, f32[48,128]{1,0:T(8,128)S(1)}, u32[]{:S(2)}, u32[]{:S(2)}) collective-permute-start(f32[48,128]{1,0:T(8,128)S(1)} %get-tuple-element.65), channel_id=1, source_target_pairs={{0,12},{4,0},{8,4},{12,8},{1,13},{5,1},{9,5},{13,9},{2,14},{6,2},{... | collective-permute-start | bytes 73736 | tf_op jit(solution)/shard_map/ppermute | solution.py:74
  28.7 4.8 %collective-permute-start.6 = (f32[48,128]{1,0:T(8,128)S(1)}, f32[48,128]{1,0:T(8,128)S(1)}, u32[]{:S(2)}, u32[]{:S(2)}) collective-permute-start(f32[48,128]{1,0:T(8,128)S(1)} %get-tuple-element.66), channel_id=1, source_target_pairs={{0,8},{4,12},{8,0},{12,4},{1,9},{5,13},{9,1},{13,5},{2,10},{6,14},... | collective-permute-start | bytes 73736 | tf_op jit(solution)/shard_map/ppermute | solution.py:74
  28.7 5.6 %collective-permute-start.7 = (f32[48,128]{1,0:T(8,128)S(1)}, f32[48,128]{1,0:T(8,128)S(1)}, u32[]{:S(2)}, u32[]{:S(2)}) collective-permute-start(f32[48,128]{1,0:T(8,128)S(1)} %get-tuple-element.67), channel_id=1, source_target_pairs={{0,4},{4,8},{8,12},{12,0},{1,5},{5,9},{9,13},{13,1},{2,6},{6,10},{... | collective-permute-start | bytes 73736 | tf_op jit(solution)/shard_map/ppermute | solution.py:74

commit v5 on v4

--- a/solution.py
+++ b/solution.py
@@ -349,9 +349,8 @@
     windows, from_left, from_right = refs[:3]
     mdamp, mgain, mid, box, half, drive, row_hit, col_hit = refs[6:14]
     oez, ohx, ohy = refs[14:17]
-    back = refs[17 : 17 + owners]
-    far_traces = refs[17 + owners]
-    ez, hx, hy, behind, damp, gain, held, beside, picked, traces, sem = refs[18 + owners :]
+    back, far_traces = refs[17 : 16 + owners], refs[16 + owners]
+    ez, hx, hy, behind, damp, gain, held, beside, picked, traces, sem = refs[17 + owners :]
     column = column_of()
     place = lax.rem(iota((WINDOW, LANES), 1), GROUP)
     right = jnp.where(column == lax.axis_size(COLS) - 1, 0.0, from_right[...])
@@ -454,24 +453,27 @@
         traces[k] = picked[0:STEPS, :]
     move = pltpu.make_async_copy(traces, far_traces, sem)
     move.start()
-    for d in range(owners):
-        a = block_of(owners, d)
+    me = lax.axis_index("gx")
+    for (out, at), d in zip(((0, 0), (1, 0), (1, 1), (2, 0)), (0, 1, 3, 2)):
+        a = lax.bitwise_xor(me, d)
         for f, ref in enumerate((ez, hx, hy)):
-            back[d][f * TILE : (f + 1) * TILE, :] = ref[a, 0:TILE, 0:LANES]
+            start = (3 * at + f) * TILE
+            back[out][start : start + TILE, :] = ref[a, 0:TILE, 0:LANES]
     move.wait()
 
 
-def place_kernel(owners, *refs):
-    pieces = refs[:owners]
-    traces = refs[owners]
-    outs = refs[owners + 1 : owners + 4]
-    out_trace = refs[owners + 4]
+def swapped(value, axis, bit):
+    return lax.ppermute(value, axis, [(k, k ^ bit) for k in range(lax.axis_size(axis))])
+
+
+def place_kernel(own, near, far, traces, *outs):
     me = lax.axis_index("gx")
-    for d in range(owners):
-        here = pl.multiple_of(lax.rem(me + d, owners) * TILE, TILE)
+    for piece, at, d in ((own, 0, 0), (near, 0, 1), (far, 0, 2), (far, 1, 3)):
+        here = pl.multiple_of(lax.bitwise_xor(me, d) * TILE, TILE)
         for f in range(3):
-            outs[f][pl.ds(here, TILE), :] = pieces[d][f * TILE : (f + 1) * TILE, :]
-    out_trace[...] = jnp.sum(traces[...], axis=0)
+            start = (3 * at + f) * TILE
+            outs[f][pl.ds(here, TILE), :] = piece[start : start + TILE, :]
+    outs[3][...] = jnp.sum(traces[...], axis=0)
 
 
 def fast_shards(
@@ -536,20 +538,22 @@
     *results, traces = call(
         functools.partial(step_kernel, owners),
         (planes,) * 3
-        + tuple(f32(3 * TILE, LANES) for _ in range(owners))
+        + (f32(3 * TILE, LANES), f32(6 * TILE, LANES), f32(3 * TILE, LANES))
         + (f32(lax.axis_size(every), STEPS, receivers),),
         (windows, from_left, from_right, *fields, *ready),
         [pltpu.VMEM(window, F32)] * 6
         + [pltpu.VMEM(tiles.shape, F32), pltpu.VMEM((3, *tiles.shape), F32)]
         + [pltpu.VMEM((8, receivers), F32)]
         + [pltpu.VMEM((lax.axis_size(every), STEPS, receivers), F32), pltpu.SemaphoreType.DMA],
-        far_outs=(3 + owners,),
+        far_outs=(6,),
         aliases={3: 0, 4: 1, 5: 2},
         flops=1 << 30,
     )
     fine, back = results[:3], results[3:]
     traces = lax.all_to_all(traces, every, 0, 0)
-    pieces = [back[0]] + [ring(back[d], "gx", owners - d) for d in range(1, owners)]
+    near = swapped(back[1], "gx", 1)
+    far = swapped(jnp.concatenate([back[2], near[3 * TILE :]]), "gx", 2)
+    pieces = (back[0], near, far)
     finals = call(
         gather_kernel,
         (f32(count, cells),) * 3,
@@ -561,7 +565,7 @@
         flops=1 << 31,
     )
     ends = call(
-        functools.partial(place_kernel, owners),
+        place_kernel,
         (f32(rows, cols),) * 3 + (f32(STEPS, receivers),),
         (*pieces, traces),
     )
@@ -815,7 +819,7 @@
         rows, cols = args[0].shape
         owners = lax.axis_size("gx")
         strips = cols == LANES and args[6].shape[2] * TILE == cols and rows == owners * TILE
-        if strips and 5 * GROUP * owners <= LANES and args[13].shape[0] == LANES:
+        if strips and owners == 4 and 5 * GROUP * owners <= LANES and args[13].shape[0] == LANES:
             return fast_shards(*args)
         return shards(*args)
 

time: 35.2 us -> 34.1 us (0.969)
  starting transfers between devices: 19.6 us -> 18.2 us
    ppermute x8 -> x5, starting transfers between devices: 13.9 us -> 9.13 us  [ring(): lax.ppermute(value, axis, [(k, (k + steps) % count) for k in range(count)])]
    ppermute x0 -> x2, starting transfers between devices: none -> 4.06 us  [swapped(): lax.ppermute(value, axis, [(k, k ^ bit) for k in range(lax.axis_size(axis...]
    all_to_all x1, waiting for transfers between devices: 0.01 us -> 3.33 us  [fast_shards(): traces = lax.all_to_all(traces, every, 0, 0)]
    ppermute x8 -> x5, waiting for transfers between devices: 5.64 us -> 2.57 us  [ring(): lax.ppermute(value, axis, [(k, (k + steps) % count) for k in range(count)])]
    all_to_all x1, starting transfers between devices: 5.7 us -> 4.99 us  [fast_shards(): traces = lax.all_to_all(traces, every, 0, 0)]
  transfers between devices with their start and end apart: 9 -> 8, of which waited for: 5 -> 4; matrix products, arithmetic and copies ran while one was open for 0% -> 0% of each run, Pallas kernels for 12% -> 13%
where the time goes in v5:
time: 34.1 us; the launch traced here: 33.9 us
  starting transfers between devices  18.2 us (53%)
  Pallas kernels  9.02 us (26%)
  waiting for transfers between devices  5.91 us (17%)
  between operations  0.73 us (2%)
    ppermute x5, starting transfers between devices, ring(): lax.ppermute(value, axis, [(k, (k + steps) % count) for k in range(count)])  9.13 us
    pallas_call x7, Pallas kernels, call(): pl.pallas_call(kernel, out_shape=outs, in_specs=[hbm if k in far else vme...  9.02 us
    all_to_all x1, starting transfers between devices, fast_shards(): traces = lax.all_to_all(traces, every, 0, 0)  4.99 us
    ppermute x2, starting transfers between devices, swapped(): lax.ppermute(value, axis, [(k, k ^ bit) for k in range(lax.axis_size(axis...  4.06 us
    all_to_all x1, waiting for transfers between devices, fast_shards(): traces = lax.all_to_all(traces, every, 0, 0)  3.33 us
    ppermute x5, waiting for transfers between devices, ring(): lax.ppermute(value, axis, [(k, (k + steps) % count) for k in range(count)])  2.57 us
  transfers between devices with their start and end apart: 8, of which 4 were waited for; matrix products, arithmetic and copies ran while one was open for 0% of the time, Pallas kernels for 13%

profile of v5, /device:TPU:0, one launch (start us, length us, event | category | flops | bytes accessed | tf_op | source)
XLA Modules:
  0.0 33.9 jit_solution(9296039812080617120)
XLA Ops:
  0.6 0.9 %shard_map.189 = (f32[88,128]{1,0:T(8,128)S(1)}, f32[88,128]{1,0:T(8,128)S(1)}, f32[88,128]{1,0:T(8,128)S(1)}, f32[88,128]{1,0:T(8,128)S(1)}) custom-call(f32[64,128]{1,0:T(8,128)} %refs_0_.1, f32[64,128]{1,0:T(8,128)} %refs_1_.1, f32[64,128]{1,0:T(8,128)} %refs_2_.1, s32[64,128]{1,0:T(8,128)} %refs_3_.1, s32[4,32]{1,0:T(4,128)} %bitcast.17), custom_call_target="tpu_custom_call" | custom-call | flops 1048576 | bytes 1048576 | tf_op jit(solution)/shard_map/pallas_call | solution.py:50
  1.5 3.1 %collective-permute-start = (f32[88,128]{1,0:T(8,128)S(1)}, f32[88,128]{1,0:T(8,128)S(1)}, u32[]{:S(2)}, u32[]{:S(2)}) collective-permute-start(f32[88,128]{1,0:T(8,128)S(1)} %get-tuple-element.43), channel_id=1, source_target_pairs={{0,4},{4,8},{8,12},{12,0},{1,5},{5,9},{9,13},{13,1},{2,6},{6,10},{... | collective-permute-start | bytes 135176 | tf_op jit(solution)/shard_map/ppermute | solution.py:74
  4.6 2.6 %collective-permute-start.1 = (f32[88,128]{1,0:T(8,128)S(1)}, f32[88,128]{1,0:T(8,128)S(1)}, u32[]{:S(2)}, u32[]{:S(2)}) collective-permute-start(f32[88,128]{1,0:T(8,128)S(1)} %get-tuple-element.44), channel_id=1, source_target_pairs={{0,8},{4,12},{8,0},{12,4},{1,9},{5,13},{9,1},{13,5},{2,10},{6,14},... | collective-permute-start | bytes 135176 | tf_op jit(solution)/shard_map/ppermute | solution.py:74
  7.2 1.3 %collective-permute-start.2 = (f32[88,128]{1,0:T(8,128)S(1)}, f32[88,128]{1,0:T(8,128)S(1)}, u32[]{:S(2)}, u32[]{:S(2)}) collective-permute-start(f32[88,128]{1,0:T(8,128)S(1)} %get-tuple-element.45), channel_id=1, source_target_pairs={{0,12},{4,0},{8,4},{12,8},{1,13},{5,1},{9,5},{13,9},{2,14},{6,2},{... | collective-permute-start | bytes 135176 | tf_op jit(solution)/shard_map/ppermute | solution.py:74
  8.6 2.0 %shard_map.190 = (f32[9,64,128]{2,1,0:T(8,128)S(1)}, f32[9,64,128]{2,1,0:T(8,128)S(1)}, f32[9,64,128]{2,1,0:T(8,128)S(1)}, f32[9,64,128]{2,1,0:T(8,128)S(1)}, f3...) custom-call(f32[32,2304]{1,0:T(8,128)} %bitcast.18, f32[32,2304]{1,0:T(8,128)} %bitcast.19, f32[32,2304]{1,0:T(8,128)} %bitcast.20, ...), custom_call_target="tpu_custom_call" | custom-call | flops 2147483648 | bytes 1048576 | tf_op jit(solution)/shard_map/pallas_call | solution.py:50
  10.6 0.0 collective-permute-done.refs_1_
  10.6 0.0 collective-permute-done.1.refs_2_
  10.6 0.7 %collective-permute-done.2.refs_3_ = f32[88,128]{1,0:T(8,128)S(1)} collective-permute-done((f32[88,128]{1,0:T(8,128)S(1)}, f32[88,128]{1,0:T(8,128)S(1)}, u32[]{:S(2)}, u32[]{:S(2)}) %collective-permute-start.2) | collective-permute-done | bytes 45088 | tf_op jit(solution)/shard_map/ppermute | solution.py:74
  11.3 0.2 shard_map.191
  11.4 0.7 %collective-permute-start.4 = (f32[24,128]{1,0:T(8,128)S(1)}, f32[24,128]{1,0:T(8,128)S(1)}, u32[]{:S(2)}, u32[]{:S(2)}) collective-permute-start(f32[24,128]{1,0:T(8,128)S(1)} %get-tuple-element.48), channel_id=1, source_target_pairs={{0,19},{1,0},{2,1},{3,2},{16,3},{17,16},{18,17},{19,18},{4,23},{5,... | collective-permute-start | bytes 36872 | tf_op jit(solution)/shard_map/ppermute | solution.py:74
  12.2 1.4 %collective-permute-start.3 = (f32[24,128]{1,0:T(8,128)S(1)}, f32[24,128]{1,0:T(8,128)S(1)}, u32[]{:S(2)}, u32[]{:S(2)}) collective-permute-start(f32[24,128]{1,0:T(8,128)S(1)} %get-tuple-element.48), channel_id=1, source_target_pairs={{0,1},{1,2},{2,3},{3,16},{16,17},{17,18},{18,19},{19,0},{4,5},{5,6... | collective-permute-start | bytes 36872 | tf_op jit(solution)/shard_map/ppermute | solution.py:74
  13.5 0.9 %shard_map.192 = (f32[9,64,128]{2,1,0:T(8,128)S(1)}, f32[9,64,128]{2,1,0:T(8,128)S(1)}, f32[64,128]{1,0:T(8,128)S(1)}, f32[64,128]{1,0:T(8,128)S(1)}, f32[8,24,2...) custom-call(f32[5,4,24,128]{3,2,1,0:T(8,128)S(1)} %get-tuple-element.47., ...), custom_call_target="tpu_custom_call" | custom-call | flops 1073741824 | bytes 1048576 | tf_op jit(solution)/shard_map/pallas_call | solution.py:50
  14.4 0.8 %collective-permute-done.4.refs_2_ = f32[24,128]{1,0:T(8,128)S(1)} collective-permute-done((f32[24,128]{1,0:T(8,128)S(1)}, f32[24,128]{1,0:T(8,128)S(1)}, u32[]{:S(2)}, u32[]{:S(2)}) %collective-permute-start.4) | collective-permute-done | bytes 12320 | tf_op jit(solution)/shard_map/ppermute | solution.py:74
  15.2 1.1 %collective-permute-done.3.refs_1_ = f32[24,128]{1,0:T(8,128)S(1)} collective-permute-done((f32[24,128]{1,0:T(8,128)S(1)}, f32[24,128]{1,0:T(8,128)S(1)}, u32[]{:S(2)}, u32[]{:S(2)}) %collective-permute-start.3) | collective-permute-done | bytes 12320 | tf_op jit(solution)/shard_map/ppermute | solution.py:74
  16.3 3.0 %shard_map.193 = (f32[9,64,128]{2,1,0:T(8,128)S(1)}, f32[9,64,128]{2,1,0:T(8,128)S(1)}, f32[9,64,128]{2,1,0:T(8,128)S(1)}, f32[48,128]{1,0:T(8,128)S(1)}, f32[96...) custom-call(f32[5,4,24,128]{3,2,1,0:T(8,128)S(1)} %get-tuple-element, ...), custom_call_target="tpu_custom_call", output_to_operand_aliasing={{0}: (3, {}), {1}: (4, {}), {2}: (5, {})} | custom-call | flops 1073741824 | bytes 1048576 | tf_op jit(solution)/shard_map/pallas_call | solution.py:50
  19.3 1.3 %collective-permute-start.5 = (f32[96,128]{1,0:T(8,128)S(1)}, f32[96,128]{1,0:T(8,128)S(1)}, u32[]{:S(2)}, u32[]{:S(2)}) collective-permute-start(f32[96,128]{1,0:T(8,128)S(1)} %get-tuple-element.64), channel_id=1, source_target_pairs={{0,4},{4,0},{8,12},{12,8},{1,5},{5,1},{9,13},{13,9},{2,6},{6,2},{1... | collective-permute-start | bytes 147464 | tf_op jit(solution)/shard_map/ppermute | solution.py:466
  20.6 5.0 %all-to-all-start = ((f32[32,3,128]{2,1,0:T(4,128)}), f32[32,3,128]{2,1,0:T(4,128)S(1)}, u32[]{:S(2)}, u32[]{:S(2)}) async-start(f32[32,3,128]{2,1,0:T(4,128)} %get-tuple-element.66), calls=%async_computation | async-start | bytes 131072 | tf_op jit(solution)/shard_map/all_to_all | solution.py:553
  25.6 0.0 collective-permute-done.5.near
  25.7 2.7 %collective-permute-start.6 = (f32[96,128]{1,0:T(8,128)S(1)}, f32[96,128]{1,0:T(8,128)S(1)}, u32[]{:S(2)}, u32[]{:S(2)}) collective-permute-start(f32[96,128]{1,0:T(8,128)S(1)} %pad_maximum_fusion), channel_id=1, source_target_pairs={{0,8},{4,12},{8,0},{12,4},{1,9},{5,13},{9,1},{13,5},{2,10},{6,14},... | collective-permute-start | bytes 147464 | tf_op jit(solution)/shard_map/ppermute | solution.py:466
  28.4 1.5 %shard_map.195 = (f32[32,2304]{1,0:T(8,128)}, f32[32,2304]{1,0:T(8,128)}, f32[32,2304]{1,0:T(8,128)}) custom-call(f32[9,64,128]{2,1,0:T(8,128)S(1)} %get-tuple-element.70.ez, f32[9,64,128]{2,1,0:T(8,128)S(1)} %get-tuple-element.71.hx, f32[9,64,128]{2,1,0:T(8,128)S(1)} %get-tuple-element.72.hy, f32[64,128]{1,0:T(8,128)S(1)} %get-tuple-element.58.refs_9_.box), custom_call_target="tpu_custom_call" | custom-call | flops 2147483648 | bytes 1048576 | tf_op jit(solution)/shard_map/pallas_call | solution.py:50
  29.9 3.3 %all-to-all-done.traces = f32[32,3,128]{2,1,0:T(4,128)S(1)} async-done(((f32[32,3,128]{2,1,0:T(4,128)}), f32[32,3,128]{2,1,0:T(4,128)S(1)}, u32[]{:S(2)}, u32[]{:S(2)}) %all-to-all-start) | async-done | bytes 49184 | tf_op jit(solution)/shard_map/all_to_all | solution.py:553
  33.2 0.0 collective-permute-done.6.far
  33.2 0.7 %shard_map.194 = (f32[64,128]{1,0:T(8,128)}, f32[64,128]{1,0:T(8,128)}, f32[64,128]{1,0:T(8,128)}, f32[3,128]{1,0:T(4,128)}) custom-call(f32[48,128]{1,0:T(8,128)S(1)} %get-tuple-element.63.own, f32[96,128]{1,0:T(8,128)S(1)} %collective-permute-done.5.near, f32[96,128]{1,0:T(8,128)S(1)} %collective-permute-done.6.far, f32[32,3,128]{2,1,0:T(4,128)S(1)} %all-to-all-done.traces), custom_call_target="tpu_custom_call" | custom-call | flops 1048576 | bytes 1048576 | tf_op jit(solution)/shard_map/pallas_call | solution.py:50
  (2 shorter events, 0.0 us)
Async XLA Ops:
  1.5 9.0 %collective-permute-start = (f32[88,128]{1,0:T(8,128)S(1)}, f32[88,128]{1,0:T(8,128)S(1)}, u32[]{:S(2)}, u32[]{:S(2)}) collective-permute-start(f32[88,128]{1,0:T(8,128)S(1)} %get-tuple-element.43), channel_id=1, source_target_pairs={{0,4},{4,8},{8,12},{12,0},{1,5},{5,9},{9,13},{13,1},{2,6},{6,10},{... | collective-permute-start | bytes 135176 | tf_op jit(solution)/shard_map/ppermute | solution.py:74
  4.6 6.0 %collective-permute-start.1 = (f32[88,128]{1,0:T(8,128)S(1)}, f32[88,128]{1,0:T(8,128)S(1)}, u32[]{:S(2)}, u32[]{:S(2)}) collective-permute-start(f32[88,128]{1,0:T(8,128)S(1)} %get-tuple-element.44), channel_id=1, source_target_pairs={{0,8},{4,12},{8,0},{12,4},{1,9},{5,13},{9,1},{13,5},{2,10},{6,14},... | collective-permute-start | bytes 135176 | tf_op jit(solution)/shard_map/ppermute | solution.py:74
  7.2 4.0 %collective-permute-start.2 = (f32[88,128]{1,0:T(8,128)S(1)}, f32[88,128]{1,0:T(8,128)S(1)}, u32[]{:S(2)}, u32[]{:S(2)}) collective-permute-start(f32[88,128]{1,0:T(8,128)S(1)} %get-tuple-element.45), channel_id=1, source_target_pairs={{0,12},{4,0},{8,4},{12,8},{1,13},{5,1},{9,5},{13,9},{2,14},{6,2},{... | collective-permute-start | bytes 135176 | tf_op jit(solution)/shard_map/ppermute | solution.py:74
  11.4 3.8 %collective-permute-start.4 = (f32[24,128]{1,0:T(8,128)S(1)}, f32[24,128]{1,0:T(8,128)S(1)}, u32[]{:S(2)}, u32[]{:S(2)}) collective-permute-start(f32[24,128]{1,0:T(8,128)S(1)} %get-tuple-element.48), channel_id=1, source_target_pairs={{0,19},{1,0},{2,1},{3,2},{16,3},{17,16},{18,17},{19,18},{4,23},{5,... | collective-permute-start | bytes 36872 | tf_op jit(solution)/shard_map/ppermute | solution.py:74
  12.2 4.1 %collective-permute-start.3 = (f32[24,128]{1,0:T(8,128)S(1)}, f32[24,128]{1,0:T(8,128)S(1)}, u32[]{:S(2)}, u32[]{:S(2)}) collective-permute-start(f32[24,128]{1,0:T(8,128)S(1)} %get-tuple-element.48), channel_id=1, source_target_pairs={{0,1},{1,2},{2,3},{3,16},{16,17},{17,18},{18,19},{19,0},{4,5},{5,6... | collective-permute-start | bytes 36872 | tf_op jit(solution)/shard_map/ppermute | solution.py:74
  19.3 6.3 %collective-permute-start.5 = (f32[96,128]{1,0:T(8,128)S(1)}, f32[96,128]{1,0:T(8,128)S(1)}, u32[]{:S(2)}, u32[]{:S(2)}) collective-permute-start(f32[96,128]{1,0:T(8,128)S(1)} %get-tuple-element.64), channel_id=1, source_target_pairs={{0,4},{4,0},{8,12},{12,8},{1,5},{5,1},{9,13},{13,9},{2,6},{6,2},{1... | collective-permute-start | bytes 147464 | tf_op jit(solution)/shard_map/ppermute | solution.py:466
  20.6 12.6 %all-to-all-start = ((f32[32,3,128]{2,1,0:T(4,128)}), f32[32,3,128]{2,1,0:T(4,128)S(1)}, u32[]{:S(2)}, u32[]{:S(2)}) async-start(f32[32,3,128]{2,1,0:T(4,128)} %get-tuple-element.66), calls=%async_computation | async-start | bytes 131072 | tf_op jit(solution)/shard_map/all_to_all | solution.py:553
  25.7 7.5 %collective-permute-start.6 = (f32[96,128]{1,0:T(8,128)S(1)}, f32[96,128]{1,0:T(8,128)S(1)}, u32[]{:S(2)}, u32[]{:S(2)}) collective-permute-start(f32[96,128]{1,0:T(8,128)S(1)} %pad_maximum_fusion), channel_id=1, source_target_pairs={{0,8},{4,12},{8,0},{12,4},{1,9},{5,13},{9,1},{13,5},{2,10},{6,14},... | collective-permute-start | bytes 147464 | tf_op jit(solution)/shard_map/ppermute | solution.py:466

commit v6 on v5

--- a/solution.py
+++ b/solution.py
@@ -481,7 +481,7 @@
     fine_ez, fine_hx, fine_hy, fine_ids, boxes, src_cells, src_wave, rcv_cells,
 ):
     owners = lax.axis_size("gx")
-    every = ("grp", "gx", "gy")
+    every = ("grp", "gy", "gx")
     rows, cols = coarse_ez.shape
     all_cols = cols * lax.axis_size(COLS)
     fine_shape = fine_ez.shape

time: 34.1 us -> 34.1 us (level)
  no operation moved by 1% of the time
where the time goes in v6:
time: 34.1 us; the launch traced here: 33.8 us
  starting transfers between devices  18.2 us (53%)
  Pallas kernels  9.02 us (26%)
  waiting for transfers between devices  5.87 us (17%)
  between operations  0.73 us (2%)
    ppermute x5, starting transfers between devices, ring(): lax.ppermute(value, axis, [(k, (k + steps) % count) for k in range(count)])  9.13 us
    pallas_call x7, Pallas kernels, call(): pl.pallas_call(kernel, out_shape=outs, in_specs=[hbm if k in far else vme...  9.02 us
    all_to_all x1, starting transfers between devices, fast_shards(): traces = lax.all_to_all(traces, every, 0, 0)  4.99 us
    ppermute x2, starting transfers between devices, swapped(): lax.ppermute(value, axis, [(k, k ^ bit) for k in range(lax.axis_size(axis...  4.06 us
    all_to_all x1, waiting for transfers between devices, fast_shards(): traces = lax.all_to_all(traces, every, 0, 0)  3.3 us
    ppermute x5, waiting for transfers between devices, ring(): lax.ppermute(value, axis, [(k, (k + steps) % count) for k in range(count)])  2.57 us
  transfers between devices with their start and end apart: 8, of which 4 were waited for; matrix products, arithmetic and copies ran while one was open for 0% of the time, Pallas kernels for 13%

profile of v6, /device:TPU:0, one launch (start us, length us, event | category | flops | bytes accessed | tf_op | source)
XLA Modules:
  0.0 33.8 jit_solution(14559822543411543951)
XLA Ops:
  0.6 0.9 %shard_map.189 = (f32[88,128]{1,0:T(8,128)S(1)}, f32[88,128]{1,0:T(8,128)S(1)}, f32[88,128]{1,0:T(8,128)S(1)}, f32[88,128]{1,0:T(8,128)S(1)}) custom-call(f32[64,128]{1,0:T(8,128)} %refs_0_.1, f32[64,128]{1,0:T(8,128)} %refs_1_.1, f32[64,128]{1,0:T(8,128)} %refs_2_.1, s32[64,128]{1,0:T(8,128)} %refs_3_.1, s32[4,32]{1,0:T(4,128)} %bitcast.17), custom_call_target="tpu_custom_call" | custom-call | flops 1048576 | bytes 1048576 | tf_op jit(solution)/shard_map/pallas_call | solution.py:50
  1.5 3.1 %collective-permute-start = (f32[88,128]{1,0:T(8,128)S(1)}, f32[88,128]{1,0:T(8,128)S(1)}, u32[]{:S(2)}, u32[]{:S(2)}) collective-permute-start(f32[88,128]{1,0:T(8,128)S(1)} %get-tuple-element.43), channel_id=1, source_target_pairs={{0,4},{4,8},{8,12},{12,0},{1,5},{5,9},{9,13},{13,1},{2,6},{6,10},{... | collective-permute-start | bytes 135176 | tf_op jit(solution)/shard_map/ppermute | solution.py:74
  4.6 2.6 %collective-permute-start.1 = (f32[88,128]{1,0:T(8,128)S(1)}, f32[88,128]{1,0:T(8,128)S(1)}, u32[]{:S(2)}, u32[]{:S(2)}) collective-permute-start(f32[88,128]{1,0:T(8,128)S(1)} %get-tuple-element.44), channel_id=1, source_target_pairs={{0,8},{4,12},{8,0},{12,4},{1,9},{5,13},{9,1},{13,5},{2,10},{6,14},... | collective-permute-start | bytes 135176 | tf_op jit(solution)/shard_map/ppermute | solution.py:74
  7.2 1.3 %collective-permute-start.2 = (f32[88,128]{1,0:T(8,128)S(1)}, f32[88,128]{1,0:T(8,128)S(1)}, u32[]{:S(2)}, u32[]{:S(2)}) collective-permute-start(f32[88,128]{1,0:T(8,128)S(1)} %get-tuple-element.45), channel_id=1, source_target_pairs={{0,12},{4,0},{8,4},{12,8},{1,13},{5,1},{9,5},{13,9},{2,14},{6,2},{... | collective-permute-start | bytes 135176 | tf_op jit(solution)/shard_map/ppermute | solution.py:74
  8.6 2.0 %shard_map.190 = (f32[9,64,128]{2,1,0:T(8,128)S(1)}, f32[9,64,128]{2,1,0:T(8,128)S(1)}, f32[9,64,128]{2,1,0:T(8,128)S(1)}, f32[9,64,128]{2,1,0:T(8,128)S(1)}, f3...) custom-call(f32[32,2304]{1,0:T(8,128)} %bitcast.18, f32[32,2304]{1,0:T(8,128)} %bitcast.19, f32[32,2304]{1,0:T(8,128)} %bitcast.20, ...), custom_call_target="tpu_custom_call" | custom-call | flops 2147483648 | bytes 1048576 | tf_op jit(solution)/shard_map/pallas_call | solution.py:50
  10.6 0.0 collective-permute-done.refs_1_
  10.6 0.0 collective-permute-done.1.refs_2_
  10.6 0.7 %collective-permute-done.2.refs_3_ = f32[88,128]{1,0:T(8,128)S(1)} collective-permute-done((f32[88,128]{1,0:T(8,128)S(1)}, f32[88,128]{1,0:T(8,128)S(1)}, u32[]{:S(2)}, u32[]{:S(2)}) %collective-permute-start.2) | collective-permute-done | bytes 45088 | tf_op jit(solution)/shard_map/ppermute | solution.py:74
  11.3 0.2 shard_map.191
  11.4 0.7 %collective-permute-start.4 = (f32[24,128]{1,0:T(8,128)S(1)}, f32[24,128]{1,0:T(8,128)S(1)}, u32[]{:S(2)}, u32[]{:S(2)}) collective-permute-start(f32[24,128]{1,0:T(8,128)S(1)} %get-tuple-element.48), channel_id=1, source_target_pairs={{0,19},{1,0},{2,1},{3,2},{16,3},{17,16},{18,17},{19,18},{4,23},{5,... | collective-permute-start | bytes 36872 | tf_op jit(solution)/shard_map/ppermute | solution.py:74
  12.2 1.4 %collective-permute-start.3 = (f32[24,128]{1,0:T(8,128)S(1)}, f32[24,128]{1,0:T(8,128)S(1)}, u32[]{:S(2)}, u32[]{:S(2)}) collective-permute-start(f32[24,128]{1,0:T(8,128)S(1)} %get-tuple-element.48), channel_id=1, source_target_pairs={{0,1},{1,2},{2,3},{3,16},{16,17},{17,18},{18,19},{19,0},{4,5},{5,6... | collective-permute-start | bytes 36872 | tf_op jit(solution)/shard_map/ppermute | solution.py:74
  13.5 0.9 %shard_map.192 = (f32[9,64,128]{2,1,0:T(8,128)S(1)}, f32[9,64,128]{2,1,0:T(8,128)S(1)}, f32[64,128]{1,0:T(8,128)S(1)}, f32[64,128]{1,0:T(8,128)S(1)}, f32[8,24,2...) custom-call(f32[5,4,24,128]{3,2,1,0:T(8,128)S(1)} %get-tuple-element.47., ...), custom_call_target="tpu_custom_call" | custom-call | flops 1073741824 | bytes 1048576 | tf_op jit(solution)/shard_map/pallas_call | solution.py:50
  14.4 0.8 %collective-permute-done.4.refs_2_ = f32[24,128]{1,0:T(8,128)S(1)} collective-permute-done((f32[24,128]{1,0:T(8,128)S(1)}, f32[24,128]{1,0:T(8,128)S(1)}, u32[]{:S(2)}, u32[]{:S(2)}) %collective-permute-start.4) | collective-permute-done | bytes 12320 | tf_op jit(solution)/shard_map/ppermute | solution.py:74
  15.2 1.1 %collective-permute-done.3.refs_1_ = f32[24,128]{1,0:T(8,128)S(1)} collective-permute-done((f32[24,128]{1,0:T(8,128)S(1)}, f32[24,128]{1,0:T(8,128)S(1)}, u32[]{:S(2)}, u32[]{:S(2)}) %collective-permute-start.3) | collective-permute-done | bytes 12320 | tf_op jit(solution)/shard_map/ppermute | solution.py:74
  16.3 3.0 %shard_map.193 = (f32[9,64,128]{2,1,0:T(8,128)S(1)}, f32[9,64,128]{2,1,0:T(8,128)S(1)}, f32[9,64,128]{2,1,0:T(8,128)S(1)}, f32[48,128]{1,0:T(8,128)S(1)}, f32[96...) custom-call(f32[5,4,24,128]{3,2,1,0:T(8,128)S(1)} %get-tuple-element, ...), custom_call_target="tpu_custom_call", output_to_operand_aliasing={{0}: (3, {}), {1}: (4, {}), {2}: (5, {})} | custom-call | flops 1073741824 | bytes 1048576 | tf_op jit(solution)/shard_map/pallas_call | solution.py:50
  19.3 1.3 %collective-permute-start.5 = (f32[96,128]{1,0:T(8,128)S(1)}, f32[96,128]{1,0:T(8,128)S(1)}, u32[]{:S(2)}, u32[]{:S(2)}) collective-permute-start(f32[96,128]{1,0:T(8,128)S(1)} %get-tuple-element.64), channel_id=1, source_target_pairs={{0,4},{4,0},{8,12},{12,8},{1,5},{5,1},{9,13},{13,9},{2,6},{6,2},{1... | collective-permute-start | bytes 147464 | tf_op jit(solution)/shard_map/ppermute | solution.py:466
  20.6 5.0 %all-to-all-start = ((f32[32,3,128]{2,1,0:T(4,128)}), f32[32,3,128]{2,1,0:T(4,128)S(1)}, u32[]{:S(2)}, u32[]{:S(2)}) async-start(f32[32,3,128]{2,1,0:T(4,128)} %get-tuple-element.66), calls=%async_computation | async-start | bytes 131072 | tf_op jit(solution)/shard_map/all_to_all | solution.py:553
  25.6 0.0 collective-permute-done.5.near
  25.7 2.7 %collective-permute-start.6 = (f32[96,128]{1,0:T(8,128)S(1)}, f32[96,128]{1,0:T(8,128)S(1)}, u32[]{:S(2)}, u32[]{:S(2)}) collective-permute-start(f32[96,128]{1,0:T(8,128)S(1)} %pad_maximum_fusion), channel_id=1, source_target_pairs={{0,8},{4,12},{8,0},{12,4},{1,9},{5,13},{9,1},{13,5},{2,10},{6,14},... | collective-permute-start | bytes 147464 | tf_op jit(solution)/shard_map/ppermute | solution.py:466
  28.4 1.5 %shard_map.195 = (f32[32,2304]{1,0:T(8,128)}, f32[32,2304]{1,0:T(8,128)}, f32[32,2304]{1,0:T(8,128)}) custom-call(f32[9,64,128]{2,1,0:T(8,128)S(1)} %get-tuple-element.70.ez, f32[9,64,128]{2,1,0:T(8,128)S(1)} %get-tuple-element.71.hx, f32[9,64,128]{2,1,0:T(8,128)S(1)} %get-tuple-element.72.hy, f32[64,128]{1,0:T(8,128)S(1)} %get-tuple-element.58.refs_9_.box), custom_call_target="tpu_custom_call" | custom-call | flops 2147483648 | bytes 1048576 | tf_op jit(solution)/shard_map/pallas_call | solution.py:50
  29.9 3.3 %all-to-all-done.traces = f32[32,3,128]{2,1,0:T(4,128)S(1)} async-done(((f32[32,3,128]{2,1,0:T(4,128)}), f32[32,3,128]{2,1,0:T(4,128)S(1)}, u32[]{:S(2)}, u32[]{:S(2)}) %all-to-all-start) | async-done | bytes 49184 | tf_op jit(solution)/shard_map/all_to_all | solution.py:553
  33.2 0.0 collective-permute-done.6.far
  33.2 0.7 %shard_map.194 = (f32[64,128]{1,0:T(8,128)}, f32[64,128]{1,0:T(8,128)}, f32[64,128]{1,0:T(8,128)}, f32[3,128]{1,0:T(4,128)}) custom-call(f32[48,128]{1,0:T(8,128)S(1)} %get-tuple-element.63.own, f32[96,128]{1,0:T(8,128)S(1)} %collective-permute-done.5.near, f32[96,128]{1,0:T(8,128)S(1)} %collective-permute-done.6.far, f32[32,3,128]{2,1,0:T(4,128)S(1)} %all-to-all-done.traces), custom_call_target="tpu_custom_call" | custom-call | flops 1048576 | bytes 1048576 | tf_op jit(solution)/shard_map/pallas_call | solution.py:50
  (2 shorter events, 0.0 us)
Async XLA Ops:
  1.5 9.0 %collective-permute-start = (f32[88,128]{1,0:T(8,128)S(1)}, f32[88,128]{1,0:T(8,128)S(1)}, u32[]{:S(2)}, u32[]{:S(2)}) collective-permute-start(f32[88,128]{1,0:T(8,128)S(1)} %get-tuple-element.43), channel_id=1, source_target_pairs={{0,4},{4,8},{8,12},{12,0},{1,5},{5,9},{9,13},{13,1},{2,6},{6,10},{... | collective-permute-start | bytes 135176 | tf_op jit(solution)/shard_map/ppermute | solution.py:74
  4.6 6.0 %collective-permute-start.1 = (f32[88,128]{1,0:T(8,128)S(1)}, f32[88,128]{1,0:T(8,128)S(1)}, u32[]{:S(2)}, u32[]{:S(2)}) collective-permute-start(f32[88,128]{1,0:T(8,128)S(1)} %get-tuple-element.44), channel_id=1, source_target_pairs={{0,8},{4,12},{8,0},{12,4},{1,9},{5,13},{9,1},{13,5},{2,10},{6,14},... | collective-permute-start | bytes 135176 | tf_op jit(solution)/shard_map/ppermute | solution.py:74
  7.2 4.0 %collective-permute-start.2 = (f32[88,128]{1,0:T(8,128)S(1)}, f32[88,128]{1,0:T(8,128)S(1)}, u32[]{:S(2)}, u32[]{:S(2)}) collective-permute-start(f32[88,128]{1,0:T(8,128)S(1)} %get-tuple-element.45), channel_id=1, source_target_pairs={{0,12},{4,0},{8,4},{12,8},{1,13},{5,1},{9,5},{13,9},{2,14},{6,2},{... | collective-permute-start | bytes 135176 | tf_op jit(solution)/shard_map/ppermute | solution.py:74
  11.4 3.8 %collective-permute-start.4 = (f32[24,128]{1,0:T(8,128)S(1)}, f32[24,128]{1,0:T(8,128)S(1)}, u32[]{:S(2)}, u32[]{:S(2)}) collective-permute-start(f32[24,128]{1,0:T(8,128)S(1)} %get-tuple-element.48), channel_id=1, source_target_pairs={{0,19},{1,0},{2,1},{3,2},{16,3},{17,16},{18,17},{19,18},{4,23},{5,... | collective-permute-start | bytes 36872 | tf_op jit(solution)/shard_map/ppermute | solution.py:74
  12.2 4.1 %collective-permute-start.3 = (f32[24,128]{1,0:T(8,128)S(1)}, f32[24,128]{1,0:T(8,128)S(1)}, u32[]{:S(2)}, u32[]{:S(2)}) collective-permute-start(f32[24,128]{1,0:T(8,128)S(1)} %get-tuple-element.48), channel_id=1, source_target_pairs={{0,1},{1,2},{2,3},{3,16},{16,17},{17,18},{18,19},{19,0},{4,5},{5,6... | collective-permute-start | bytes 36872 | tf_op jit(solution)/shard_map/ppermute | solution.py:74
  19.3 6.3 %collective-permute-start.5 = (f32[96,128]{1,0:T(8,128)S(1)}, f32[96,128]{1,0:T(8,128)S(1)}, u32[]{:S(2)}, u32[]{:S(2)}) collective-permute-start(f32[96,128]{1,0:T(8,128)S(1)} %get-tuple-element.64), channel_id=1, source_target_pairs={{0,4},{4,0},{8,12},{12,8},{1,5},{5,1},{9,13},{13,9},{2,6},{6,2},{1... | collective-permute-start | bytes 147464 | tf_op jit(solution)/shard_map/ppermute | solution.py:466
  20.6 12.5 %all-to-all-start = ((f32[32,3,128]{2,1,0:T(4,128)}), f32[32,3,128]{2,1,0:T(4,128)S(1)}, u32[]{:S(2)}, u32[]{:S(2)}) async-start(f32[32,3,128]{2,1,0:T(4,128)} %get-tuple-element.66), calls=%async_computation | async-start | bytes 131072 | tf_op jit(solution)/shard_map/all_to_all | solution.py:553
  25.7 7.5 %collective-permute-start.6 = (f32[96,128]{1,0:T(8,128)S(1)}, f32[96,128]{1,0:T(8,128)S(1)}, u32[]{:S(2)}, u32[]{:S(2)}) collective-permute-start(f32[96,128]{1,0:T(8,128)S(1)} %pad_maximum_fusion), channel_id=1, source_target_pairs={{0,8},{4,12},{8,0},{12,4},{1,9},{5,13},{9,1},{13,5},{2,10},{6,14},... | collective-permute-start | bytes 147464 | tf_op jit(solution)/shard_map/ppermute | solution.py:466
